TPU v7x, 32 devices: a whole 2x2x4 slice. The times are simulated.
32 devices in a mesh: tables: 8 (over z, y), cells: 4 (over x, core).
Axes of the slice: x: 2, y: 2, z: 4, core: 2. Of those that a mesh axis runs over, the one named last changes fastest.
Arguments:
- cells_in: bfloat16 [8, 128, 112, 192], P('tables', 'cells'), may hold values from -6 to 6
- train_count: int32 [8], P('tables'), may hold values from 32 to 96
- feat_count: int32 [8], P('tables'), may hold values from 28 to 112
- feat_qkv: bfloat16 [192, 576], replicated, may hold values from -2 to 2
- feat_proj: bfloat16 [192, 192], replicated, may hold values from -2 to 2
- row_qkv: bfloat16 [192, 576], replicated, may hold values from -2 to 2
- row_proj: bfloat16 [192, 192], replicated, may hold values from -0.4375 to 0.4375
- w_in: bfloat16 [192, 768], replicated, may hold values from -0.4375 to 0.4375
- w_out: bfloat16 [768, 192], replicated, may hold values from -0.21875 to 0.21875
- cotangent: bfloat16 [8, 128, 112, 192], P('tables', 'cells'), may hold values from -6 to 6
Outputs:
- cells_out: bfloat16 [8, 128, 112, 192], P('tables', 'cells')
- grad_in: float32 [192, 768], P(None, ('tables', 'cells'))
- grad_out: float32 [768, 192], P(('tables', 'cells'))
All inputs are finite; a program needn't handle non-finite values.
Results may differ from a plain program's by a relative error of at most 0.018.
Values may be sent and summed in bfloat16 or wider, within the bound.
No kernel may reach another device: no remote copies, remote signals or barrier semaphores. Data moves between devices by JAX's collectives and lax.ppermute only.
A program may use at most 128 MiB of HBM per device.

v0:
```python
import functools
import math

import jax
import jax.numpy as jnp
from jax import lax
from jax.experimental import pallas as pl
from jax.experimental.pallas import tpu as pltpu
from jax.sharding import PartitionSpec as P


HEADS = 6
HEAD_DIM = 32
BF = jnp.bfloat16
F32 = jnp.float32
ERFC_K = 3.5
ERFC_C = (
    0.4096238545958983,
    1.030471715475736,
    9.637057789606283,
    -24.75291485624482,
    177.3359613786631,
    -181.2859739558248,
)
NT = (((1,), (1,)), ((), ()))
TN = (((0,), (0,)), ((), ()))


def dot(a, b, dims=(((1,), (0,)), ((), ()))):
    return lax.dot_general(a, b, dims, preferred_element_type=F32)


def layer_norm(values):
    mean = jnp.mean(values, axis=0, keepdims=True)
    centred = values - mean
    var = jnp.mean(centred * centred, axis=0, keepdims=True)
    return centred * lax.rsqrt(var + 1e-05)


def one_hot(rows, cols):
    row = lax.broadcasted_iota(jnp.int32, (rows, cols), 0)
    col = lax.broadcasted_iota(jnp.int32, (rows, cols), 1)
    return (row == col).astype(F32).astype(BF)


def finish_items(att_ref, ats, w_proj_t, flip, residual_t):
    lanes = att_ref.shape[2]
    mixed = dot(w_proj_t, jnp.concatenate([att_ref[at] for at in ats], axis=1))
    done = []
    for a, at in enumerate(ats):
        normed = layer_norm(residual_t(at).astype(F32) + mixed[:, a * lanes : (a + 1) * lanes]).astype(BF)
        done.append(dot(flip, normed, NT).astype(BF))
    return done


def swap_matrix(side):
    out = lax.broadcasted_iota(jnp.int32, (side * side, side * side), 0)
    src = lax.broadcasted_iota(jnp.int32, (side * side, side * side), 1)
    return (src == (out % side) * side + out // side).astype(F32).astype(BF)


def pack(parts):
    if len(parts) == 1:
        return parts[0]
    a, b = parts
    cut = a.shape[-1] // 128 * 128
    return jnp.concatenate([a[..., :cut], b[..., :cut], a[..., cut:], b[..., cut:]], axis=-1)


def unpack(block, per, width):
    if per == 1:
        return [block]
    cut = width // 128 * 128
    rest = width - cut
    return [
        jnp.concatenate(
            [block[..., q * cut : (q + 1) * cut], block[..., 2 * cut + q * rest : 2 * cut + (q + 1) * rest]],
            axis=-1,
        )
        for q in range(2)
    ]


CELLS = ("chips", "core")


def cell_index():
    return lax.axis_index("chips") * 2 + lax.axis_index("core")


def mask_of(keys, count):
    rows = lax.broadcasted_iota(jnp.int32, (keys, 1), 0) < count
    lanes = lax.broadcasted_iota(jnp.int32, (1, keys), 1) < count
    return rows, lanes


def keep_projected(refs, at, q_v, k_rows, masks):
    q_ref, k_ref, v_ref = refs
    width, keys = q_ref.shape[1], k_ref.shape[1]
    key_row, key_lane = masks
    scale = F32(math.log2(math.e) / math.sqrt(HEAD_DIM))
    q_ref[at] = (q_v[:width] * scale).astype(BF)
    v_ref[at] = jnp.where(key_lane, q_v[width:, :keys], F32(0)).astype(BF)
    k_ref[at] = jnp.where(key_row, k_rows[:keys], k_rows[0:1]).astype(BF)


def score_blocks(q_own, lanes):
    hd = HEAD_DIM
    width = q_own.shape[0]
    blank = jnp.zeros((hd, lanes), BF)
    blocks = []
    for i in range(HEADS // 2):
        lo = 2 * i * hd
        tile = lo // 128 * 128
        end = min(tile + 128, width)
        pieces = [
            jnp.concatenate([q_own[lo : lo + hd], blank], axis=1),
            jnp.concatenate([blank, q_own[lo + hd : lo + 2 * hd]], axis=1),
        ]
        if lo > tile:
            pieces = [jnp.zeros((lo - tile, 2 * lanes), BF)] + pieces
        if lo + 2 * hd < end:
            pieces = pieces + [jnp.zeros((end - lo - 2 * hd, 2 * lanes), BF)]
        blocks.append((tile, end, jnp.concatenate(pieces, axis=0)))
    return blocks


def attend(refs, att_ref, ats, ones):
    q_ref, k_ref, v_ref = refs
    lanes = q_ref.shape[2]
    hd = HEAD_DIM
    scores = []
    for at in ats:
        k_own = k_ref[at]
        for tile, end, block in score_blocks(q_ref[at], lanes):
            scores.append(dot(k_own[:, tile:end], block))
    weights = [jnp.exp2(s - jnp.max(s, axis=0, keepdims=True)).astype(BF) for s in scores]
    for n, at in enumerate(ats):
        v_own = v_ref[at]
        for i in range(HEADS // 2):
            lo = 2 * i * hd
            lhs = jnp.concatenate([v_own[lo : lo + 2 * hd], ones], axis=0)
            mixed = dot(lhs, weights[n * (HEADS // 2) + i])
            scale = 1.0 / mixed[2 * hd : 2 * hd + 1]
            att_ref[at, lo : lo + hd] = (mixed[:hd, :lanes] * scale[:, :lanes]).astype(BF)
            att_ref[at, lo + hd : lo + 2 * hd] = (mixed[hd : 2 * hd, lanes:] * scale[:, lanes:]).astype(BF)


def loop(count, most, body):
    group = max(d for d in range(1, most + 1) if count % d == 0)

    def step(i, carry):
        body([i * group + a for a in range(group)])
        return carry

    lax.fori_loop(0, count // group, step, 0)


def pad_lanes(value, lanes):
    rows, n = value.shape
    return value if n == lanes else jnp.concatenate([value, jnp.zeros((rows, lanes - n), value.dtype)], axis=1)


def feature_kernel(groups, per, first, rows, cuts, count_ref, cells_ref, wqkv_ref, wproj_ref, *refs):
    outs = refs[: groups * cuts]
    q_ref, k_ref, v_ref, att_ref, mid_ref, swap_ref = refs[groups * cuts :]
    _, width, feats = cells_ref.shape
    lanes = q_ref.shape[2]
    fg = feats // groups
    half = fg // per
    count = count_ref[0]
    w_t = wqkv_ref[...].T
    w_qv = jnp.concatenate([w_t[:width], w_t[2 * width :]], axis=0)
    w_k = w_t[width : 2 * width]
    w_proj_t = wproj_ref[...].T
    flip = one_hot(feats, lanes)
    masks = mask_of(feats, count)
    ones = jnp.broadcast_to(jnp.where(masks[1], F32(1), F32(0)), (16, feats)).astype(BF)
    kept = (q_ref, k_ref, v_ref)

    def project(ats):
        x_t = [pad_lanes(cells_ref[first + at], lanes) for at in ats]
        q_v = dot(w_qv, jnp.concatenate(x_t, axis=1))
        x = [t.T[:feats] for t in x_t]
        k = dot(jnp.concatenate(x, axis=0), w_k, NT)
        for a, at in enumerate(ats):
            keep_projected(kept, at, q_v[:, a * lanes : (a + 1) * lanes], k[a * feats : (a + 1) * feats], masks)

    def finish(ats):
        own = lambda at: pad_lanes(cells_ref[first + at], lanes)
        for at, value in zip(ats, finish_items(att_ref, ats, w_proj_t, flip, own)):
            mid_ref[at] = value

    loop(rows, 8, project)
    loop(rows, 8, lambda ats: attend(kept, att_ref, ats, ones))
    loop(rows, 8, finish)
    swap = swap_matrix(rows)
    for f in range(feats // rows):
        block = mid_ref[:, f * rows : (f + 1) * rows, :].reshape(rows * rows, width)
        swap_ref[f * rows : (f + 1) * rows] = dot(swap, block).astype(BF).reshape(rows, rows, width)
    here = cell_index()
    size = half // cuts
    for c in range(cuts):
        for m in range(groups):
            base = (here ^ m) * fg + c * size
            outs[c * groups + m][...] = pack([swap_ref[pl.ds(base + q * half, size)] for q in range(per)])


IN_VMEM = pl.BlockSpec(memory_space=pltpu.VMEM)
IN_SMEM = pl.BlockSpec(memory_space=pltpu.SMEM)


def attention_scratch(items, width, lanes, keys):
    return [
        pltpu.VMEM((items, width, lanes), BF),
        pltpu.VMEM((items, keys, width), BF),
        pltpu.VMEM((items, width, keys), BF),
        pltpu.VMEM((items, width, lanes), BF),
    ]


def near(shape, dtype=BF):
    return pltpu.VMEM(shape, dtype)


def bring(*arrays):
    return [pltpu.with_memory_space_constraint(x, pltpu.VMEM) for x in arrays]


PARAMS = pltpu.CompilerParams(vmem_limit_bytes=14 * 2**20)


def cost(flops):
    return pl.CostEstimate(flops=flops, transcendentals=0, bytes_accessed=10**6)


def feature_chunk(block_t, count, wqkv, wproj, groups, per, chunk, rows, cuts):
    _, width, feats = block_t.shape
    half = feats // groups // per
    lanes = -(-feats // 128) * 128
    operands = [block_t, wqkv, wproj]
    if chunk == 0:
        base, specs = 0, [pl.BlockSpec((rows, width, feats), lambda i: (0, 0, 0)), IN_VMEM, IN_VMEM]
        operands = [pltpu.with_memory_space_constraint(x, pltpu.HBM) for x in operands]
    else:
        base, specs = chunk * rows, [IN_VMEM] * 3
        operands = bring(*operands)
    return pl.pallas_call(
        functools.partial(feature_kernel, groups, per, base, rows, cuts),
        grid=(1,),
        in_specs=[IN_SMEM] + specs,
        out_specs=[IN_VMEM] * (groups * cuts),
        out_shape=[near((half // cuts, rows, per * width))] * (groups * cuts),
        scratch_shapes=attention_scratch(rows, width, lanes, feats)
        + [pltpu.VMEM((rows, feats, width), BF), pltpu.VMEM((feats, rows, width), BF)],
        compiler_params=PARAMS,
        cost_estimate=cost(10**8),
    )(count, *operands)


def row_kernel(groups, per, chunks, firsts, count_ref, wqkv_ref, wproj_ref, *refs):
    ins = refs[: groups * chunks]
    outs = refs[groups * chunks : groups * chunks + groups]
    q_ref, k_ref, v_ref, att_ref, x_ref, xt_ref, y_ref = refs[groups * chunks + groups :]
    pairs, local, _ = outs[0].shape
    sub_rows = local // chunks
    items, rows, width = x_ref.shape
    keys = k_ref.shape[1]
    count = count_ref[0]
    w_t = wqkv_ref[...].T
    w_qv = jnp.concatenate([w_t[:width], w_t[2 * width :], one_hot(width, width)], axis=0)
    w_k = w_t[width : 2 * width]
    w_proj_t = wproj_ref[...].T
    flip = one_hot(rows, rows)
    masks = mask_of(keys, count)
    ones = jnp.broadcast_to(jnp.where(masks[1], F32(1), F32(0)), (16, keys)).astype(BF)
    kept = (q_ref, k_ref, v_ref)
    here = cell_index()
    for m in range(groups):
        for k in range(chunks):
            at = pl.multiple_of((here ^ m) * local + k * sub_rows, sub_rows)
            for q, part in enumerate(unpack(ins[k * groups + m][firsts[k] : firsts[k] + pairs], per, width)):
                x_ref[q * pairs : (q + 1) * pairs, pl.ds(at, sub_rows), :] = part

    def project(ats):
        x = jnp.concatenate([x_ref[at] for at in ats], axis=0)
        q_v = dot(w_qv, x, NT)
        for a, at in enumerate(ats):
            k = dot(x[a * rows : a * rows + keys], w_k, NT)
            own = q_v[:, a * rows : (a + 1) * rows]
            xt_ref[at] = own[2 * width :].astype(BF)
            keep_projected(kept, at, own[: 2 * width], k, masks)

    def finish(ps):
        ats = [q * pairs + p for p in ps for q in range(per)]
        done = finish_items(att_ref, ats, w_proj_t, flip, lambda at: xt_ref[at])
        for a, p in enumerate(ps):
            y_ref[p] = pack(done[a * per : (a + 1) * per])

    most = max(1, 1024 // rows)
    loop(items, min(most, 7), project)
    loop(items, min(most, 7), lambda ats: attend(kept, att_ref, ats, ones))
    loop(pairs, min(most, 7), finish)
    for m in range(groups):
        at = pl.multiple_of((here ^ m) * local, local)
        outs[m][...] = y_ref[:, pl.ds(at, local), :]


def row_chunk(pieces, count, wqkv, wproj, groups, per, chunks, pairs, firsts):
    sub_rows, packed = pieces[0].shape[1:]
    width = wproj.shape[0]
    local = sub_rows * chunks
    rows = local * groups
    keys = rows - rows // 4
    return pl.pallas_call(
        functools.partial(row_kernel, groups, per, chunks, firsts),
        in_specs=[IN_SMEM] + [IN_VMEM] * (2 + len(pieces)),
        out_specs=[IN_VMEM] * groups,
        out_shape=[near((pairs, local, packed))] * groups,
        scratch_shapes=attention_scratch(pairs * per, width, rows, keys)
        + [
            pltpu.VMEM((pairs * per, rows, width), BF),
            pltpu.VMEM((pairs * per, width, rows), BF),
            pltpu.VMEM((pairs, rows, packed), BF),
        ],
        compiler_params=PARAMS,
        cost_estimate=cost(10**8),
    )(count, *bring(wqkv, wproj, *pieces))


def swap_kernel(in_ref, out_ref, x_ref):
    first, width, second = in_ref.shape
    lanes = -(-second // 128) * 128
    side = 16
    swap = swap_matrix(side)
    for a in range(first):
        x_ref[a] = pad_lanes(in_ref[a], lanes).T[:second]
    for a in range(first // side):
        for b in range(second // side):
            block = x_ref[a * side : (a + 1) * side, b * side : (b + 1) * side, :]
            swapped = dot(swap, block.reshape(side * side, width)).astype(BF)
            out_ref[b * side : (b + 1) * side, a * side : (a + 1) * side, :] = swapped.reshape(side, side, width)


def swap_cotangent(array_t):
    first, width, second = array_t.shape
    return pl.pallas_call(
        swap_kernel,
        in_specs=[IN_VMEM],
        out_specs=IN_VMEM,
        out_shape=near((second, first, width)),
        scratch_shapes=[pltpu.VMEM((first, second, width), BF)],
        compiler_params=PARAMS,
        cost_estimate=cost(10**8),
        name="swap_cotangent",
    )(*bring(array_t))


def output_kernel(groups, per, chunks, *refs):
    parts, (out_ref, f_ref, y_ref) = refs[:-3], refs[-3:]
    feats, local, width = f_ref.shape
    half = feats // groups // per
    pairs = half // chunks
    size = pairs * local
    lanes = -(-feats // 128) * 128
    here = cell_index()
    count = parts[0].shape[0]
    for n, part in enumerate(parts):
        for b in range(count):
            at = n * count + b
            base = (here ^ (at // chunks)) * (half * per) + (at % chunks) * pairs
            for q in range(per):
                rows = part[b, q * size : (q + 1) * size].reshape(pairs, local, width)
                f_ref[pl.ds(base + q * half, pairs)] = rows
    side = 16
    swap = swap_matrix(side)
    for f in range(0, feats, side):
        for r in range(0, local, side):
            block = f_ref[f : f + side, r : r + side, :].reshape(side * side, width)
            y_ref[r : r + side, f : f + side, :] = dot(swap, block).astype(BF).reshape(side, side, width)
    for r in range(local):
        y = y_ref[r]
        if lanes > feats:
            y = jnp.concatenate([y, jnp.zeros((lanes - feats, width), BF)], axis=0)
        out_ref[r] = y.T[:, :feats]


def make_output(parts, groups, per, chunks, feats, local):
    width = parts[0].shape[-1]
    return pl.pallas_call(
        functools.partial(output_kernel, groups, per, chunks),
        in_specs=[IN_VMEM] * len(parts),
        out_specs=IN_VMEM,
        out_shape=jax.ShapeDtypeStruct((local, width, feats), BF),
        scratch_shapes=[pltpu.VMEM((feats, local, width), BF), pltpu.VMEM((local, feats, width), BF)],
        compiler_params=PARAMS,
        cost_estimate=cost(10**8),
        name="make_output",
    )(*bring(*parts))


def gelu_and_slope(pre):
    size = jnp.abs(pre)
    bell = jnp.exp2(pre * pre * F32(-0.5 * math.log2(math.e)))
    t = 1.0 / (size + F32(ERFC_K))
    poly = F32(ERFC_C[-1])
    for coefficient in ERFC_C[-2::-1]:
        poly = poly * t + F32(coefficient)
    tail = poly * t * bell
    cdf = jnp.where(pre >= 0, 1.0 - tail, tail)
    return pre * cdf, cdf + pre * (bell * F32(1.0 / math.sqrt(2.0 * math.pi)))


def dense_kernel(groups, per, chunks, first, factor, *refs):
    last = factor is not None
    blocks = refs[-1].shape[0]
    ins = refs[:blocks]
    win_ref, woutt_ref, cot_ref = refs[blocks : blocks + 3]
    rest = refs[blocks + 3 :]
    if first > 0:
        prev_in, prev_out = rest[:2]
        rest = rest[2:]
    if last:
        out_ref, keep_ref, send_ref, gin_ref, gout_ref, n_ref = rest
    else:
        out_ref, gin_ref, gout_ref, n_ref = rest
    pairs, local, _ = ins[0].shape
    width, _ = win_ref.shape
    size = pairs * local
    fg = cot_ref.shape[0] // groups
    half = fg // per
    here = cell_index()
    for b in range(blocks):
        for q, part in enumerate(unpack(ins[b][...], per, width)):
            n_ref[b, q * size : (q + 1) * size] = part.reshape(size, width)
    if first > 0:
        gin_ref[...] = prev_in[...]
        gout_ref[...] = prev_out[...]
    else:
        gin_ref[...] = jnp.zeros_like(gin_ref)
        gout_ref[...] = jnp.zeros_like(gout_ref)
    w_in = win_ref[...]
    w_out_t = woutt_ref[...]

    def step(b, carry):
        at = first + b
        feature = (here ^ (at // chunks)) * fg + (at % chunks) * pairs
        normed = n_ref[b]
        cot = [cot_ref[pl.ds(feature + q * half, pairs)].reshape(size, width) for q in range(per)]
        cot = jnp.concatenate(cot, axis=0)
        act, slope = gelu_and_slope(dot(normed, w_in))
        act = act.astype(BF)
        out_ref[b] = (normed.astype(F32) + dot(act, w_out_t, NT)).astype(BF)
        dpre = (dot(cot, w_out_t) * slope).astype(BF)
        gin_ref[...] += dot(normed, dpre, TN)
        gout_ref[...] += dot(cot, act, TN)
        return carry

    lax.fori_loop(0, blocks, step, 0)
    if last:
        both = pack([(gin_ref[...].T * F32(factor)).astype(BF), (gout_ref[...].T * F32(factor)).astype(BF)])
        both = both.reshape(keep_ref.shape[0], 2, *keep_ref.shape[1:])
        even = here % 2 == 0
        keep_ref[...] = jnp.where(even, both[:, 0], both[:, 1])
        send_ref[...] = jnp.where(even, both[:, 1], both[:, 0])


def dense_part(blocks, cot_t, w_in, w_out_t, prev, groups, per, chunks, first, factor, shares):
    pairs, local, _ = blocks[0].shape
    width, hid = w_in.shape
    size = per * pairs * local
    count = len(blocks)
    outs = [near((count, size, width))]
    operands = list(blocks) + [w_in, w_out_t, cot_t]
    if first > 0:
        operands += list(prev)
    scratch = []
    if factor is None:
        outs += [near((width, hid), F32)] * 2
    else:
        outs += [near((shares // 2, hid // shares, 2 * width))] * 2
        scratch = [pltpu.VMEM((width, hid), F32)] * 2
    scratch += [pltpu.VMEM((count, size, width), BF)]
    return pl.pallas_call(
        functools.partial(dense_kernel, groups, per, chunks, first, factor),
        in_specs=[IN_VMEM] * len(operands),
        out_specs=[IN_VMEM] * len(outs),
        out_shape=outs,
        scratch_shapes=scratch,
        compiler_params=PARAMS,
        cost_estimate=cost(10**8),
    )(*bring(*operands))


def add_kernel(a_ref, b_ref, out_ref):
    out_ref[...] = (a_ref[...].astype(F32) + b_ref[...].astype(F32)).astype(BF)


def add_pair(a, b):
    return pl.pallas_call(
        add_kernel,
        in_specs=[IN_VMEM] * 2,
        out_specs=IN_VMEM,
        out_shape=jax.ShapeDtypeStruct(a.shape, BF),
        compiler_params=PARAMS,
        cost_estimate=cost(10**6),
        name="add_pair",
    )(*bring(a, b))


def exchange(pieces, groups):
    come = [pieces[0]]
    for m in range(1, groups):
        come.append(lax.ppermute(pieces[m], CELLS, [(s, s ^ m) for s in range(groups)]))
    return come


def per_device(
    cells_in, train_count, feat_count, feat_qkv, feat_proj, row_qkv, row_proj, w_in, w_out, cotangent
):
    block_t = jnp.swapaxes(cells_in[0], 1, 2)
    local, width, feats = block_t.shape
    groups = lax.axis_size(CELLS)
    tables = lax.axis_size("tables")
    fg = feats // groups
    per = 2 if fg % 2 == 0 else 1
    half = fg // per
    sub_rows = 16
    row_chunks = local // sub_rows
    feat_chunks = 2 if half % 2 == 0 else 1
    factor = 1.0 / math.sqrt(tables * local * groups * feats)
    pairs = half // feat_chunks
    pieces = [[] for _ in range(feat_chunks)]
    firsts = []
    for k in range(row_chunks):
        cuts = feat_chunks if k == row_chunks - 1 else 1
        sent = feature_chunk(block_t, feat_count, feat_qkv, feat_proj, groups, per, k, sub_rows, cuts)
        come = [exchange(sent[c * groups : (c + 1) * groups], groups) for c in range(cuts)]
        for j in range(feat_chunks):
            pieces[j] += come[j % cuts]
        firsts.append(cuts == 1)
    cot_t = swap_cotangent(jnp.swapaxes(cotangent[0], 1, 2))
    back = []
    for j in range(feat_chunks):
        starts = tuple(j * pairs if whole else 0 for whole in firsts)
        done = row_chunk(pieces[j], train_count, row_qkv, row_proj, groups, per, row_chunks, pairs, starts)
        back.append(exchange(done, groups))
    w_out_t = w_out.T
    shares = tables * groups
    blocks = [back[j][m] for m in range(groups) for j in range(feat_chunks)]
    cut = len(blocks) // 2
    args = (cot_t, w_in, w_out_t)
    shape = (groups, per, feat_chunks)
    out_0, *partial = dense_part(blocks[:cut], *args, None, *shape, 0, None, shares)
    out_1, keep, send = dense_part(blocks[cut:], *args, partial, *shape, cut, factor, shares)
    other = lax.ppermute(send, "core", [(0, 1), (1, 0)])
    pieces = add_pair(keep, other)
    total = lax.all_to_all(pieces, ("tables", "chips"), split_axis=0, concat_axis=0, tiled=True)
    total = jnp.sum(total.astype(F32), axis=0)
    output = make_output([out_0, out_1], *shape, feats, local)
    grad_in, grad_out = unpack(total, 2, width)
    return (jnp.swapaxes(output, 1, 2)[None], grad_in.T, grad_out)


def solution(mesh):
    tables, cells = mesh.devices.shape
    split = jax.sharding.Mesh(mesh.devices.reshape(tables, cells // 2, 2), ("tables", "chips", "core"))
    spread = P("tables", CELLS, None, None)
    shares = ("tables",) + CELLS
    return jax.shard_map(
        per_device,
        mesh=split,
        in_specs=(spread, P("tables"), P("tables"), P(), P(), P(), P(), P(), P(), spread),
        out_specs=(spread, P(None, shares), P(shares, None)),
        check_vma=False,
    )
```

profile of v0, /device:TPU:0, one launch (start us, length us, event | category | flops | bytes accessed | tf_op | source)
XLA Modules:
  0.0 92.8 jit_solution(560631377018046237)
XLA Ops:
  1.3 1.4 %copy-done = bf16[1,32,112,192]{2,3,1,0:T(8,128)(2,1)S(1)} copy-done((bf16[1,32,112,192]{2,3,1,0:T(8,128)(2,1)S(1)}, bf16[1,32,112,192]{2,3,1,0:T(8,128)(2,1)}, u32[]{:S(2)}) %copy-start) | copy-done | bytes 1376280
  2.7 0.9 %copy-done.5 = bf16[192,576]{1,0:T(8,128)(2,1)S(1)} copy-done((bf16[192,576]{1,0:T(8,128)(2,1)S(1)}, bf16[192,576]{1,0:T(8,128)(2,1)}, u32[]{:S(2)}) %copy-start.5) | copy-done | bytes 221208
  3.6 0.9 copy-done.6
  4.5 4.8 %shard_map.122 = (bf16[7,16,384]{2,1,0:T(8,128)(2,1)S(1)}, bf16[7,16,384]{2,1,0:T(8,128)(2,1)S(1)}, bf16[7,16,384]{2,1,0:T(8,128)(2,1)S(1)}, bf16[7,16,384]{2,1,...) custom-call(s32[1]{0:T(128)S(6)} %copy.14.count_ref, ...), custom_call_target="tpu_custom_call" | custom-call | flops 100000000 | bytes 1000000 | tf_op jit(solution)/shard_map/pallas_call | solution.py:248
  9.9 6.1 %shard_map.121 = (bf16[14,16,384]{2,1,0:T(8,128)(2,1)S(1)}, bf16[14,16,384]{2,1,0:T(8,128)(2,1)S(1)}, bf16[14,16,384]{2,1,0:T(8,128)(2,1)S(1)}, bf16[14,16,384]{2,1,0:T(8,128)(2,1)S(1)}) custom-call(s32[1]{0:T(128)S(6)} %copy.14.count_ref, bf16[32,192,112]{2,1,0:T(8,128)(2,1)} %bitcast.12, bf16[192,576]{1,0:T(8,128)(2,1)} %wqkv_ref.5, bf16[192,192]{1,0:T(8,128)(2,1)} %wproj_ref.5), custom_call_target="tpu_custom_call" | custom-call | flops 100000000 | bytes 1000000 | tf_op jit(solution)/shard_map/pallas_call | solution.py:248
  16.2 3.0 %collective-permute-start.1 = (bf16[14,16,384]{2,1,0:T(8,128)(2,1)S(1)}, bf16[14,16,384]{2,1,0:T(8,128)(2,1)S(1)}, u32[]{:S(2)}, u32[]{:S(2)}) collective-permute-start(bf16[14,16,384]{2,1,0:T(8,128)(2,1)S(1)} %get-tuple-element.31), channel_id=1, source_target_pairs={{0,2},{1,3},{2,0},{3,1},{4,6},{5,7},{6,4},{7,5},{8,10},{9,11},{10,... | collective-permute-start | bytes 516104 | tf_op jit(solution)/shard_map/ppermute | solution.py:514
  19.1 1.4 %collective-permute-start.4 = (bf16[7,16,384]{2,1,0:T(8,128)(2,1)S(1)}, bf16[7,16,384]{2,1,0:T(8,128)(2,1)S(1)}, u32[]{:S(2)}, u32[]{:S(2)}) collective-permute-start(bf16[7,16,384]{2,1,0:T(8,128)(2,1)S(1)} %get-tuple-element.35), channel_id=1, source_target_pairs={{0,2},{1,3},{2,0},{3,1},{4,6},{5,7},{6,4},{7,5},{8,10},{9,11},{10,... | collective-permute-start | bytes 258056 | tf_op jit(solution)/shard_map/ppermute | solution.py:514
  21.5 8.3 %collective-permute-done.4.refs_6_ = bf16[7,16,384]{2,1,0:T(8,128)(2,1)S(1)} collective-permute-done((bf16[7,16,384]{2,1,0:T(8,128)(2,1)S(1)}, bf16[7,16,384]{2,1,0:T(8,128)(2,1)S(1)}, u32[]{:S(2)}, u32[]{:S(2)}) %collective-permute-start.4) | collective-permute-done | bytes 86048 | tf_op jit(solution)/shard_map/ppermute | solution.py:514
  30.5 4.2 %shard_map.123 = (bf16[7,32,384]{2,1,0:T(8,128)(2,1)S(1)}, bf16[7,32,384]{2,1,0:T(8,128)(2,1)S(1)}, bf16[7,32,384]{2,1,0:T(8,128)(2,1)S(1)}, bf16[7,32,384]{2,1,0:T(8,128)(2,1)S(1)}) custom-call(s32[1]{0:T(128)S(6)} %copy.13.count_ref, bf16[192,576]{1,0:T(8,128)(2,1)S(1)} %copy-done.4, bf16[192,192]{1,0:T(8,128)(2,1)S(1)} %copy-done.7, ...), custom_call_target="tpu_custom_call" | custom-call | flops 100000000 | bytes 1000000 | tf_op jit(solution)/shard_map/pallas_call | solution.py:315
  35.3 1.8 %collective-permute-start.7 = (bf16[7,16,384]{2,1,0:T(8,128)(2,1)S(1)}, bf16[7,16,384]{2,1,0:T(8,128)(2,1)S(1)}, u32[]{:S(2)}, u32[]{:S(2)}) collective-permute-start(bf16[7,16,384]{2,1,0:T(8,128)(2,1)S(1)} %get-tuple-element.40), channel_id=1, source_target_pairs={{0,2},{1,3},{2,0},{3,1},{4,6},{5,7},{6,4},{7,5},{8,10},{9,11},{10,... | collective-permute-start | bytes 258056 | tf_op jit(solution)/shard_map/ppermute | solution.py:514
  37.1 3.2 %collective-permute-done.7.refs_6_ = bf16[7,16,384]{2,1,0:T(8,128)(2,1)S(1)} collective-permute-done((bf16[7,16,384]{2,1,0:T(8,128)(2,1)S(1)}, bf16[7,16,384]{2,1,0:T(8,128)(2,1)S(1)}, u32[]{:S(2)}, u32[]{:S(2)}) %collective-permute-start.7) | collective-permute-done | bytes 86048 | tf_op jit(solution)/shard_map/ppermute | solution.py:514
  40.4 1.5 %collective-permute-done.8.refs_7_ = bf16[7,16,384]{2,1,0:T(8,128)(2,1)S(1)} collective-permute-done((bf16[7,16,384]{2,1,0:T(8,128)(2,1)S(1)}, bf16[7,16,384]{2,1,0:T(8,128)(2,1)S(1)}, u32[]{:S(2)}, u32[]{:S(2)}) %collective-permute-start.8) | collective-permute-done | bytes 86048 | tf_op jit(solution)/shard_map/ppermute | solution.py:514
  41.9 4.2 %shard_map.124 = (bf16[7,32,384]{2,1,0:T(8,128)(2,1)S(1)}, bf16[7,32,384]{2,1,0:T(8,128)(2,1)S(1)}, bf16[7,32,384]{2,1,0:T(8,128)(2,1)S(1)}, bf16[7,32,384]{2,1,0:T(8,128)(2,1)S(1)}) custom-call(s32[1]{0:T(128)S(6)} %copy.13.count_ref, bf16[192,576]{1,0:T(8,128)(2,1)S(1)} %copy-done.4, bf16[192,192]{1,0:T(8,128)(2,1)S(1)} %copy-done.7, ...), custom_call_target="tpu_custom_call" | custom-call | flops 100000000 | bytes 1000000 | tf_op jit(solution)/shard_map/pallas_call | solution.py:315
  46.3 1.7 %collective-permute-start.11 = (bf16[7,32,384]{2,1,0:T(8,128)(2,1)S(1)}, bf16[7,32,384]{2,1,0:T(8,128)(2,1)S(1)}, u32[]{:S(2)}, u32[]{:S(2)}) collective-permute-start(bf16[7,32,384]{2,1,0:T(8,128)(2,1)S(1)} %get-tuple-element.46), channel_id=1, source_target_pairs={{0,2},{1,3},{2,0},{3,1},{4,6},{5,7},{6,4},{7,5},{8,10},{9,11},{10,... | collective-permute-start | bytes 516104 | tf_op jit(solution)/shard_map/ppermute | solution.py:514
  49.1 0.9 collective-permute-start.14
  50.0 1.0 %swap_cotangent.1.refs_6_ = bf16[112,32,192]{2,1,0:T(8,128)(2,1)S(1)} custom-call(bf16[32,192,112]{2,1,0:T(8,128)(2,1)S(1)} %bitcast.14), custom_call_target="tpu_custom_call" | custom-call | flops 100000000 | bytes 1000000 | tf_op jit(solution)/shard_map/swap_cotangent/pallas_call | solution.py:347
  51.1 7.8 %shard_map.125 = (bf16[4,448,192]{2,1,0:T(8,128)(2,1)S(1)}, f32[192,768]{1,0:T(8,128)S(1)}, f32[192,768]{1,0:T(8,128)S(1)}) custom-call(bf16[7,32,384]{2,1,0:T(8,128)(2,1)S(1)} %get-tuple-element.37.refs_0_, bf16[7,32,384]{2,1,0:T(8,128)(2,1)S(1)} %get-tuple-element.42.refs_1_, bf16[7,32,384]{2,1,0:T(8,128)(2,1)S(1)} %collective-permute-done.9.refs_2_, ...), custom_call_target="tpu_custom_call" | custom-call | flops 100000000 | bytes 1000000 | tf_op jit(solution)/shard_map/pallas_call | solution.py:484
  58.9 1.2 %collective-permute-done.13.refs_2_ = bf16[7,32,384]{2,1,0:T(8,128)(2,1)S(1)} collective-permute-done((bf16[7,32,384]{2,1,0:T(8,128)(2,1)S(1)}, bf16[7,32,384]{2,1,0:T(8,128)(2,1)S(1)}, u32[]{:S(2)}, u32[]{:S(2)}) %collective-permute-start.13) | collective-permute-done | bytes 172064 | tf_op jit(solution)/shard_map/ppermute | solution.py:514
  60.1 3.3 %collective-permute-done.14.refs_3_ = bf16[7,32,384]{2,1,0:T(8,128)(2,1)S(1)} collective-permute-done((bf16[7,32,384]{2,1,0:T(8,128)(2,1)S(1)}, bf16[7,32,384]{2,1,0:T(8,128)(2,1)S(1)}, u32[]{:S(2)}, u32[]{:S(2)}) %collective-permute-start.14) | collective-permute-done | bytes 172064 | tf_op jit(solution)/shard_map/ppermute | solution.py:514
  63.4 8.1 %shard_map.126 = (bf16[4,448,192]{2,1,0:T(8,128)(2,1)S(1)}, bf16[16,24,384]{2,1,0:T(8,128)(2,1)S(1)}, bf16[16,24,384]{2,1,0:T(8,128)(2,1)S(1)}) custom-call(bf16[7,32,384]{2,1,0:T(8,128)(2,1)S(1)} %collective-permute-done.11.refs_0_, bf16[7,32,384]{2,1,0:T(8,128)(2,1)S(1)} %collective-permute-done.12.refs_1_, ...), custom_call_target="tpu_custom_call" | custom-call | flops 100000000 | bytes 1000000 | tf_op jit(solution)/shard_map/pallas_call | solution.py:484
  72.0 1.2 %collective-permute-done.15.b_ref = bf16[16,24,384]{2,1,0:T(8,128)(2,1)S(1)} collective-permute-done((bf16[16,24,384]{2,1,0:T(8,128)(2,1)S(1)}, bf16[16,24,384]{2,1,0:T(8,128)(2,1)S(1)}, u32[]{:S(2)}, u32[]{:S(2)}) %collective-permute-start.15) | collective-permute-done | bytes 294944 | tf_op jit(solution)/shard_map/ppermute | solution.py:556
  74.0 6.8 %all-to-all-start = ((bf16[16,24,384]{2,1,0:T(8,128)(2,1)}), bf16[16,24,384]{2,1,0:T(8,128)(2,1)S(1)}, u32[]{:S(2)}, u32[]{:S(2)}) async-start(bf16[16,24,384]{2,1,0:T(8,128)(2,1)} %add_pair.1), calls=%async_computation | async-start | bytes 589824 | tf_op jit(solution)/shard_map/all_to_all | solution.py:558
  80.8 2.4 %make_output.1 = bf16[32,192,112]{2,1,0:T(8,128)(2,1)} custom-call(bf16[4,448,192]{2,1,0:T(8,128)(2,1)S(1)} %get-tuple-element.45.refs_0_, bf16[4,448,192]{2,1,0:T(8,128)(2,1)S(1)} %get-tuple-element.52.refs_1_), custom_call_target="tpu_custom_call" | custom-call | flops 100000000 | bytes 1000000 | tf_op jit(solution)/shard_map/make_output/pallas_call | solution.py:390
  83.2 8.8 %all-to-all-done = bf16[16,24,384]{2,1,0:T(8,128)(2,1)S(1)} async-done(((bf16[16,24,384]{2,1,0:T(8,128)(2,1)}), bf16[16,24,384]{2,1,0:T(8,128)(2,1)S(1)}, u32[]{:S(2)}, u32[]{:S(2)}) %all-to-all-start) | async-done | bytes 294944 | tf_op jit(solution)/shard_map/all_to_all | solution.py:558
  (39 shorter events, 5.6 us)
Async XLA Ops:
  1.3 1.4 %copy-start = (bf16[1,32,112,192]{2,3,1,0:T(8,128)(2,1)S(1)}, bf16[1,32,112,192]{2,3,1,0:T(8,128)(2,1)}, u32[]{:S(2)}) copy-start(bf16[1,32,112,192]{2,3,1,0:T(8,128)(2,1)} %param.10) | copy-start | bytes 4128772
  2.7 0.9 %copy-start.5 = (bf16[192,576]{1,0:T(8,128)(2,1)S(1)}, bf16[192,576]{1,0:T(8,128)(2,1)}, u32[]{:S(2)}) copy-start(bf16[192,576]{1,0:T(8,128)(2,1)} %wqkv_ref.5) | copy-start | bytes 663556
  4.5 26.0 %copy-start.4 = (bf16[192,576]{1,0:T(8,128)(2,1)S(1)}, bf16[192,576]{1,0:T(8,128)(2,1)}, u32[]{:S(2)}) copy-start(bf16[192,576]{1,0:T(8,128)(2,1)} %wqkv_ref.7) | copy-start | bytes 663556
  4.5 26.0 %copy-start.7 = (bf16[192,192]{1,0:T(8,128)(2,1)S(1)}, bf16[192,192]{1,0:T(8,128)(2,1)}, u32[]{:S(2)}) copy-start(bf16[192,192]{1,0:T(8,128)(2,1)} %wproj_ref.7) | copy-start | bytes 221188
  9.4 11.2 %collective-permute-start.3 = (bf16[7,16,384]{2,1,0:T(8,128)(2,1)S(1)}, bf16[7,16,384]{2,1,0:T(8,128)(2,1)S(1)}, u32[]{:S(2)}, u32[]{:S(2)}) collective-permute-start(bf16[7,16,384]{2,1,0:T(8,128)(2,1)S(1)} %get-tuple-element.34), channel_id=1, source_target_pairs={{0,1},{1,0},{2,3},{3,2},{4,5},{5,4},{6,7},{7,6},{8,9},{9,8},{10,11... | collective-permute-start | bytes 258056 | tf_op jit(solution)/shard_map/ppermute | solution.py:514
  16.1 34.0 %copy-start.1 = (bf16[1,32,112,192]{2,3,1,0:T(8,128)(2,1)S(1)}, bf16[1,32,112,192]{2,3,1,0:T(8,128)(2,1)}, u32[]{:S(2)}) copy-start(bf16[1,32,112,192]{2,3,1,0:T(8,128)(2,1)} %param.19) | copy-start | bytes 4128772
  16.1 14.4 %collective-permute-start = (bf16[14,16,384]{2,1,0:T(8,128)(2,1)S(1)}, bf16[14,16,384]{2,1,0:T(8,128)(2,1)S(1)}, u32[]{:S(2)}, u32[]{:S(2)}) collective-permute-start(bf16[14,16,384]{2,1,0:T(8,128)(2,1)S(1)} %get-tuple-element.30), channel_id=1, source_target_pairs={{0,1},{1,0},{2,3},{3,2},{4,5},{5,4},{6,7},{7,6},{8,9},{9,8},{10,11... | collective-permute-start | bytes 516104 | tf_op jit(solution)/shard_map/ppermute | solution.py:514
  16.2 14.4 %collective-permute-start.1 = (bf16[14,16,384]{2,1,0:T(8,128)(2,1)S(1)}, bf16[14,16,384]{2,1,0:T(8,128)(2,1)S(1)}, u32[]{:S(2)}, u32[]{:S(2)}) collective-permute-start(bf16[14,16,384]{2,1,0:T(8,128)(2,1)S(1)} %get-tuple-element.31), channel_id=1, source_target_pairs={{0,2},{1,3},{2,0},{3,1},{4,6},{5,7},{6,4},{7,5},{8,10},{9,11},{10,... | collective-permute-start | bytes 516104 | tf_op jit(solution)/shard_map/ppermute | solution.py:514
  19.1 11.4 %collective-permute-start.2 = (bf16[14,16,384]{2,1,0:T(8,128)(2,1)S(1)}, bf16[14,16,384]{2,1,0:T(8,128)(2,1)S(1)}, u32[]{:S(2)}, u32[]{:S(2)}) collective-permute-start(bf16[14,16,384]{2,1,0:T(8,128)(2,1)S(1)} %get-tuple-element.32), channel_id=1, source_target_pairs={{0,3},{1,2},{2,1},{3,0},{4,7},{5,6},{6,5},{7,4},{8,11},{9,10},{10,... | collective-permute-start | bytes 516104 | tf_op jit(solution)/shard_map/ppermute | solution.py:514
  19.1 10.7 %collective-permute-start.4 = (bf16[7,16,384]{2,1,0:T(8,128)(2,1)S(1)}, bf16[7,16,384]{2,1,0:T(8,128)(2,1)S(1)}, u32[]{:S(2)}, u32[]{:S(2)}) collective-permute-start(bf16[7,16,384]{2,1,0:T(8,128)(2,1)S(1)} %get-tuple-element.35), channel_id=1, source_target_pairs={{0,2},{1,3},{2,0},{3,1},{4,6},{5,7},{6,4},{7,5},{8,10},{9,11},{10,... | collective-permute-start | bytes 258056 | tf_op jit(solution)/shard_map/ppermute | solution.py:514
  20.6 9.9 %collective-permute-start.5 = (bf16[7,16,384]{2,1,0:T(8,128)(2,1)S(1)}, bf16[7,16,384]{2,1,0:T(8,128)(2,1)S(1)}, u32[]{:S(2)}, u32[]{:S(2)}) collective-permute-start(bf16[7,16,384]{2,1,0:T(8,128)(2,1)S(1)} %get-tuple-element.36), channel_id=1, source_target_pairs={{0,3},{1,2},{2,1},{3,0},{4,7},{5,6},{6,5},{7,4},{8,11},{9,10},{10,... | collective-permute-start | bytes 258056 | tf_op jit(solution)/shard_map/ppermute | solution.py:514
  34.8 14.4 %collective-permute-start.9 = (bf16[7,32,384]{2,1,0:T(8,128)(2,1)S(1)}, bf16[7,32,384]{2,1,0:T(8,128)(2,1)S(1)}, u32[]{:S(2)}, u32[]{:S(2)}) collective-permute-start(bf16[7,32,384]{2,1,0:T(8,128)(2,1)S(1)} %get-tuple-element.43), channel_id=1, source_target_pairs={{0,1},{1,0},{2,3},{3,2},{4,5},{5,4},{6,7},{7,6},{8,9},{9,8},{10,11... | collective-permute-start | bytes 516104 | tf_op jit(solution)/shard_map/ppermute | solution.py:514
  35.3 1.9 %collective-permute-start.6 = (bf16[7,16,384]{2,1,0:T(8,128)(2,1)S(1)}, bf16[7,16,384]{2,1,0:T(8,128)(2,1)S(1)}, u32[]{:S(2)}, u32[]{:S(2)}) collective-permute-start(bf16[7,16,384]{2,1,0:T(8,128)(2,1)S(1)} %get-tuple-element.39), channel_id=1, source_target_pairs={{0,1},{1,0},{2,3},{3,2},{4,5},{5,4},{6,7},{7,6},{8,9},{9,8},{10,11... | collective-permute-start | bytes 258056 | tf_op jit(solution)/shard_map/ppermute | solution.py:514
  35.3 5.0 %collective-permute-start.7 = (bf16[7,16,384]{2,1,0:T(8,128)(2,1)S(1)}, bf16[7,16,384]{2,1,0:T(8,128)(2,1)S(1)}, u32[]{:S(2)}, u32[]{:S(2)}) collective-permute-start(bf16[7,16,384]{2,1,0:T(8,128)(2,1)S(1)} %get-tuple-element.40), channel_id=1, source_target_pairs={{0,2},{1,3},{2,0},{3,1},{4,6},{5,7},{6,4},{7,5},{8,10},{9,11},{10,... | collective-permute-start | bytes 258056 | tf_op jit(solution)/shard_map/ppermute | solution.py:514
  37.1 4.8 %collective-permute-start.8 = (bf16[7,16,384]{2,1,0:T(8,128)(2,1)S(1)}, bf16[7,16,384]{2,1,0:T(8,128)(2,1)S(1)}, u32[]{:S(2)}, u32[]{:S(2)}) collective-permute-start(bf16[7,16,384]{2,1,0:T(8,128)(2,1)S(1)} %get-tuple-element.41), channel_id=1, source_target_pairs={{0,3},{1,2},{2,1},{3,0},{4,7},{5,6},{6,5},{7,4},{8,11},{9,10},{10,... | collective-permute-start | bytes 258056 | tf_op jit(solution)/shard_map/ppermute | solution.py:514
  46.1 5.0 %collective-permute-start.10 = (bf16[7,32,384]{2,1,0:T(8,128)(2,1)S(1)}, bf16[7,32,384]{2,1,0:T(8,128)(2,1)S(1)}, u32[]{:S(2)}, u32[]{:S(2)}) collective-permute-start(bf16[7,32,384]{2,1,0:T(8,128)(2,1)S(1)} %get-tuple-element.44), channel_id=1, source_target_pairs={{0,1},{1,0},{2,3},{3,2},{4,5},{5,4},{6,7},{7,6},{8,9},{9,8},{10,11... | collective-permute-start | bytes 516104 | tf_op jit(solution)/shard_map/ppermute | solution.py:514
  46.3 12.6 %collective-permute-start.11 = (bf16[7,32,384]{2,1,0:T(8,128)(2,1)S(1)}, bf16[7,32,384]{2,1,0:T(8,128)(2,1)S(1)}, u32[]{:S(2)}, u32[]{:S(2)}) collective-permute-start(bf16[7,32,384]{2,1,0:T(8,128)(2,1)S(1)} %get-tuple-element.46), channel_id=1, source_target_pairs={{0,2},{1,3},{2,0},{3,1},{4,6},{5,7},{6,4},{7,5},{8,10},{9,11},{10,... | collective-permute-start | bytes 516104 | tf_op jit(solution)/shard_map/ppermute | solution.py:514
  47.9 10.9 %collective-permute-start.12 = (bf16[7,32,384]{2,1,0:T(8,128)(2,1)S(1)}, bf16[7,32,384]{2,1,0:T(8,128)(2,1)S(1)}, u32[]{:S(2)}, u32[]{:S(2)}) collective-permute-start(bf16[7,32,384]{2,1,0:T(8,128)(2,1)S(1)} %get-tuple-element.47), channel_id=1, source_target_pairs={{0,2},{1,3},{2,0},{3,1},{4,6},{5,7},{6,4},{7,5},{8,10},{9,11},{10,... | collective-permute-start | bytes 516104 | tf_op jit(solution)/shard_map/ppermute | solution.py:514
  48.3 11.8 %collective-permute-start.13 = (bf16[7,32,384]{2,1,0:T(8,128)(2,1)S(1)}, bf16[7,32,384]{2,1,0:T(8,128)(2,1)S(1)}, u32[]{:S(2)}, u32[]{:S(2)}) collective-permute-start(bf16[7,32,384]{2,1,0:T(8,128)(2,1)S(1)} %get-tuple-element.48), channel_id=1, source_target_pairs={{0,3},{1,2},{2,1},{3,0},{4,7},{5,6},{6,5},{7,4},{8,11},{9,10},{10,... | collective-permute-start | bytes 516104 | tf_op jit(solution)/shard_map/ppermute | solution.py:514
  49.1 14.3 %collective-permute-start.14 = (bf16[7,32,384]{2,1,0:T(8,128)(2,1)S(1)}, bf16[7,32,384]{2,1,0:T(8,128)(2,1)S(1)}, u32[]{:S(2)}, u32[]{:S(2)}) collective-permute-start(bf16[7,32,384]{2,1,0:T(8,128)(2,1)S(1)} %get-tuple-element.49), channel_id=1, source_target_pairs={{0,3},{1,2},{2,1},{3,0},{4,7},{5,6},{6,5},{7,4},{8,11},{9,10},{10,... | collective-permute-start | bytes 516104 | tf_op jit(solution)/shard_map/ppermute | solution.py:514
  50.0 1.0 %copy-start.2 = (bf16[192,768]{1,0:T(8,128)(2,1)S(1)}, bf16[192,768]{1,0:T(8,128)(2,1)}, u32[]{:S(2)}) copy-start(bf16[192,768]{1,0:T(8,128)(2,1)} %refs_4_.3) | copy-start | bytes 884740
  50.0 1.0 %copy-start.3 = (bf16[768,192]{0,1:T(8,128)(2,1)S(1)}, bf16[768,192]{0,1:T(8,128)(2,1)}, u32[]{:S(2)}) copy-start(bf16[768,192]{0,1:T(8,128)(2,1)} %param.18) | copy-start | bytes 884740
  71.5 1.7 %collective-permute-start.15 = (bf16[16,24,384]{2,1,0:T(8,128)(2,1)S(1)}, bf16[16,24,384]{2,1,0:T(8,128)(2,1)S(1)}, u32[]{:S(2)}, u32[]{:S(2)}) collective-permute-start(bf16[16,24,384]{2,1,0:T(8,128)(2,1)S(1)} %get-tuple-element.54), channel_id=1, source_target_pairs={{0,1},{1,0},{2,3},{3,2},{4,5},{5,4},{6,7},{7,6},{8,9},{9,8},{10,11... | collective-permute-start | bytes 884744 | tf_op jit(solution)/shard_map/ppermute | solution.py:556
  74.0 18.0 %all-to-all-start = ((bf16[16,24,384]{2,1,0:T(8,128)(2,1)}), bf16[16,24,384]{2,1,0:T(8,128)(2,1)S(1)}, u32[]{:S(2)}, u32[]{:S(2)}) async-start(bf16[16,24,384]{2,1,0:T(8,128)(2,1)} %add_pair.1), calls=%async_computation | async-start | bytes 589824 | tf_op jit(solution)/shard_map/all_to_all | solution.py:558
  (1 other events, 0.9 us)
where the time goes:
time: 93.1 us; the launch traced here: 92.8 us
  Pallas kernels  39.5 us (42%)
  waiting for transfers between devices  28.2 us (30%)
  starting transfers between devices  18.9 us (20%)
  local copies, waits for them, and re-layouts  3.34 us (4%)
  between operations  2.08 us (2%)
    ppermute x15, waiting for transfers between devices, exchange(): lax.ppermute(pieces[m], CELLS, [(s, s ^ m) for s in range(groups)])  18.3 us
    pallas_call x2, Pallas kernels, dense_part(): pl.pallas_call(functools.partial(dense_kernel, groups, per, chunks, first...  15.9 us
    ppermute x15, starting transfers between devices, exchange(): lax.ppermute(pieces[m], CELLS, [(s, s ^ m) for s in range(groups)])  11.7 us
    pallas_call x2, Pallas kernels, feature_chunk(): pl.pallas_call(functools.partial(feature_kernel, groups, per, base, rows,...  11 us
    all_to_all x1, waiting for transfers between devices, per_device(): lax.all_to_all(pieces, ('tables', 'chips'), split_axis=0, concat_axis=0,...  8.78 us
    pallas_call x2, Pallas kernels, row_chunk(): pl.pallas_call(functools.partial(row_kernel, groups, per, chunks, firsts)...  8.41 us
    all_to_all x1, starting transfers between devices, per_device(): lax.all_to_all(pieces, ('tables', 'chips'), split_axis=0, concat_axis=0,...  6.79 us
    unnamed x16, local copies, waits for them, and re-layouts  3.26 us
  transfers between devices with their start and end apart: 17, of which 8 were waited for; matrix products, arithmetic and copies ran while one was open for 0% of the time, Pallas kernels for 23%

commit v1 on v0

--- a/solution.py
+++ b/solution.py
@@ -13,14 +13,13 @@
 HEAD_DIM = 32
 BF = jnp.bfloat16
 F32 = jnp.float32
-ERFC_K = 3.5
+ERFC_K = 2.9
 ERFC_C = (
-    0.4096238545958983,
-    1.030471715475736,
-    9.637057789606283,
-    -24.75291485624482,
-    177.3359613786631,
-    -181.2859739558248,
+    0.38553786502648235,
+    1.4917549496141058,
+    -0.32977430445565825,
+    21.663540536082817,
+    -21.146073738657215,
 )
 NT = (((1,), (1,)), ((), ()))
 TN = (((0,), (0,)), ((), ()))
@@ -163,12 +162,29 @@
 
 def feature_kernel(groups, per, first, rows, cuts, count_ref, cells_ref, wqkv_ref, wproj_ref, *refs):
     outs = refs[: groups * cuts]
-    q_ref, k_ref, v_ref, att_ref, mid_ref, swap_ref = refs[groups * cuts :]
+    refs = refs[groups * cuts :]
+    parts = 2 if first == 0 else 1
+    waits = [[] for _ in range(parts)]
+    if first == 0:
+        sems, wqkv_buf, wproj_buf, cells_buf = refs[6:]
+        refs = refs[:6]
+        step = rows // parts
+        moves = [(wqkv_ref, wqkv_buf), (wproj_ref, wproj_buf)]
+        for n in range(parts):
+            moves.append((cells_ref.at[pl.ds(n * step, step)], cells_buf.at[pl.ds(n * step, step)]))
+        moves = [pltpu.make_async_copy(a, b, sems.at[n]) for n, (a, b) in enumerate(moves)]
+        for move in moves:
+            move.start()
+        for move in moves[:2]:
+            move.wait()
+        waits = [[move] for move in moves[2:]]
+        wqkv_ref, wproj_ref, cells_ref = wqkv_buf, wproj_buf, cells_buf
+    count = count_ref[0]
+    q_ref, k_ref, v_ref, att_ref, mid_ref, swap_ref = refs
     _, width, feats = cells_ref.shape
     lanes = q_ref.shape[2]
     fg = feats // groups
     half = fg // per
-    count = count_ref[0]
     w_t = wqkv_ref[...].T
     w_qv = jnp.concatenate([w_t[:width], w_t[2 * width :]], axis=0)
     w_k = w_t[width : 2 * width]
@@ -191,9 +207,13 @@
         for at, value in zip(ats, finish_items(att_ref, ats, w_proj_t, flip, own)):
             mid_ref[at] = value
 
-    loop(rows, 8, project)
+    for n, moves in enumerate(waits):
+        for move in moves:
+            move.wait()
+        step = rows // parts
+        project(list(range(n * step, (n + 1) * step)))
     loop(rows, 8, lambda ats: attend(kept, att_ref, ats, ones))
-    loop(rows, 8, finish)
+    loop(rows, 16, finish)
     swap = swap_matrix(rows)
     for f in range(feats // rows):
         block = mid_ref[:, f * rows : (f + 1) * rows, :].reshape(rows * rows, width)
@@ -206,6 +226,7 @@
             outs[c * groups + m][...] = pack([swap_ref[pl.ds(base + q * half, size)] for q in range(per)])
 
 
+BLOCKS = 2
 IN_VMEM = pl.BlockSpec(memory_space=pltpu.VMEM)
 IN_SMEM = pl.BlockSpec(memory_space=pltpu.SMEM)
 
@@ -238,21 +259,25 @@
     _, width, feats = block_t.shape
     half = feats // groups // per
     lanes = -(-feats // 128) * 128
+    outs = [near((half // cuts, rows, per * width))] * (groups * cuts)
+    scratch = attention_scratch(rows, width, lanes, feats)
+    scratch += [pltpu.VMEM((rows, feats, width), BF), pltpu.VMEM((feats, rows, width), BF)]
     operands = [block_t, wqkv, wproj]
     if chunk == 0:
-        base, specs = 0, [pl.BlockSpec((rows, width, feats), lambda i: (0, 0, 0)), IN_VMEM, IN_VMEM]
         operands = [pltpu.with_memory_space_constraint(x, pltpu.HBM) for x in operands]
+        specs = [pl.BlockSpec(memory_space=pltpu.HBM)] * 3
+        scratch += [pltpu.SemaphoreType.DMA((4,))]
+        scratch += [pltpu.VMEM(x.shape, BF) for x in (wqkv, wproj)]
+        scratch += [pltpu.VMEM((rows, width, feats), BF)]
     else:
-        base, specs = chunk * rows, [IN_VMEM] * 3
         operands = bring(*operands)
+        specs = [IN_VMEM] * 3
     return pl.pallas_call(
-        functools.partial(feature_kernel, groups, per, base, rows, cuts),
-        grid=(1,),
+        functools.partial(feature_kernel, groups, per, chunk * rows, rows, cuts),
         in_specs=[IN_SMEM] + specs,
-        out_specs=[IN_VMEM] * (groups * cuts),
-        out_shape=[near((half // cuts, rows, per * width))] * (groups * cuts),
-        scratch_shapes=attention_scratch(rows, width, lanes, feats)
-        + [pltpu.VMEM((rows, feats, width), BF), pltpu.VMEM((feats, rows, width), BF)],
+        out_specs=[IN_VMEM] * len(outs),
+        out_shape=outs,
+        scratch_shapes=scratch,
         compiler_params=PARAMS,
         cost_estimate=cost(10**8),
     )(count, *operands)
@@ -298,7 +323,7 @@
             y_ref[p] = pack(done[a * per : (a + 1) * per])
 
     most = max(1, 1024 // rows)
-    loop(items, min(most, 7), project)
+    loop(items, min(2 * most, 14), project)
     loop(items, min(most, 7), lambda ats: attend(kept, att_ref, ats, ones))
     loop(pairs, min(most, 7), finish)
     for m in range(groups):
@@ -442,7 +467,7 @@
     w_in = win_ref[...]
     w_out_t = woutt_ref[...]
 
-    def step(b, carry):
+    def step(b):
         at = first + b
         feature = (here ^ (at // chunks)) * fg + (at % chunks) * pairs
         normed = n_ref[b]
@@ -454,9 +479,8 @@
         dpre = (dot(cot, w_out_t) * slope).astype(BF)
         gin_ref[...] += dot(normed, dpre, TN)
         gout_ref[...] += dot(cot, act, TN)
-        return carry
-
-    lax.fori_loop(0, blocks, step, 0)
+
+    loop(blocks, BLOCKS, lambda bs: [step(b) for b in bs])
     if last:
         both = pack([(gin_ref[...].T * F32(factor)).astype(BF), (gout_ref[...].T * F32(factor)).astype(BF)])
         both = both.reshape(keep_ref.shape[0], 2, *keep_ref.shape[1:])

time: 93.1 us -> 91.1 us (0.979)
  Pallas kernels: 39.5 us -> 36.7 us
    pallas_call x2, Pallas kernels: 15.9 us -> 14.5 us  [dense_part(): pl.pallas_call(functools.partial(dense_kernel, groups, per, chunks, first...]
  transfers between devices with their start and end apart: 17 -> 17, of which waited for: 8 -> 8; matrix products, arithmetic and copies ran while one was open for 0% -> 0% of each run, Pallas kernels for 23% -> 22%
where the time goes in v1:
time: 91.1 us; the launch traced here: 90.7 us
  Pallas kernels  36.7 us (40%)
  waiting for transfers between devices  29 us (32%)
  starting transfers between devices  18.9 us (21%)
  local copies, waits for them, and re-layouts  3.34 us (4%)
  between operations  2.08 us (2%)
    ppermute x15, waiting for transfers between devices, exchange(): lax.ppermute(pieces[m], CELLS, [(s, s ^ m) for s in range(groups)])  19 us
    pallas_call x2, Pallas kernels, dense_part(): pl.pallas_call(functools.partial(dense_kernel, groups, per, chunks, first...  14.5 us
    ppermute x15, starting transfers between devices, exchange(): lax.ppermute(pieces[m], CELLS, [(s, s ^ m) for s in range(groups)])  11.7 us
    pallas_call x2, Pallas kernels, feature_chunk(): pl.pallas_call(functools.partial(feature_kernel, groups, per, chunk * row...  10 us
    all_to_all x1, waiting for transfers between devices, per_device(): lax.all_to_all(pieces, ('tables', 'chips'), split_axis=0, concat_axis=0,...  8.78 us
    pallas_call x2, Pallas kernels, row_chunk(): pl.pallas_call(functools.partial(row_kernel, groups, per, chunks, firsts)...  7.92 us
    all_to_all x1, starting transfers between devices, per_device(): lax.all_to_all(pieces, ('tables', 'chips'), split_axis=0, concat_axis=0,...  6.77 us
    unnamed x16, local copies, waits for them, and re-layouts  3.26 us
  transfers between devices with their start and end apart: 17, of which 8 were waited for; matrix products, arithmetic and copies ran while one was open for 0% of the time, Pallas kernels for 22%

profile of v1, /device:TPU:0, one launch (start us, length us, event | category | flops | bytes accessed | tf_op | source)
XLA Modules:
  0.0 90.7 jit_solution(3542490367210728997)
XLA Ops:
  1.3 1.4 %copy-done = bf16[1,32,112,192]{2,3,1,0:T(8,128)(2,1)S(1)} copy-done((bf16[1,32,112,192]{2,3,1,0:T(8,128)(2,1)S(1)}, bf16[1,32,112,192]{2,3,1,0:T(8,128)(2,1)}, u32[]{:S(2)}) %copy-start) | copy-done | bytes 1376280
  2.7 0.9 %copy-done.5 = bf16[192,576]{1,0:T(8,128)(2,1)S(1)} copy-done((bf16[192,576]{1,0:T(8,128)(2,1)S(1)}, bf16[192,576]{1,0:T(8,128)(2,1)}, u32[]{:S(2)}) %copy-start.5) | copy-done | bytes 221208
  3.6 0.9 copy-done.6
  4.5 4.1 %shard_map.122 = (bf16[7,16,384]{2,1,0:T(8,128)(2,1)S(1)}, bf16[7,16,384]{2,1,0:T(8,128)(2,1)S(1)}, bf16[7,16,384]{2,1,0:T(8,128)(2,1)S(1)}, bf16[7,16,384]{2,1,...) custom-call(s32[1]{0:T(128)S(6)} %copy.14.count_ref, ...), custom_call_target="tpu_custom_call" | custom-call | flops 100000000 | bytes 1000000 | tf_op jit(solution)/shard_map/pallas_call | solution.py:275
  9.2 5.9 %shard_map.121 = (bf16[14,16,384]{2,1,0:T(8,128)(2,1)S(1)}, bf16[14,16,384]{2,1,0:T(8,128)(2,1)S(1)}, bf16[14,16,384]{2,1,0:T(8,128)(2,1)S(1)}, bf16[14,16,384]{2,1,0:T(8,128)(2,1)S(1)}) custom-call(s32[1]{0:T(128)S(6)} %copy.14.count_ref, bf16[32,192,112]{2,1,0:T(8,128)(2,1)} %bitcast.12, bf16[192,576]{1,0:T(8,128)(2,1)} %wqkv_ref.5, bf16[192,192]{1,0:T(8,128)(2,1)} %wproj_ref.5), custom_call_target="tpu_custom_call" | custom-call | flops 100000000 | bytes 1000000 | tf_op jit(solution)/shard_map/pallas_call | solution.py:275
  15.2 3.0 %collective-permute-start.1 = (bf16[14,16,384]{2,1,0:T(8,128)(2,1)S(1)}, bf16[14,16,384]{2,1,0:T(8,128)(2,1)S(1)}, u32[]{:S(2)}, u32[]{:S(2)}) collective-permute-start(bf16[14,16,384]{2,1,0:T(8,128)(2,1)S(1)} %get-tuple-element.31), channel_id=1, source_target_pairs={{0,2},{1,3},{2,0},{3,1},{4,6},{5,7},{6,4},{7,5},{8,10},{9,11},{10,... | collective-permute-start | bytes 516104 | tf_op jit(solution)/shard_map/ppermute | solution.py:538
  18.2 1.4 %collective-permute-start.4 = (bf16[7,16,384]{2,1,0:T(8,128)(2,1)S(1)}, bf16[7,16,384]{2,1,0:T(8,128)(2,1)S(1)}, u32[]{:S(2)}, u32[]{:S(2)}) collective-permute-start(bf16[7,16,384]{2,1,0:T(8,128)(2,1)S(1)} %get-tuple-element.35), channel_id=1, source_target_pairs={{0,2},{1,3},{2,0},{3,1},{4,6},{5,7},{6,4},{7,5},{8,10},{9,11},{10,... | collective-permute-start | bytes 258056 | tf_op jit(solution)/shard_map/ppermute | solution.py:538
  20.6 8.3 %collective-permute-done.4.refs_6_ = bf16[7,16,384]{2,1,0:T(8,128)(2,1)S(1)} collective-permute-done((bf16[7,16,384]{2,1,0:T(8,128)(2,1)S(1)}, bf16[7,16,384]{2,1,0:T(8,128)(2,1)S(1)}, u32[]{:S(2)}, u32[]{:S(2)}) %collective-permute-start.4) | collective-permute-done | bytes 86048 | tf_op jit(solution)/shard_map/ppermute | solution.py:538
  29.6 3.9 %shard_map.123 = (bf16[7,32,384]{2,1,0:T(8,128)(2,1)S(1)}, bf16[7,32,384]{2,1,0:T(8,128)(2,1)S(1)}, bf16[7,32,384]{2,1,0:T(8,128)(2,1)S(1)}, bf16[7,32,384]{2,1,0:T(8,128)(2,1)S(1)}) custom-call(s32[1]{0:T(128)S(6)} %copy.13.count_ref, bf16[192,576]{1,0:T(8,128)(2,1)S(1)} %copy-done.4, bf16[192,192]{1,0:T(8,128)(2,1)S(1)} %copy-done.7, ...), custom_call_target="tpu_custom_call" | custom-call | flops 100000000 | bytes 1000000 | tf_op jit(solution)/shard_map/pallas_call | solution.py:340
  34.1 1.8 %collective-permute-start.7 = (bf16[7,16,384]{2,1,0:T(8,128)(2,1)S(1)}, bf16[7,16,384]{2,1,0:T(8,128)(2,1)S(1)}, u32[]{:S(2)}, u32[]{:S(2)}) collective-permute-start(bf16[7,16,384]{2,1,0:T(8,128)(2,1)S(1)} %get-tuple-element.40), channel_id=1, source_target_pairs={{0,2},{1,3},{2,0},{3,1},{4,6},{5,7},{6,4},{7,5},{8,10},{9,11},{10,... | collective-permute-start | bytes 258056 | tf_op jit(solution)/shard_map/ppermute | solution.py:538
  35.9 3.2 %collective-permute-done.7.refs_6_ = bf16[7,16,384]{2,1,0:T(8,128)(2,1)S(1)} collective-permute-done((bf16[7,16,384]{2,1,0:T(8,128)(2,1)S(1)}, bf16[7,16,384]{2,1,0:T(8,128)(2,1)S(1)}, u32[]{:S(2)}, u32[]{:S(2)}) %collective-permute-start.7) | collective-permute-done | bytes 86048 | tf_op jit(solution)/shard_map/ppermute | solution.py:538
  39.1 1.5 %collective-permute-done.8.refs_7_ = bf16[7,16,384]{2,1,0:T(8,128)(2,1)S(1)} collective-permute-done((bf16[7,16,384]{2,1,0:T(8,128)(2,1)S(1)}, bf16[7,16,384]{2,1,0:T(8,128)(2,1)S(1)}, u32[]{:S(2)}, u32[]{:S(2)}) %collective-permute-start.8) | collective-permute-done | bytes 86048 | tf_op jit(solution)/shard_map/ppermute | solution.py:538
  40.6 4.0 %shard_map.124 = (bf16[7,32,384]{2,1,0:T(8,128)(2,1)S(1)}, bf16[7,32,384]{2,1,0:T(8,128)(2,1)S(1)}, bf16[7,32,384]{2,1,0:T(8,128)(2,1)S(1)}, bf16[7,32,384]{2,1,0:T(8,128)(2,1)S(1)}) custom-call(s32[1]{0:T(128)S(6)} %copy.13.count_ref, bf16[192,576]{1,0:T(8,128)(2,1)S(1)} %copy-done.4, bf16[192,192]{1,0:T(8,128)(2,1)S(1)} %copy-done.7, ...), custom_call_target="tpu_custom_call" | custom-call | flops 100000000 | bytes 1000000 | tf_op jit(solution)/shard_map/pallas_call | solution.py:340
  44.9 1.7 %collective-permute-start.11 = (bf16[7,32,384]{2,1,0:T(8,128)(2,1)S(1)}, bf16[7,32,384]{2,1,0:T(8,128)(2,1)S(1)}, u32[]{:S(2)}, u32[]{:S(2)}) collective-permute-start(bf16[7,32,384]{2,1,0:T(8,128)(2,1)S(1)} %get-tuple-element.46), channel_id=1, source_target_pairs={{0,2},{1,3},{2,0},{3,1},{4,6},{5,7},{6,4},{7,5},{8,10},{9,11},{10,... | collective-permute-start | bytes 516104 | tf_op jit(solution)/shard_map/ppermute | solution.py:538
  47.7 0.9 %collective-permute-start.14 = (bf16[7,32,384]{2,1,0:T(8,128)(2,1)S(1)}, bf16[7,32,384]{2,1,0:T(8,128)(2,1)S(1)}, u32[]{:S(2)}, u32[]{:S(2)}) collective-permute-start(bf16[7,32,384]{2,1,0:T(8,128)(2,1)S(1)} %get-tuple-element.49), channel_id=1, source_target_pairs={{0,3},{1,2},{2,1},{3,0},{4,7},{5,6},{6,5},{7,4},{8,11},{9,10},{10,... | collective-permute-start | bytes 516104 | tf_op jit(solution)/shard_map/ppermute | solution.py:538
  48.6 1.0 %swap_cotangent.1.refs_6_ = bf16[112,32,192]{2,1,0:T(8,128)(2,1)S(1)} custom-call(bf16[32,192,112]{2,1,0:T(8,128)(2,1)S(1)} %bitcast.14), custom_call_target="tpu_custom_call" | custom-call | flops 100000000 | bytes 1000000 | tf_op jit(solution)/shard_map/swap_cotangent/pallas_call | solution.py:372
  49.7 7.0 %shard_map.125 = (bf16[4,448,192]{2,1,0:T(8,128)(2,1)S(1)}, f32[192,768]{1,0:T(8,128)S(1)}, f32[192,768]{1,0:T(8,128)S(1)}) custom-call(bf16[7,32,384]{2,1,0:T(8,128)(2,1)S(1)} %get-tuple-element.37.refs_0_, bf16[7,32,384]{2,1,0:T(8,128)(2,1)S(1)} %get-tuple-element.42.refs_1_, bf16[7,32,384]{2,1,0:T(8,128)(2,1)S(1)} %collective-permute-done.9.refs_2_, ...), custom_call_target="tpu_custom_call" | custom-call | flops 100000000 | bytes 1000000 | tf_op jit(solution)/shard_map/pallas_call | solution.py:508
  56.7 2.0 %collective-permute-done.13.refs_2_ = bf16[7,32,384]{2,1,0:T(8,128)(2,1)S(1)} collective-permute-done((bf16[7,32,384]{2,1,0:T(8,128)(2,1)S(1)}, bf16[7,32,384]{2,1,0:T(8,128)(2,1)S(1)}, u32[]{:S(2)}, u32[]{:S(2)}) %collective-permute-start.13) | collective-permute-done | bytes 172064 | tf_op jit(solution)/shard_map/ppermute | solution.py:538
  58.7 3.3 %collective-permute-done.14.refs_3_ = bf16[7,32,384]{2,1,0:T(8,128)(2,1)S(1)} collective-permute-done((bf16[7,32,384]{2,1,0:T(8,128)(2,1)S(1)}, bf16[7,32,384]{2,1,0:T(8,128)(2,1)S(1)}, u32[]{:S(2)}, u32[]{:S(2)}) %collective-permute-start.14) | collective-permute-done | bytes 172064 | tf_op jit(solution)/shard_map/ppermute | solution.py:538
  62.0 7.5 %shard_map.126 = (bf16[4,448,192]{2,1,0:T(8,128)(2,1)S(1)}, bf16[16,24,384]{2,1,0:T(8,128)(2,1)S(1)}, bf16[16,24,384]{2,1,0:T(8,128)(2,1)S(1)}) custom-call(bf16[7,32,384]{2,1,0:T(8,128)(2,1)S(1)} %collective-permute-done.11.refs_0_, bf16[7,32,384]{2,1,0:T(8,128)(2,1)S(1)} %collective-permute-done.12.refs_1_, ...), custom_call_target="tpu_custom_call" | custom-call | flops 100000000 | bytes 1000000 | tf_op jit(solution)/shard_map/pallas_call | solution.py:508
  70.0 1.2 %collective-permute-done.15.b_ref = bf16[16,24,384]{2,1,0:T(8,128)(2,1)S(1)} collective-permute-done((bf16[16,24,384]{2,1,0:T(8,128)(2,1)S(1)}, bf16[16,24,384]{2,1,0:T(8,128)(2,1)S(1)}, u32[]{:S(2)}, u32[]{:S(2)}) %collective-permute-start.15) | collective-permute-done | bytes 294944 | tf_op jit(solution)/shard_map/ppermute | solution.py:580
  72.0 6.8 %all-to-all-start = ((bf16[16,24,384]{2,1,0:T(8,128)(2,1)}), bf16[16,24,384]{2,1,0:T(8,128)(2,1)S(1)}, u32[]{:S(2)}, u32[]{:S(2)}) async-start(bf16[16,24,384]{2,1,0:T(8,128)(2,1)} %add_pair.1), calls=%async_computation | async-start | bytes 589824 | tf_op jit(solution)/shard_map/all_to_all | solution.py:582
  78.7 2.4 %make_output.1 = bf16[32,192,112]{2,1,0:T(8,128)(2,1)} custom-call(bf16[4,448,192]{2,1,0:T(8,128)(2,1)S(1)} %get-tuple-element.45.refs_0_, bf16[4,448,192]{2,1,0:T(8,128)(2,1)S(1)} %get-tuple-element.52.refs_1_), custom_call_target="tpu_custom_call" | custom-call | flops 100000000 | bytes 1000000 | tf_op jit(solution)/shard_map/make_output/pallas_call | solution.py:415
  81.2 8.8 %all-to-all-done = bf16[16,24,384]{2,1,0:T(8,128)(2,1)S(1)} async-done(((bf16[16,24,384]{2,1,0:T(8,128)(2,1)}), bf16[16,24,384]{2,1,0:T(8,128)(2,1)S(1)}, u32[]{:S(2)}, u32[]{:S(2)}) %all-to-all-start) | async-done | bytes 294944 | tf_op jit(solution)/shard_map/all_to_all | solution.py:582
  (39 shorter events, 5.6 us)
Async XLA Ops:
  1.3 1.4 %copy-start = (bf16[1,32,112,192]{2,3,1,0:T(8,128)(2,1)S(1)}, bf16[1,32,112,192]{2,3,1,0:T(8,128)(2,1)}, u32[]{:S(2)}) copy-start(bf16[1,32,112,192]{2,3,1,0:T(8,128)(2,1)} %param.10) | copy-start | bytes 4128772
  2.7 0.9 %copy-start.5 = (bf16[192,576]{1,0:T(8,128)(2,1)S(1)}, bf16[192,576]{1,0:T(8,128)(2,1)}, u32[]{:S(2)}) copy-start(bf16[192,576]{1,0:T(8,128)(2,1)} %wqkv_ref.5) | copy-start | bytes 663556
  4.5 25.1 %copy-start.4 = (bf16[192,576]{1,0:T(8,128)(2,1)S(1)}, bf16[192,576]{1,0:T(8,128)(2,1)}, u32[]{:S(2)}) copy-start(bf16[192,576]{1,0:T(8,128)(2,1)} %wqkv_ref.7) | copy-start | bytes 663556
  4.5 25.1 %copy-start.7 = (bf16[192,192]{1,0:T(8,128)(2,1)S(1)}, bf16[192,192]{1,0:T(8,128)(2,1)}, u32[]{:S(2)}) copy-start(bf16[192,192]{1,0:T(8,128)(2,1)} %wproj_ref.7) | copy-start | bytes 221188
  8.7 11.0 %collective-permute-start.3 = (bf16[7,16,384]{2,1,0:T(8,128)(2,1)S(1)}, bf16[7,16,384]{2,1,0:T(8,128)(2,1)S(1)}, u32[]{:S(2)}, u32[]{:S(2)}) collective-permute-start(bf16[7,16,384]{2,1,0:T(8,128)(2,1)S(1)} %get-tuple-element.34), channel_id=1, source_target_pairs={{0,1},{1,0},{2,3},{3,2},{4,5},{5,4},{6,7},{7,6},{8,9},{9,8},{10,11... | collective-permute-start | bytes 258056 | tf_op jit(solution)/shard_map/ppermute | solution.py:538
  15.1 33.5 %copy-start.1 = (bf16[1,32,112,192]{2,3,1,0:T(8,128)(2,1)S(1)}, bf16[1,32,112,192]{2,3,1,0:T(8,128)(2,1)}, u32[]{:S(2)}) copy-start(bf16[1,32,112,192]{2,3,1,0:T(8,128)(2,1)} %param.19) | copy-start | bytes 4128772
  15.1 14.4 %collective-permute-start = (bf16[14,16,384]{2,1,0:T(8,128)(2,1)S(1)}, bf16[14,16,384]{2,1,0:T(8,128)(2,1)S(1)}, u32[]{:S(2)}, u32[]{:S(2)}) collective-permute-start(bf16[14,16,384]{2,1,0:T(8,128)(2,1)S(1)} %get-tuple-element.30), channel_id=1, source_target_pairs={{0,1},{1,0},{2,3},{3,2},{4,5},{5,4},{6,7},{7,6},{8,9},{9,8},{10,11... | collective-permute-start | bytes 516104 | tf_op jit(solution)/shard_map/ppermute | solution.py:538
  15.2 14.4 %collective-permute-start.1 = (bf16[14,16,384]{2,1,0:T(8,128)(2,1)S(1)}, bf16[14,16,384]{2,1,0:T(8,128)(2,1)S(1)}, u32[]{:S(2)}, u32[]{:S(2)}) collective-permute-start(bf16[14,16,384]{2,1,0:T(8,128)(2,1)S(1)} %get-tuple-element.31), channel_id=1, source_target_pairs={{0,2},{1,3},{2,0},{3,1},{4,6},{5,7},{6,4},{7,5},{8,10},{9,11},{10,... | collective-permute-start | bytes 516104 | tf_op jit(solution)/shard_map/ppermute | solution.py:538
  18.2 11.4 %collective-permute-start.2 = (bf16[14,16,384]{2,1,0:T(8,128)(2,1)S(1)}, bf16[14,16,384]{2,1,0:T(8,128)(2,1)S(1)}, u32[]{:S(2)}, u32[]{:S(2)}) collective-permute-start(bf16[14,16,384]{2,1,0:T(8,128)(2,1)S(1)} %get-tuple-element.32), channel_id=1, source_target_pairs={{0,3},{1,2},{2,1},{3,0},{4,7},{5,6},{6,5},{7,4},{8,11},{9,10},{10,... | collective-permute-start | bytes 516104 | tf_op jit(solution)/shard_map/ppermute | solution.py:538
  18.2 10.7 %collective-permute-start.4 = (bf16[7,16,384]{2,1,0:T(8,128)(2,1)S(1)}, bf16[7,16,384]{2,1,0:T(8,128)(2,1)S(1)}, u32[]{:S(2)}, u32[]{:S(2)}) collective-permute-start(bf16[7,16,384]{2,1,0:T(8,128)(2,1)S(1)} %get-tuple-element.35), channel_id=1, source_target_pairs={{0,2},{1,3},{2,0},{3,1},{4,6},{5,7},{6,4},{7,5},{8,10},{9,11},{10,... | collective-permute-start | bytes 258056 | tf_op jit(solution)/shard_map/ppermute | solution.py:538
  19.6 9.9 %collective-permute-start.5 = (bf16[7,16,384]{2,1,0:T(8,128)(2,1)S(1)}, bf16[7,16,384]{2,1,0:T(8,128)(2,1)S(1)}, u32[]{:S(2)}, u32[]{:S(2)}) collective-permute-start(bf16[7,16,384]{2,1,0:T(8,128)(2,1)S(1)} %get-tuple-element.36), channel_id=1, source_target_pairs={{0,3},{1,2},{2,1},{3,0},{4,7},{5,6},{6,5},{7,4},{8,11},{9,10},{10,... | collective-permute-start | bytes 258056 | tf_op jit(solution)/shard_map/ppermute | solution.py:538
  33.5 14.2 %collective-permute-start.9 = (bf16[7,32,384]{2,1,0:T(8,128)(2,1)S(1)}, bf16[7,32,384]{2,1,0:T(8,128)(2,1)S(1)}, u32[]{:S(2)}, u32[]{:S(2)}) collective-permute-start(bf16[7,32,384]{2,1,0:T(8,128)(2,1)S(1)} %get-tuple-element.43), channel_id=1, source_target_pairs={{0,1},{1,0},{2,3},{3,2},{4,5},{5,4},{6,7},{7,6},{8,9},{9,8},{10,11... | collective-permute-start | bytes 516104 | tf_op jit(solution)/shard_map/ppermute | solution.py:538
  34.0 1.9 %collective-permute-start.6 = (bf16[7,16,384]{2,1,0:T(8,128)(2,1)S(1)}, bf16[7,16,384]{2,1,0:T(8,128)(2,1)S(1)}, u32[]{:S(2)}, u32[]{:S(2)}) collective-permute-start(bf16[7,16,384]{2,1,0:T(8,128)(2,1)S(1)} %get-tuple-element.39), channel_id=1, source_target_pairs={{0,1},{1,0},{2,3},{3,2},{4,5},{5,4},{6,7},{7,6},{8,9},{9,8},{10,11... | collective-permute-start | bytes 258056 | tf_op jit(solution)/shard_map/ppermute | solution.py:538
  34.1 5.0 %collective-permute-start.7 = (bf16[7,16,384]{2,1,0:T(8,128)(2,1)S(1)}, bf16[7,16,384]{2,1,0:T(8,128)(2,1)S(1)}, u32[]{:S(2)}, u32[]{:S(2)}) collective-permute-start(bf16[7,16,384]{2,1,0:T(8,128)(2,1)S(1)} %get-tuple-element.40), channel_id=1, source_target_pairs={{0,2},{1,3},{2,0},{3,1},{4,6},{5,7},{6,4},{7,5},{8,10},{9,11},{10,... | collective-permute-start | bytes 258056 | tf_op jit(solution)/shard_map/ppermute | solution.py:538
  35.8 4.8 %collective-permute-start.8 = (bf16[7,16,384]{2,1,0:T(8,128)(2,1)S(1)}, bf16[7,16,384]{2,1,0:T(8,128)(2,1)S(1)}, u32[]{:S(2)}, u32[]{:S(2)}) collective-permute-start(bf16[7,16,384]{2,1,0:T(8,128)(2,1)S(1)} %get-tuple-element.41), channel_id=1, source_target_pairs={{0,3},{1,2},{2,1},{3,0},{4,7},{5,6},{6,5},{7,4},{8,11},{9,10},{10,... | collective-permute-start | bytes 258056 | tf_op jit(solution)/shard_map/ppermute | solution.py:538
  44.7 5.0 %collective-permute-start.10 = (bf16[7,32,384]{2,1,0:T(8,128)(2,1)S(1)}, bf16[7,32,384]{2,1,0:T(8,128)(2,1)S(1)}, u32[]{:S(2)}, u32[]{:S(2)}) collective-permute-start(bf16[7,32,384]{2,1,0:T(8,128)(2,1)S(1)} %get-tuple-element.44), channel_id=1, source_target_pairs={{0,1},{1,0},{2,3},{3,2},{4,5},{5,4},{6,7},{7,6},{8,9},{9,8},{10,11... | collective-permute-start | bytes 516104 | tf_op jit(solution)/shard_map/ppermute | solution.py:538
  44.9 11.8 %collective-permute-start.11 = (bf16[7,32,384]{2,1,0:T(8,128)(2,1)S(1)}, bf16[7,32,384]{2,1,0:T(8,128)(2,1)S(1)}, u32[]{:S(2)}, u32[]{:S(2)}) collective-permute-start(bf16[7,32,384]{2,1,0:T(8,128)(2,1)S(1)} %get-tuple-element.46), channel_id=1, source_target_pairs={{0,2},{1,3},{2,0},{3,1},{4,6},{5,7},{6,4},{7,5},{8,10},{9,11},{10,... | collective-permute-start | bytes 516104 | tf_op jit(solution)/shard_map/ppermute | solution.py:538
  46.5 10.2 %collective-permute-start.12 = (bf16[7,32,384]{2,1,0:T(8,128)(2,1)S(1)}, bf16[7,32,384]{2,1,0:T(8,128)(2,1)S(1)}, u32[]{:S(2)}, u32[]{:S(2)}) collective-permute-start(bf16[7,32,384]{2,1,0:T(8,128)(2,1)S(1)} %get-tuple-element.47), channel_id=1, source_target_pairs={{0,2},{1,3},{2,0},{3,1},{4,6},{5,7},{6,4},{7,5},{8,10},{9,11},{10,... | collective-permute-start | bytes 516104 | tf_op jit(solution)/shard_map/ppermute | solution.py:538
  46.9 11.8 %collective-permute-start.13 = (bf16[7,32,384]{2,1,0:T(8,128)(2,1)S(1)}, bf16[7,32,384]{2,1,0:T(8,128)(2,1)S(1)}, u32[]{:S(2)}, u32[]{:S(2)}) collective-permute-start(bf16[7,32,384]{2,1,0:T(8,128)(2,1)S(1)} %get-tuple-element.48), channel_id=1, source_target_pairs={{0,3},{1,2},{2,1},{3,0},{4,7},{5,6},{6,5},{7,4},{8,11},{9,10},{10,... | collective-permute-start | bytes 516104 | tf_op jit(solution)/shard_map/ppermute | solution.py:538
  47.7 14.3 %collective-permute-start.14 = (bf16[7,32,384]{2,1,0:T(8,128)(2,1)S(1)}, bf16[7,32,384]{2,1,0:T(8,128)(2,1)S(1)}, u32[]{:S(2)}, u32[]{:S(2)}) collective-permute-start(bf16[7,32,384]{2,1,0:T(8,128)(2,1)S(1)} %get-tuple-element.49), channel_id=1, source_target_pairs={{0,3},{1,2},{2,1},{3,0},{4,7},{5,6},{6,5},{7,4},{8,11},{9,10},{10,... | collective-permute-start | bytes 516104 | tf_op jit(solution)/shard_map/ppermute | solution.py:538
  48.6 1.0 %copy-start.2 = (bf16[192,768]{1,0:T(8,128)(2,1)S(1)}, bf16[192,768]{1,0:T(8,128)(2,1)}, u32[]{:S(2)}) copy-start(bf16[192,768]{1,0:T(8,128)(2,1)} %refs_4_.3) | copy-start | bytes 884740
  48.6 1.1 %copy-start.3 = (bf16[768,192]{0,1:T(8,128)(2,1)S(1)}, bf16[768,192]{0,1:T(8,128)(2,1)}, u32[]{:S(2)}) copy-start(bf16[768,192]{0,1:T(8,128)(2,1)} %param.18) | copy-start | bytes 884740
  69.5 1.7 %collective-permute-start.15 = (bf16[16,24,384]{2,1,0:T(8,128)(2,1)S(1)}, bf16[16,24,384]{2,1,0:T(8,128)(2,1)S(1)}, u32[]{:S(2)}, u32[]{:S(2)}) collective-permute-start(bf16[16,24,384]{2,1,0:T(8,128)(2,1)S(1)} %get-tuple-element.54), channel_id=1, source_target_pairs={{0,1},{1,0},{2,3},{3,2},{4,5},{5,4},{6,7},{7,6},{8,9},{9,8},{10,11... | collective-permute-start | bytes 884744 | tf_op jit(solution)/shard_map/ppermute | solution.py:580
  72.0 18.0 %all-to-all-start = ((bf16[16,24,384]{2,1,0:T(8,128)(2,1)}), bf16[16,24,384]{2,1,0:T(8,128)(2,1)S(1)}, u32[]{:S(2)}, u32[]{:S(2)}) async-start(bf16[16,24,384]{2,1,0:T(8,128)(2,1)} %add_pair.1), calls=%async_computation | async-start | bytes 589824 | tf_op jit(solution)/shard_map/all_to_all | solution.py:582
  (1 other events, 0.9 us)

commit v2 on v1

--- a/solution.py
+++ b/solution.py
@@ -163,7 +163,7 @@
 def feature_kernel(groups, per, first, rows, cuts, count_ref, cells_ref, wqkv_ref, wproj_ref, *refs):
     outs = refs[: groups * cuts]
     refs = refs[groups * cuts :]
-    parts = 2 if first == 0 else 1
+    parts = 1
     waits = [[] for _ in range(parts)]
     if first == 0:
         sems, wqkv_buf, wproj_buf, cells_buf = refs[6:]
@@ -381,7 +381,7 @@
     )(*bring(array_t))
 
 
-def output_kernel(groups, per, chunks, *refs):
+def output_kernel(groups, per, chunks, spots, *refs):
     parts, (out_ref, f_ref, y_ref) = refs[:-3], refs[-3:]
     feats, local, width = f_ref.shape
     half = feats // groups // per
@@ -389,11 +389,9 @@
     size = pairs * local
     lanes = -(-feats // 128) * 128
     here = cell_index()
-    count = parts[0].shape[0]
-    for n, part in enumerate(parts):
-        for b in range(count):
-            at = n * count + b
-            base = (here ^ (at // chunks)) * (half * per) + (at % chunks) * pairs
+    for (first_m, some, first_j), part in zip(spots, parts):
+        for b in range(part.shape[0]):
+            base = (here ^ (first_m + b // some)) * (half * per) + (first_j + b % some) * pairs
             for q in range(per):
                 rows = part[b, q * size : (q + 1) * size].reshape(pairs, local, width)
                 f_ref[pl.ds(base + q * half, pairs)] = rows
@@ -410,10 +408,10 @@
         out_ref[r] = y.T[:, :feats]
 
 
-def make_output(parts, groups, per, chunks, feats, local):
+def make_output(parts, spots, groups, per, chunks, feats, local):
     width = parts[0].shape[-1]
     return pl.pallas_call(
-        functools.partial(output_kernel, groups, per, chunks),
+        functools.partial(output_kernel, groups, per, chunks, spots),
         in_specs=[IN_VMEM] * len(parts),
         out_specs=IN_VMEM,
         out_shape=jax.ShapeDtypeStruct((local, width, feats), BF),
@@ -436,17 +434,15 @@
     return pre * cdf, cdf + pre * (bell * F32(1.0 / math.sqrt(2.0 * math.pi)))
 
 
-def dense_kernel(groups, per, chunks, first, factor, *refs):
+def dense_kernel(groups, per, spot, fresh, factor, *refs):
+    first_m, chunks, first_j = spot
     last = factor is not None
     blocks = refs[-1].shape[0]
     ins = refs[:blocks]
     win_ref, woutt_ref, cot_ref = refs[blocks : blocks + 3]
-    rest = refs[blocks + 3 :]
-    if first > 0:
-        prev_in, prev_out = rest[:2]
-        rest = rest[2:]
+    rest = refs[blocks + (3 if fresh else 5) :]
     if last:
-        out_ref, keep_ref, send_ref, gin_ref, gout_ref, n_ref = rest
+        out_ref, gin_ref, gout_ref, keep_ref, send_ref, n_ref = rest
     else:
         out_ref, gin_ref, gout_ref, n_ref = rest
     pairs, local, _ = ins[0].shape
@@ -458,18 +454,15 @@
     for b in range(blocks):
         for q, part in enumerate(unpack(ins[b][...], per, width)):
             n_ref[b, q * size : (q + 1) * size] = part.reshape(size, width)
-    if first > 0:
-        gin_ref[...] = prev_in[...]
-        gout_ref[...] = prev_out[...]
-    else:
+    if fresh:
         gin_ref[...] = jnp.zeros_like(gin_ref)
         gout_ref[...] = jnp.zeros_like(gout_ref)
     w_in = win_ref[...]
     w_out_t = woutt_ref[...]
 
     def step(b):
-        at = first + b
-        feature = (here ^ (at // chunks)) * fg + (at % chunks) * pairs
+        group = here ^ (first_m + b // chunks)
+        feature = group * fg + (first_j + b % chunks) * pairs
         normed = n_ref[b]
         cot = [cot_ref[pl.ds(feature + q * half, pairs)].reshape(size, width) for q in range(per)]
         cot = jnp.concatenate(cot, axis=0)
@@ -489,28 +482,26 @@
         send_ref[...] = jnp.where(even, both[:, 1], both[:, 0])
 
 
-def dense_part(blocks, cot_t, w_in, w_out_t, prev, groups, per, chunks, first, factor, shares):
+def dense_part(blocks, cot_t, w_in, w_out_t, prev, groups, per, spot, factor, shares):
     pairs, local, _ = blocks[0].shape
     width, hid = w_in.shape
     size = per * pairs * local
     count = len(blocks)
-    outs = [near((count, size, width))]
+    outs = [near((count, size, width))] + [near((width, hid), F32)] * 2
     operands = list(blocks) + [w_in, w_out_t, cot_t]
-    if first > 0:
+    alias = {}
+    if prev is not None:
+        alias = {len(operands) + n: 1 + n for n in range(2)}
         operands += list(prev)
-    scratch = []
-    if factor is None:
-        outs += [near((width, hid), F32)] * 2
-    else:
+    if factor is not None:
         outs += [near((shares // 2, hid // shares, 2 * width))] * 2
-        scratch = [pltpu.VMEM((width, hid), F32)] * 2
-    scratch += [pltpu.VMEM((count, size, width), BF)]
     return pl.pallas_call(
-        functools.partial(dense_kernel, groups, per, chunks, first, factor),
+        functools.partial(dense_kernel, groups, per, spot, prev is None, factor),
         in_specs=[IN_VMEM] * len(operands),
         out_specs=[IN_VMEM] * len(outs),
         out_shape=outs,
-        scratch_shapes=scratch,
+        input_output_aliases=alias,
+        scratch_shapes=[pltpu.VMEM((count, size, width), BF)],
         compiler_params=PARAMS,
         cost_estimate=cost(10**8),
     )(*bring(*operands))
@@ -525,7 +516,7 @@
         add_kernel,
         in_specs=[IN_VMEM] * 2,
         out_specs=IN_VMEM,
-        out_shape=jax.ShapeDtypeStruct(a.shape, BF),
+        out_shape=near(a.shape),
         compiler_params=PARAMS,
         cost_estimate=cost(10**6),
         name="add_pair",
@@ -571,17 +562,22 @@
         back.append(exchange(done, groups))
     w_out_t = w_out.T
     shares = tables * groups
-    blocks = [back[j][m] for m in range(groups) for j in range(feat_chunks)]
-    cut = len(blocks) // 2
-    args = (cot_t, w_in, w_out_t)
-    shape = (groups, per, feat_chunks)
-    out_0, *partial = dense_part(blocks[:cut], *args, None, *shape, 0, None, shares)
-    out_1, keep, send = dense_part(blocks[cut:], *args, partial, *shape, cut, factor, shares)
+    near_by = groups // 2
+    spots = [(0, feat_chunks, 0)] + [(near_by, 1, j) for j in range(feat_chunks)]
+    parts = []
+    grads = None
+    for spot in spots:
+        first_m, some, first_j = spot
+        blocks = [back[first_j + j][first_m + m] for m in range(near_by) for j in range(some)]
+        scale = factor if spot == spots[-1] else None
+        made, *grads = dense_part(blocks, cot_t, w_in, w_out_t, grads, groups, per, spot, scale, shares)
+        parts.append(made)
+    keep, send = grads[2:]
     other = lax.ppermute(send, "core", [(0, 1), (1, 0)])
     pieces = add_pair(keep, other)
     total = lax.all_to_all(pieces, ("tables", "chips"), split_axis=0, concat_axis=0, tiled=True)
     total = jnp.sum(total.astype(F32), axis=0)
-    output = make_output([out_0, out_1], *shape, feats, local)
+    output = make_output(parts, spots, groups, per, feat_chunks, feats, local)
     grad_in, grad_out = unpack(total, 2, width)
     return (jnp.swapaxes(output, 1, 2)[None], grad_in.T, grad_out)
 

time: 91.1 us -> 86.9 us (0.954)
  waiting for transfers between devices: 29 us -> 25.9 us
    ppermute x15, waiting for transfers between devices: 19 us -> 15.9 us  [exchange(): lax.ppermute(pieces[m], CELLS, [(s, s ^ m) for s in range(groups)])]
    pallas_call x3 -> x4, Pallas kernels: 16.9 us -> 16.6 us  [the longest x3 14.2 us: dense_part(): pl.pallas_call(functools.partial(dense_kernel, groups, per, spot, prev is...]
  transfers between devices with their start and end apart: 17 -> 17, of which waited for: 8 -> 7; matrix products, arithmetic and copies ran while one was open for 0% -> 0% of each run, Pallas kernels for 22% -> 27%
where the time goes in v2:
time: 86.9 us; the launch traced here: 86.5 us
  Pallas kernels  35.9 us (41%)
  waiting for transfers between devices  25.9 us (30%)
  starting transfers between devices  18.7 us (22%)
  local copies, waits for them, and re-layouts  3.34 us (4%)
  between operations  2.09 us (2%)
    ppermute x15, waiting for transfers between devices, exchange(): lax.ppermute(pieces[m], CELLS, [(s, s ^ m) for s in range(groups)])  15.9 us
    pallas_call x3, Pallas kernels, dense_part(): pl.pallas_call(functools.partial(dense_kernel, groups, per, spot, prev is...  14.2 us
    ppermute x15, starting transfers between devices, exchange(): lax.ppermute(pieces[m], CELLS, [(s, s ^ m) for s in range(groups)])  11.4 us
    pallas_call x2, Pallas kernels, feature_chunk(): pl.pallas_call(functools.partial(feature_kernel, groups, per, chunk * row...  9.59 us
    all_to_all x1, waiting for transfers between devices, per_device(): lax.all_to_all(pieces, ('tables', 'chips'), split_axis=0, concat_axis=0,...  8.78 us
    pallas_call x2, Pallas kernels, row_chunk(): pl.pallas_call(functools.partial(row_kernel, groups, per, chunks, firsts)...  7.91 us
    all_to_all x1, starting transfers between devices, per_device(): lax.all_to_all(pieces, ('tables', 'chips'), split_axis=0, concat_axis=0,...  6.77 us
    unnamed x16, local copies, waits for them, and re-layouts  3.26 us
  transfers between devices with their start and end apart: 17, of which 7 were waited for; matrix products, arithmetic and copies ran while one was open for 0% of the time, Pallas kernels for 27%

profile of v2, /device:TPU:0, one launch (start us, length us, event | category | flops | bytes accessed | tf_op | source)
XLA Modules:
  0.0 86.5 jit_solution(7041748611667639654)
XLA Ops:
  1.3 1.4 %copy-done = bf16[1,32,112,192]{2,3,1,0:T(8,128)(2,1)S(1)} copy-done((bf16[1,32,112,192]{2,3,1,0:T(8,128)(2,1)S(1)}, bf16[1,32,112,192]{2,3,1,0:T(8,128)(2,1)}, u32[]{:S(2)}) %copy-start) | copy-done | bytes 1376280
  2.7 0.9 %copy-done.5 = bf16[192,576]{1,0:T(8,128)(2,1)S(1)} copy-done((bf16[192,576]{1,0:T(8,128)(2,1)S(1)}, bf16[192,576]{1,0:T(8,128)(2,1)}, u32[]{:S(2)}) %copy-start.5) | copy-done | bytes 221208
  3.6 0.9 %copy-done.6 = bf16[192,192]{1,0:T(8,128)(2,1)S(1)} copy-done((bf16[192,192]{1,0:T(8,128)(2,1)S(1)}, bf16[192,192]{1,0:T(8,128)(2,1)}, u32[]{:S(2)}) %copy-start.6) | copy-done | bytes 73752
  4.5 4.1 %shard_map.122 = (bf16[7,16,384]{2,1,0:T(8,128)(2,1)S(1)}, bf16[7,16,384]{2,1,0:T(8,128)(2,1)S(1)}, bf16[7,16,384]{2,1,0:T(8,128)(2,1)S(1)}, bf16[7,16,384]{2,1,...) custom-call(s32[1]{0:T(128)S(6)} %copy.22.count_ref, ...), custom_call_target="tpu_custom_call" | custom-call | flops 100000000 | bytes 1000000 | tf_op jit(solution)/shard_map/pallas_call | solution.py:275
  9.2 5.5 %shard_map.121 = (bf16[14,16,384]{2,1,0:T(8,128)(2,1)S(1)}, bf16[14,16,384]{2,1,0:T(8,128)(2,1)S(1)}, bf16[14,16,384]{2,1,0:T(8,128)(2,1)S(1)}, bf16[14,16,384]{2,1,0:T(8,128)(2,1)S(1)}) custom-call(s32[1]{0:T(128)S(6)} %copy.22.count_ref, bf16[32,192,112]{2,1,0:T(8,128)(2,1)} %bitcast.12, bf16[192,576]{1,0:T(8,128)(2,1)} %wqkv_ref.5, bf16[192,192]{1,0:T(8,128)(2,1)} %wproj_ref.5), custom_call_target="tpu_custom_call" | custom-call | flops 100000000 | bytes 1000000 | tf_op jit(solution)/shard_map/pallas_call | solution.py:275
  14.8 3.0 %collective-permute-start.1 = (bf16[14,16,384]{2,1,0:T(8,128)(2,1)S(1)}, bf16[14,16,384]{2,1,0:T(8,128)(2,1)S(1)}, u32[]{:S(2)}, u32[]{:S(2)}) collective-permute-start(bf16[14,16,384]{2,1,0:T(8,128)(2,1)S(1)} %get-tuple-element.34), channel_id=1, source_target_pairs={{0,2},{1,3},{2,0},{3,1},{4,6},{5,7},{6,4},{7,5},{8,10},{9,11},{10,... | collective-permute-start | bytes 516104 | tf_op jit(solution)/shard_map/ppermute | solution.py:529
  17.8 1.4 %collective-permute-start.7 = (bf16[7,16,384]{2,1,0:T(8,128)(2,1)S(1)}, bf16[7,16,384]{2,1,0:T(8,128)(2,1)S(1)}, u32[]{:S(2)}, u32[]{:S(2)}) collective-permute-start(bf16[7,16,384]{2,1,0:T(8,128)(2,1)S(1)} %get-tuple-element.43), channel_id=1, source_target_pairs={{0,2},{1,3},{2,0},{3,1},{4,6},{5,7},{6,4},{7,5},{8,10},{9,11},{10,... | collective-permute-start | bytes 258056 | tf_op jit(solution)/shard_map/ppermute | solution.py:529
  20.2 8.3 %collective-permute-done.7.refs_6_ = bf16[7,16,384]{2,1,0:T(8,128)(2,1)S(1)} collective-permute-done((bf16[7,16,384]{2,1,0:T(8,128)(2,1)S(1)}, bf16[7,16,384]{2,1,0:T(8,128)(2,1)S(1)}, u32[]{:S(2)}, u32[]{:S(2)}) %collective-permute-start.7) | collective-permute-done | bytes 86048 | tf_op jit(solution)/shard_map/ppermute | solution.py:529
  29.2 3.9 %shard_map.124 = (bf16[7,32,384]{2,1,0:T(8,128)(2,1)S(1)}, bf16[7,32,384]{2,1,0:T(8,128)(2,1)S(1)}, bf16[7,32,384]{2,1,0:T(8,128)(2,1)S(1)}, bf16[7,32,384]{2,1,0:T(8,128)(2,1)S(1)}) custom-call(s32[1]{0:T(128)S(6)} %copy.21.count_ref, bf16[192,576]{1,0:T(8,128)(2,1)S(1)} %copy-done.4, bf16[192,192]{1,0:T(8,128)(2,1)S(1)} %copy-done.7, ...), custom_call_target="tpu_custom_call" | custom-call | flops 100000000 | bytes 1000000 | tf_op jit(solution)/shard_map/pallas_call | solution.py:340
  33.6 1.8 %collective-permute-start.4 = (bf16[7,16,384]{2,1,0:T(8,128)(2,1)S(1)}, bf16[7,16,384]{2,1,0:T(8,128)(2,1)S(1)}, u32[]{:S(2)}, u32[]{:S(2)}) collective-permute-start(bf16[7,16,384]{2,1,0:T(8,128)(2,1)S(1)} %get-tuple-element.38), channel_id=1, source_target_pairs={{0,2},{1,3},{2,0},{3,1},{4,6},{5,7},{6,4},{7,5},{8,10},{9,11},{10,... | collective-permute-start | bytes 258056 | tf_op jit(solution)/shard_map/ppermute | solution.py:529
  35.4 3.2 %collective-permute-done.4.refs_6_ = bf16[7,16,384]{2,1,0:T(8,128)(2,1)S(1)} collective-permute-done((bf16[7,16,384]{2,1,0:T(8,128)(2,1)S(1)}, bf16[7,16,384]{2,1,0:T(8,128)(2,1)S(1)}, u32[]{:S(2)}, u32[]{:S(2)}) %collective-permute-start.4) | collective-permute-done | bytes 86048 | tf_op jit(solution)/shard_map/ppermute | solution.py:529
  38.7 1.5 %collective-permute-done.5.refs_7_ = bf16[7,16,384]{2,1,0:T(8,128)(2,1)S(1)} collective-permute-done((bf16[7,16,384]{2,1,0:T(8,128)(2,1)S(1)}, bf16[7,16,384]{2,1,0:T(8,128)(2,1)S(1)}, u32[]{:S(2)}, u32[]{:S(2)}) %collective-permute-start.5) | collective-permute-done | bytes 86048 | tf_op jit(solution)/shard_map/ppermute | solution.py:529
  40.2 4.0 %shard_map.123 = (bf16[7,32,384]{2,1,0:T(8,128)(2,1)S(1)}, bf16[7,32,384]{2,1,0:T(8,128)(2,1)S(1)}, bf16[7,32,384]{2,1,0:T(8,128)(2,1)S(1)}, bf16[7,32,384]{2,1,0:T(8,128)(2,1)S(1)}) custom-call(s32[1]{0:T(128)S(6)} %copy.21.count_ref, bf16[192,576]{1,0:T(8,128)(2,1)S(1)} %copy-done.4, bf16[192,192]{1,0:T(8,128)(2,1)S(1)} %copy-done.7, ...), custom_call_target="tpu_custom_call" | custom-call | flops 100000000 | bytes 1000000 | tf_op jit(solution)/shard_map/pallas_call | solution.py:340
  44.4 1.7 %collective-permute-start.11 = (bf16[7,32,384]{2,1,0:T(8,128)(2,1)S(1)}, bf16[7,32,384]{2,1,0:T(8,128)(2,1)S(1)}, u32[]{:S(2)}, u32[]{:S(2)}) collective-permute-start(bf16[7,32,384]{2,1,0:T(8,128)(2,1)S(1)} %get-tuple-element.49), channel_id=1, source_target_pairs={{0,2},{1,3},{2,0},{3,1},{4,6},{5,7},{6,4},{7,5},{8,10},{9,11},{10,... | collective-permute-start | bytes 516104 | tf_op jit(solution)/shard_map/ppermute | solution.py:529
  46.2 1.4 %collective-permute-start.13 = (bf16[7,32,384]{2,1,0:T(8,128)(2,1)S(1)}, bf16[7,32,384]{2,1,0:T(8,128)(2,1)S(1)}, u32[]{:S(2)}, u32[]{:S(2)}) collective-permute-start(bf16[7,32,384]{2,1,0:T(8,128)(2,1)S(1)} %get-tuple-element.54), channel_id=1, source_target_pairs={{0,2},{1,3},{2,0},{3,1},{4,6},{5,7},{6,4},{7,5},{8,10},{9,11},{10,... | collective-permute-start | bytes 516104 | tf_op jit(solution)/shard_map/ppermute | solution.py:529
  47.9 1.0 %swap_cotangent.1.refs_6_.refs_4_ = bf16[112,32,192]{2,1,0:T(8,128)(2,1)S(1)} custom-call(bf16[32,192,112]{2,1,0:T(8,128)(2,1)S(1)} %bitcast.17), custom_call_target="tpu_custom_call" | custom-call | flops 100000000 | bytes 1000000 | tf_op jit(solution)/shard_map/swap_cotangent/pallas_call | solution.py:372
  49.0 7.0 %shard_map.125 = (bf16[4,448,192]{2,1,0:T(8,128)(2,1)S(1)}, f32[192,768]{1,0:T(8,128)S(1)}, f32[192,768]{1,0:T(8,128)S(1)}) custom-call(bf16[7,32,384]{2,1,0:T(8,128)(2,1)S(1)} %get-tuple-element.40.refs_0_, bf16[7,32,384]{2,1,0:T(8,128)(2,1)S(1)} %get-tuple-element.45.refs_1_, bf16[7,32,384]{2,1,0:T(8,128)(2,1)S(1)} %collective-permute-done.9.refs_2_, ...), custom_call_target="tpu_custom_call" | custom-call | flops 100000000 | bytes 1000000 | tf_op jit(solution)/shard_map/pallas_call | solution.py:498
  56.0 3.4 %shard_map.126 = (bf16[2,448,192]{2,1,0:T(8,128)(2,1)S(1)}, f32[192,768]{1,0:T(8,128)S(1)}, f32[192,768]{1,0:T(8,128)S(1)}) custom-call(bf16[7,32,384]{2,1,0:T(8,128)(2,1)S(1)} %collective-permute-done.11.refs_0_, bf16[7,32,384]{2,1,0:T(8,128)(2,1)S(1)} %collective-permute-done.12.refs_1_, ...), custom_call_target="tpu_custom_call", output_to_operand_aliasing={{1}: (5, {}), {2}: (6, {})} | custom-call | flops 100000000 | bytes 1000000 | tf_op jit(solution)/shard_map/pallas_call | solution.py:498
  59.4 2.2 %collective-permute-done.14.refs_1_ = bf16[7,32,384]{2,1,0:T(8,128)(2,1)S(1)} collective-permute-done((bf16[7,32,384]{2,1,0:T(8,128)(2,1)S(1)}, bf16[7,32,384]{2,1,0:T(8,128)(2,1)S(1)}, u32[]{:S(2)}, u32[]{:S(2)}) %collective-permute-start.14) | collective-permute-done | bytes 172064 | tf_op jit(solution)/shard_map/ppermute | solution.py:529
  61.6 3.8 %shard_map.127 = (bf16[2,448,192]{2,1,0:T(8,128)(2,1)S(1)}, f32[192,768]{1,0:T(8,128)S(1)}, f32[192,768]{1,0:T(8,128)S(1)}, bf16[16,24,384]{2,1,0:T(8,128)(2,1)S(1)}, bf16[16,24,384]{2,1,0:T(8,128)(2,1)S(1)}) custom-call(bf16[7,32,384]{2,1,0:T(8,128)(2,1)S(1)} %collective-permute-done.13.refs_0_, ...), custom_call_target="tpu_custom_call", output_to_operand_aliasing={{1}: (5, {}), {2}: (6, {})} | custom-call | flops 100000000 | bytes 1000000 | tf_op jit(solution)/shard_map/pallas_call | solution.py:498
  65.8 1.2 %collective-permute-done.15.b_ref = bf16[16,24,384]{2,1,0:T(8,128)(2,1)S(1)} collective-permute-done((bf16[16,24,384]{2,1,0:T(8,128)(2,1)S(1)}, bf16[16,24,384]{2,1,0:T(8,128)(2,1)S(1)}, u32[]{:S(2)}, u32[]{:S(2)}) %collective-permute-start.15) | collective-permute-done | bytes 294944 | tf_op jit(solution)/shard_map/ppermute | solution.py:576
  67.8 6.8 %all-to-all-start = ((bf16[16,24,384]{2,1,0:T(8,128)(2,1)}), bf16[16,24,384]{2,1,0:T(8,128)(2,1)S(1)}, u32[]{:S(2)}, u32[]{:S(2)}) async-start(bf16[16,24,384]{2,1,0:T(8,128)(2,1)} %add_pair.1), calls=%async_computation | async-start | bytes 589824 | tf_op jit(solution)/shard_map/all_to_all | solution.py:578
  74.6 2.4 %make_output.1 = bf16[32,192,112]{2,1,0:T(8,128)(2,1)} custom-call(bf16[4,448,192]{2,1,0:T(8,128)(2,1)S(1)} %get-tuple-element.48.refs_0_, bf16[2,448,192]{2,1,0:T(8,128)(2,1)S(1)} %get-tuple-element.53.refs_1_, bf16[2,448,192]{2,1,0:T(8,128)(2,1)S(1)} %get-tuple-element.58.refs_2_), custom_call_target="tpu_custom_call" | custom-call | flops 100000000 | bytes 1000000 | tf_op jit(solution)/shard_map/make_output/pallas_call | solution.py:413
  77.0 8.8 %all-to-all-done = bf16[16,24,384]{2,1,0:T(8,128)(2,1)S(1)} async-done(((bf16[16,24,384]{2,1,0:T(8,128)(2,1)}), bf16[16,24,384]{2,1,0:T(8,128)(2,1)S(1)}, u32[]{:S(2)}, u32[]{:S(2)}) %all-to-all-start) | async-done | bytes 294944 | tf_op jit(solution)/shard_map/all_to_all | solution.py:578
  (40 shorter events, 4.9 us)
Async XLA Ops:
  1.3 1.4 %copy-start = (bf16[1,32,112,192]{2,3,1,0:T(8,128)(2,1)S(1)}, bf16[1,32,112,192]{2,3,1,0:T(8,128)(2,1)}, u32[]{:S(2)}) copy-start(bf16[1,32,112,192]{2,3,1,0:T(8,128)(2,1)} %param.10) | copy-start | bytes 4128772
  2.7 0.9 %copy-start.5 = (bf16[192,576]{1,0:T(8,128)(2,1)S(1)}, bf16[192,576]{1,0:T(8,128)(2,1)}, u32[]{:S(2)}) copy-start(bf16[192,576]{1,0:T(8,128)(2,1)} %wqkv_ref.5) | copy-start | bytes 663556
  4.5 24.6 %copy-start.4 = (bf16[192,576]{1,0:T(8,128)(2,1)S(1)}, bf16[192,576]{1,0:T(8,128)(2,1)}, u32[]{:S(2)}) copy-start(bf16[192,576]{1,0:T(8,128)(2,1)} %wqkv_ref.7) | copy-start | bytes 663556
  4.5 24.6 %copy-start.7 = (bf16[192,192]{1,0:T(8,128)(2,1)S(1)}, bf16[192,192]{1,0:T(8,128)(2,1)}, u32[]{:S(2)}) copy-start(bf16[192,192]{1,0:T(8,128)(2,1)} %wproj_ref.7) | copy-start | bytes 221188
  8.7 10.5 %collective-permute-start.6 = (bf16[7,16,384]{2,1,0:T(8,128)(2,1)S(1)}, bf16[7,16,384]{2,1,0:T(8,128)(2,1)S(1)}, u32[]{:S(2)}, u32[]{:S(2)}) collective-permute-start(bf16[7,16,384]{2,1,0:T(8,128)(2,1)S(1)} %get-tuple-element.42), channel_id=1, source_target_pairs={{0,1},{1,0},{2,3},{3,2},{4,5},{5,4},{6,7},{7,6},{8,9},{9,8},{10,11... | collective-permute-start | bytes 258056 | tf_op jit(solution)/shard_map/ppermute | solution.py:529
  14.7 33.2 %copy-start.3 = (bf16[1,32,112,192]{2,3,1,0:T(8,128)(2,1)S(1)}, bf16[1,32,112,192]{2,3,1,0:T(8,128)(2,1)}, u32[]{:S(2)}) copy-start(bf16[1,32,112,192]{2,3,1,0:T(8,128)(2,1)} %param.19) | copy-start | bytes 4128772
  14.7 14.4 %collective-permute-start = (bf16[14,16,384]{2,1,0:T(8,128)(2,1)S(1)}, bf16[14,16,384]{2,1,0:T(8,128)(2,1)S(1)}, u32[]{:S(2)}, u32[]{:S(2)}) collective-permute-start(bf16[14,16,384]{2,1,0:T(8,128)(2,1)S(1)} %get-tuple-element.33), channel_id=1, source_target_pairs={{0,1},{1,0},{2,3},{3,2},{4,5},{5,4},{6,7},{7,6},{8,9},{9,8},{10,11... | collective-permute-start | bytes 516104 | tf_op jit(solution)/shard_map/ppermute | solution.py:529
  14.8 14.4 %collective-permute-start.1 = (bf16[14,16,384]{2,1,0:T(8,128)(2,1)S(1)}, bf16[14,16,384]{2,1,0:T(8,128)(2,1)S(1)}, u32[]{:S(2)}, u32[]{:S(2)}) collective-permute-start(bf16[14,16,384]{2,1,0:T(8,128)(2,1)S(1)} %get-tuple-element.34), channel_id=1, source_target_pairs={{0,2},{1,3},{2,0},{3,1},{4,6},{5,7},{6,4},{7,5},{8,10},{9,11},{10,... | collective-permute-start | bytes 516104 | tf_op jit(solution)/shard_map/ppermute | solution.py:529
  17.8 11.4 %collective-permute-start.2 = (bf16[14,16,384]{2,1,0:T(8,128)(2,1)S(1)}, bf16[14,16,384]{2,1,0:T(8,128)(2,1)S(1)}, u32[]{:S(2)}, u32[]{:S(2)}) collective-permute-start(bf16[14,16,384]{2,1,0:T(8,128)(2,1)S(1)} %get-tuple-element.35), channel_id=1, source_target_pairs={{0,3},{1,2},{2,1},{3,0},{4,7},{5,6},{6,5},{7,4},{8,11},{9,10},{10,... | collective-permute-start | bytes 516104 | tf_op jit(solution)/shard_map/ppermute | solution.py:529
  17.8 10.7 %collective-permute-start.7 = (bf16[7,16,384]{2,1,0:T(8,128)(2,1)S(1)}, bf16[7,16,384]{2,1,0:T(8,128)(2,1)S(1)}, u32[]{:S(2)}, u32[]{:S(2)}) collective-permute-start(bf16[7,16,384]{2,1,0:T(8,128)(2,1)S(1)} %get-tuple-element.43), channel_id=1, source_target_pairs={{0,2},{1,3},{2,0},{3,1},{4,6},{5,7},{6,4},{7,5},{8,10},{9,11},{10,... | collective-permute-start | bytes 258056 | tf_op jit(solution)/shard_map/ppermute | solution.py:529
  19.2 9.9 %collective-permute-start.8 = (bf16[7,16,384]{2,1,0:T(8,128)(2,1)S(1)}, bf16[7,16,384]{2,1,0:T(8,128)(2,1)S(1)}, u32[]{:S(2)}, u32[]{:S(2)}) collective-permute-start(bf16[7,16,384]{2,1,0:T(8,128)(2,1)S(1)} %get-tuple-element.44), channel_id=1, source_target_pairs={{0,3},{1,2},{2,1},{3,0},{4,7},{5,6},{6,5},{7,4},{8,11},{9,10},{10,... | collective-permute-start | bytes 258056 | tf_op jit(solution)/shard_map/ppermute | solution.py:529
  33.1 14.5 %collective-permute-start.10 = (bf16[7,32,384]{2,1,0:T(8,128)(2,1)S(1)}, bf16[7,32,384]{2,1,0:T(8,128)(2,1)S(1)}, u32[]{:S(2)}, u32[]{:S(2)}) collective-permute-start(bf16[7,32,384]{2,1,0:T(8,128)(2,1)S(1)} %get-tuple-element.47), channel_id=1, source_target_pairs={{0,1},{1,0},{2,3},{3,2},{4,5},{5,4},{6,7},{7,6},{8,9},{9,8},{10,11... | collective-permute-start | bytes 516104 | tf_op jit(solution)/shard_map/ppermute | solution.py:529
  33.6 1.9 %collective-permute-start.3 = (bf16[7,16,384]{2,1,0:T(8,128)(2,1)S(1)}, bf16[7,16,384]{2,1,0:T(8,128)(2,1)S(1)}, u32[]{:S(2)}, u32[]{:S(2)}) collective-permute-start(bf16[7,16,384]{2,1,0:T(8,128)(2,1)S(1)} %get-tuple-element.37), channel_id=1, source_target_pairs={{0,1},{1,0},{2,3},{3,2},{4,5},{5,4},{6,7},{7,6},{8,9},{9,8},{10,11... | collective-permute-start | bytes 258056 | tf_op jit(solution)/shard_map/ppermute | solution.py:529
  33.6 5.0 %collective-permute-start.4 = (bf16[7,16,384]{2,1,0:T(8,128)(2,1)S(1)}, bf16[7,16,384]{2,1,0:T(8,128)(2,1)S(1)}, u32[]{:S(2)}, u32[]{:S(2)}) collective-permute-start(bf16[7,16,384]{2,1,0:T(8,128)(2,1)S(1)} %get-tuple-element.38), channel_id=1, source_target_pairs={{0,2},{1,3},{2,0},{3,1},{4,6},{5,7},{6,4},{7,5},{8,10},{9,11},{10,... | collective-permute-start | bytes 258056 | tf_op jit(solution)/shard_map/ppermute | solution.py:529
  35.4 4.8 %collective-permute-start.5 = (bf16[7,16,384]{2,1,0:T(8,128)(2,1)S(1)}, bf16[7,16,384]{2,1,0:T(8,128)(2,1)S(1)}, u32[]{:S(2)}, u32[]{:S(2)}) collective-permute-start(bf16[7,16,384]{2,1,0:T(8,128)(2,1)S(1)} %get-tuple-element.39), channel_id=1, source_target_pairs={{0,3},{1,2},{2,1},{3,0},{4,7},{5,6},{6,5},{7,4},{8,11},{9,10},{10,... | collective-permute-start | bytes 258056 | tf_op jit(solution)/shard_map/ppermute | solution.py:529
  44.2 4.7 %collective-permute-start.9 = (bf16[7,32,384]{2,1,0:T(8,128)(2,1)S(1)}, bf16[7,32,384]{2,1,0:T(8,128)(2,1)S(1)}, u32[]{:S(2)}, u32[]{:S(2)}) collective-permute-start(bf16[7,32,384]{2,1,0:T(8,128)(2,1)S(1)} %get-tuple-element.46), channel_id=1, source_target_pairs={{0,1},{1,0},{2,3},{3,2},{4,5},{5,4},{6,7},{7,6},{8,9},{9,8},{10,11... | collective-permute-start | bytes 516104 | tf_op jit(solution)/shard_map/ppermute | solution.py:529
  44.4 11.5 %collective-permute-start.11 = (bf16[7,32,384]{2,1,0:T(8,128)(2,1)S(1)}, bf16[7,32,384]{2,1,0:T(8,128)(2,1)S(1)}, u32[]{:S(2)}, u32[]{:S(2)}) collective-permute-start(bf16[7,32,384]{2,1,0:T(8,128)(2,1)S(1)} %get-tuple-element.49), channel_id=1, source_target_pairs={{0,2},{1,3},{2,0},{3,1},{4,6},{5,7},{6,4},{7,5},{8,10},{9,11},{10,... | collective-permute-start | bytes 516104 | tf_op jit(solution)/shard_map/ppermute | solution.py:529
  46.1 9.9 %collective-permute-start.12 = (bf16[7,32,384]{2,1,0:T(8,128)(2,1)S(1)}, bf16[7,32,384]{2,1,0:T(8,128)(2,1)S(1)}, u32[]{:S(2)}, u32[]{:S(2)}) collective-permute-start(bf16[7,32,384]{2,1,0:T(8,128)(2,1)S(1)} %get-tuple-element.50), channel_id=1, source_target_pairs={{0,3},{1,2},{2,1},{3,0},{4,7},{5,6},{6,5},{7,4},{8,11},{9,10},{10,... | collective-permute-start | bytes 516104 | tf_op jit(solution)/shard_map/ppermute | solution.py:529
  46.2 13.2 %collective-permute-start.13 = (bf16[7,32,384]{2,1,0:T(8,128)(2,1)S(1)}, bf16[7,32,384]{2,1,0:T(8,128)(2,1)S(1)}, u32[]{:S(2)}, u32[]{:S(2)}) collective-permute-start(bf16[7,32,384]{2,1,0:T(8,128)(2,1)S(1)} %get-tuple-element.54), channel_id=1, source_target_pairs={{0,2},{1,3},{2,0},{3,1},{4,6},{5,7},{6,4},{7,5},{8,10},{9,11},{10,... | collective-permute-start | bytes 516104 | tf_op jit(solution)/shard_map/ppermute | solution.py:529
  47.6 14.0 %collective-permute-start.14 = (bf16[7,32,384]{2,1,0:T(8,128)(2,1)S(1)}, bf16[7,32,384]{2,1,0:T(8,128)(2,1)S(1)}, u32[]{:S(2)}, u32[]{:S(2)}) collective-permute-start(bf16[7,32,384]{2,1,0:T(8,128)(2,1)S(1)} %get-tuple-element.55), channel_id=1, source_target_pairs={{0,3},{1,2},{2,1},{3,0},{4,7},{5,6},{6,5},{7,4},{8,11},{9,10},{10,... | collective-permute-start | bytes 516104 | tf_op jit(solution)/shard_map/ppermute | solution.py:529
  47.9 1.0 %copy-start.1 = (bf16[192,768]{1,0:T(8,128)(2,1)S(1)}, bf16[192,768]{1,0:T(8,128)(2,1)}, u32[]{:S(2)}) copy-start(bf16[192,768]{1,0:T(8,128)(2,1)} %refs_2_.3) | copy-start | bytes 884740
  47.9 1.0 %copy-start.2 = (bf16[768,192]{0,1:T(8,128)(2,1)S(1)}, bf16[768,192]{0,1:T(8,128)(2,1)}, u32[]{:S(2)}) copy-start(bf16[768,192]{0,1:T(8,128)(2,1)} %param.18) | copy-start | bytes 884740
  65.3 1.7 %collective-permute-start.15 = (bf16[16,24,384]{2,1,0:T(8,128)(2,1)S(1)}, bf16[16,24,384]{2,1,0:T(8,128)(2,1)S(1)}, u32[]{:S(2)}, u32[]{:S(2)}) collective-permute-start(bf16[16,24,384]{2,1,0:T(8,128)(2,1)S(1)} %get-tuple-element.60), channel_id=1, source_target_pairs={{0,1},{1,0},{2,3},{3,2},{4,5},{5,4},{6,7},{7,6},{8,9},{9,8},{10,11... | collective-permute-start | bytes 884744 | tf_op jit(solution)/shard_map/ppermute | solution.py:576
  67.8 18.0 %all-to-all-start = ((bf16[16,24,384]{2,1,0:T(8,128)(2,1)}), bf16[16,24,384]{2,1,0:T(8,128)(2,1)S(1)}, u32[]{:S(2)}, u32[]{:S(2)}) async-start(bf16[16,24,384]{2,1,0:T(8,128)(2,1)} %add_pair.1), calls=%async_computation | async-start | bytes 589824 | tf_op jit(solution)/shard_map/all_to_all | solution.py:578
  (1 other events, 0.9 us)

commit v3 on v2

--- a/solution.py
+++ b/solution.py
@@ -160,26 +160,30 @@
     return value if n == lanes else jnp.concatenate([value, jnp.zeros((rows, lanes - n), value.dtype)], axis=1)
 
 
-def feature_kernel(groups, per, first, rows, cuts, count_ref, cells_ref, wqkv_ref, wproj_ref, *refs):
-    outs = refs[: groups * cuts]
-    refs = refs[groups * cuts :]
-    parts = 1
-    waits = [[] for _ in range(parts)]
-    if first == 0:
-        sems, wqkv_buf, wproj_buf, cells_buf = refs[6:]
-        refs = refs[:6]
-        step = rows // parts
-        moves = [(wqkv_ref, wqkv_buf), (wproj_ref, wproj_buf)]
-        for n in range(parts):
-            moves.append((cells_ref.at[pl.ds(n * step, step)], cells_buf.at[pl.ds(n * step, step)]))
+def feature_kernel(groups, per, base, rows, cuts, lead, *refs):
+    count_ref, cells_ref, wqkv_ref, wproj_ref, *refs = refs
+    count = count_ref[0]
+    first = base
+    if lead:
+        outs = refs[: groups * cuts]
+        wqkv_buf, wproj_buf, rest_buf, *refs = refs[groups * cuts :]
+        sems, cells_buf = refs[6:]
+        moves = [(wqkv_ref, wqkv_buf), (wproj_ref, wproj_buf), (cells_ref.at[pl.ds(0, rows)], cells_buf)]
+        late = (cells_ref.at[pl.ds(rows, rest_buf.shape[0])], rest_buf)
         moves = [pltpu.make_async_copy(a, b, sems.at[n]) for n, (a, b) in enumerate(moves)]
+        late = pltpu.make_async_copy(*late, sems.at[3])
         for move in moves:
             move.start()
-        for move in moves[:2]:
+        for move in moves:
             move.wait()
-        waits = [[move] for move in moves[2:]]
         wqkv_ref, wproj_ref, cells_ref = wqkv_buf, wproj_buf, cells_buf
-    count = count_ref[0]
+    else:
+        cot_ref, *refs = refs
+        outs = refs[: groups * cuts]
+        cot_buf, *refs = refs[groups * cuts :]
+        late = pltpu.make_async_copy(cot_ref, cot_buf, refs[6].at[0])
+    late.start()
+    refs = refs[:6]
     q_ref, k_ref, v_ref, att_ref, mid_ref, swap_ref = refs
     _, width, feats = cells_ref.shape
     lanes = q_ref.shape[2]
@@ -207,11 +211,7 @@
         for at, value in zip(ats, finish_items(att_ref, ats, w_proj_t, flip, own)):
             mid_ref[at] = value
 
-    for n, moves in enumerate(waits):
-        for move in moves:
-            move.wait()
-        step = rows // parts
-        project(list(range(n * step, (n + 1) * step)))
+    loop(rows, 16, project)
     loop(rows, 8, lambda ats: attend(kept, att_ref, ats, ones))
     loop(rows, 16, finish)
     swap = swap_matrix(rows)
@@ -224,6 +224,7 @@
         for m in range(groups):
             base = (here ^ m) * fg + c * size
             outs[c * groups + m][...] = pack([swap_ref[pl.ds(base + q * half, size)] for q in range(per)])
+    late.wait()
 
 
 BLOCKS = 2
@@ -255,31 +256,35 @@
     return pl.CostEstimate(flops=flops, transcendentals=0, bytes_accessed=10**6)
 
 
-def feature_chunk(block_t, count, wqkv, wproj, groups, per, chunk, rows, cuts):
-    _, width, feats = block_t.shape
+def feature_chunk(cells_t, count, wqkv, wproj, cot_t, groups, per, base, rows, cuts):
+    whole, width, feats = cells_t.shape
     half = feats // groups // per
     lanes = -(-feats // 128) * 128
+    far = pl.BlockSpec(memory_space=pltpu.HBM)
+    lead = cot_t is None
     outs = [near((half // cuts, rows, per * width))] * (groups * cuts)
     scratch = attention_scratch(rows, width, lanes, feats)
     scratch += [pltpu.VMEM((rows, feats, width), BF), pltpu.VMEM((feats, rows, width), BF)]
-    operands = [block_t, wqkv, wproj]
-    if chunk == 0:
+    operands = [cells_t, wqkv, wproj]
+    if lead:
         operands = [pltpu.with_memory_space_constraint(x, pltpu.HBM) for x in operands]
-        specs = [pl.BlockSpec(memory_space=pltpu.HBM)] * 3
-        scratch += [pltpu.SemaphoreType.DMA((4,))]
-        scratch += [pltpu.VMEM(x.shape, BF) for x in (wqkv, wproj)]
-        scratch += [pltpu.VMEM((rows, width, feats), BF)]
+        specs = [far] * 3
+        outs += [near(wqkv.shape), near(wproj.shape), near((whole - rows, width, feats))]
+        scratch += [pltpu.SemaphoreType.DMA((4,)), pltpu.VMEM((rows, width, feats), BF)]
     else:
-        operands = bring(*operands)
-        specs = [IN_VMEM] * 3
+        operands = bring(*operands) + [pltpu.with_memory_space_constraint(cot_t, pltpu.HBM)]
+        specs = [IN_VMEM] * 3 + [far]
+        outs += [near(cot_t.shape)]
+        scratch += [pltpu.SemaphoreType.DMA((1,))]
     return pl.pallas_call(
-        functools.partial(feature_kernel, groups, per, chunk * rows, rows, cuts),
+        functools.partial(feature_kernel, groups, per, base, rows, cuts, lead),
         in_specs=[IN_SMEM] + specs,
         out_specs=[IN_VMEM] * len(outs),
         out_shape=outs,
         scratch_shapes=scratch,
         compiler_params=PARAMS,
         cost_estimate=cost(10**8),
+        name="feature_0" if lead else "feature_1",
     )(count, *operands)
 
 
@@ -546,18 +551,23 @@
     factor = 1.0 / math.sqrt(tables * local * groups * feats)
     pairs = half // feat_chunks
     pieces = [[] for _ in range(feat_chunks)]
-    firsts = []
-    for k in range(row_chunks):
-        cuts = feat_chunks if k == row_chunks - 1 else 1
-        sent = feature_chunk(block_t, feat_count, feat_qkv, feat_proj, groups, per, k, sub_rows, cuts)
-        come = [exchange(sent[c * groups : (c + 1) * groups], groups) for c in range(cuts)]
-        for j in range(feat_chunks):
-            pieces[j] += come[j % cuts]
-        firsts.append(cuts == 1)
-    cot_t = swap_cotangent(jnp.swapaxes(cotangent[0], 1, 2))
+    cot_t = jnp.swapaxes(cotangent[0], 1, 2)
+    sent = feature_chunk(
+        block_t, feat_count, feat_qkv, feat_proj, None, groups, per, 0, sub_rows, 1
+    )
+    *sent, wqkv_v, wproj_v, rest = sent
+    come = exchange(sent, groups)
+    for j in range(feat_chunks):
+        pieces[j] += come
+    *sent, cot_v = feature_chunk(
+        rest, feat_count, wqkv_v, wproj_v, cot_t, groups, per, 0, sub_rows, feat_chunks
+    )
+    for j in range(feat_chunks):
+        pieces[j] += exchange(sent[j * groups : (j + 1) * groups], groups)
+    cot_t = swap_cotangent(cot_v)
     back = []
     for j in range(feat_chunks):
-        starts = tuple(j * pairs if whole else 0 for whole in firsts)
+        starts = (j * pairs, 0)
         done = row_chunk(pieces[j], train_count, row_qkv, row_proj, groups, per, row_chunks, pairs, starts)
         back.append(exchange(done, groups))
     w_out_t = w_out.T

time: 86.9 us -> 83.6 us (0.962)
  local copies, waits for them, and re-layouts: 3.34 us -> 0.1 us
    unnamed x16 -> x8, local copies, waits for them, and re-layouts: 3.26 us -> 0.02 us
  transfers between devices with their start and end apart: 17 -> 17, of which waited for: 7 -> 7; matrix products, arithmetic and copies ran while one was open for 0% -> 0% of each run, Pallas kernels for 27% -> 21%
where the time goes in v3:
time: 83.6 us; the launch traced here: 83.3 us
  Pallas kernels  36 us (43%)
  waiting for transfers between devices  25.9 us (31%)
  starting transfers between devices  18.6 us (22%)
  between operations  2.09 us (2%)
    ppermute x15, waiting for transfers between devices, exchange(): lax.ppermute(pieces[m], CELLS, [(s, s ^ m) for s in range(groups)])  15.9 us
    pallas_call x3, Pallas kernels, dense_part(): pl.pallas_call(functools.partial(dense_kernel, groups, per, spot, prev is...  14.2 us
    ppermute x15, starting transfers between devices, exchange(): lax.ppermute(pieces[m], CELLS, [(s, s ^ m) for s in range(groups)])  11.3 us
    pallas_call x2, Pallas kernels, feature_chunk(): pl.pallas_call(functools.partial(feature_kernel, groups, per, base, rows,...  9.64 us
    all_to_all x1, waiting for transfers between devices, per_device(): lax.all_to_all(pieces, ('tables', 'chips'), split_axis=0, concat_axis=0,...  8.77 us
    pallas_call x2, Pallas kernels, row_chunk(): pl.pallas_call(functools.partial(row_kernel, groups, per, chunks, firsts)...  7.92 us
    all_to_all x1, starting transfers between devices, per_device(): lax.all_to_all(pieces, ('tables', 'chips'), split_axis=0, concat_axis=0,...  6.77 us
    pallas_call x1, Pallas kernels, make_output(): pl.pallas_call(functools.partial(output_kernel, groups, per, chunks, spot...  2.44 us
  transfers between devices with their start and end apart: 17, of which 7 were waited for; matrix products, arithmetic and copies ran while one was open for 0% of the time, Pallas kernels for 21%

profile of v3, /device:TPU:0, one launch (start us, length us, event | category | flops | bytes accessed | tf_op | source)
XLA Modules:
  0.0 83.3 jit_solution(15822937885468392194)
XLA Ops:
  1.3 5.5 %feature_0.1 = (bf16[14,16,384]{2,1,0:T(8,128)(2,1)S(1)}, bf16[14,16,384]{2,1,0:T(8,128)(2,1)S(1)}, bf16[14,16,384]{2,1,0:T(8,128)(2,1)S(1)}, bf16[14,16,384]{2,...) custom-call(s32[1]{0:T(128)S(6)} %copy.22.refs_0_, ...), custom_call_target="tpu_custom_call" | custom-call | flops 100000000 | bytes 1000000 | tf_op jit(solution)/shard_map/feature_0/pallas_call | solution.py:279
  6.8 4.2 %feature_1.1 = (bf16[7,16,384]{2,1,0:T(8,128)(2,1)S(1)}, bf16[7,16,384]{2,1,0:T(8,128)(2,1)S(1)}, bf16[7,16,384]{2,1,0:T(8,128)(2,1)S(1)}, bf16[7,16,384]{2,1,0:...) custom-call(s32[1]{0:T(128)S(6)} %copy.22.refs_0_, ...), custom_call_target="tpu_custom_call" | custom-call | flops 100000000 | bytes 1000000 | tf_op jit(solution)/shard_map/feature_1/pallas_call | solution.py:279
  11.6 2.9 %collective-permute-start.1 = (bf16[14,16,384]{2,1,0:T(8,128)(2,1)S(1)}, bf16[14,16,384]{2,1,0:T(8,128)(2,1)S(1)}, u32[]{:S(2)}, u32[]{:S(2)}) collective-permute-start(bf16[14,16,384]{2,1,0:T(8,128)(2,1)S(1)} %get-tuple-element.38), channel_id=1, source_target_pairs={{0,2},{1,3},{2,0},{3,1},{4,6},{5,7},{6,4},{7,5},{8,10},{9,11},{10,... | collective-permute-start | bytes 516104 | tf_op jit(solution)/shard_map/ppermute | solution.py:534
  14.5 1.4 %collective-permute-start.7 = (bf16[7,16,384]{2,1,0:T(8,128)(2,1)S(1)}, bf16[7,16,384]{2,1,0:T(8,128)(2,1)S(1)}, u32[]{:S(2)}, u32[]{:S(2)}) collective-permute-start(bf16[7,16,384]{2,1,0:T(8,128)(2,1)S(1)} %get-tuple-element.50), channel_id=1, source_target_pairs={{0,2},{1,3},{2,0},{3,1},{4,6},{5,7},{6,4},{7,5},{8,10},{9,11},{10,... | collective-permute-start | bytes 258056 | tf_op jit(solution)/shard_map/ppermute | solution.py:534
  16.9 8.3 %collective-permute-done.7.refs_6_ = bf16[7,16,384]{2,1,0:T(8,128)(2,1)S(1)} collective-permute-done((bf16[7,16,384]{2,1,0:T(8,128)(2,1)S(1)}, bf16[7,16,384]{2,1,0:T(8,128)(2,1)S(1)}, u32[]{:S(2)}, u32[]{:S(2)}) %collective-permute-start.7) | collective-permute-done | bytes 86048 | tf_op jit(solution)/shard_map/ppermute | solution.py:534
  25.2 0.6 collective-permute-done.8.refs_7_
  25.9 3.9 %shard_map.122 = (bf16[7,32,384]{2,1,0:T(8,128)(2,1)S(1)}, bf16[7,32,384]{2,1,0:T(8,128)(2,1)S(1)}, bf16[7,32,384]{2,1,0:T(8,128)(2,1)S(1)}, bf16[7,32,384]{2,1,0:T(8,128)(2,1)S(1)}) custom-call(s32[1]{0:T(128)S(6)} %copy.21.count_ref, bf16[192,576]{1,0:T(8,128)(2,1)S(1)} %copy-done.2, bf16[192,192]{1,0:T(8,128)(2,1)S(1)} %copy-done.3, ...), custom_call_target="tpu_custom_call" | custom-call | flops 100000000 | bytes 1000000 | tf_op jit(solution)/shard_map/pallas_call | solution.py:345
  30.4 1.8 %collective-permute-start.4 = (bf16[7,16,384]{2,1,0:T(8,128)(2,1)S(1)}, bf16[7,16,384]{2,1,0:T(8,128)(2,1)S(1)}, u32[]{:S(2)}, u32[]{:S(2)}) collective-permute-start(bf16[7,16,384]{2,1,0:T(8,128)(2,1)S(1)} %get-tuple-element.45), channel_id=1, source_target_pairs={{0,2},{1,3},{2,0},{3,1},{4,6},{5,7},{6,4},{7,5},{8,10},{9,11},{10,... | collective-permute-start | bytes 258056 | tf_op jit(solution)/shard_map/ppermute | solution.py:534
  32.2 3.2 %collective-permute-done.4.refs_6_ = bf16[7,16,384]{2,1,0:T(8,128)(2,1)S(1)} collective-permute-done((bf16[7,16,384]{2,1,0:T(8,128)(2,1)S(1)}, bf16[7,16,384]{2,1,0:T(8,128)(2,1)S(1)}, u32[]{:S(2)}, u32[]{:S(2)}) %collective-permute-start.4) | collective-permute-done | bytes 86048 | tf_op jit(solution)/shard_map/ppermute | solution.py:534
  35.4 1.5 %collective-permute-done.5.refs_7_ = bf16[7,16,384]{2,1,0:T(8,128)(2,1)S(1)} collective-permute-done((bf16[7,16,384]{2,1,0:T(8,128)(2,1)S(1)}, bf16[7,16,384]{2,1,0:T(8,128)(2,1)S(1)}, u32[]{:S(2)}, u32[]{:S(2)}) %collective-permute-start.5) | collective-permute-done | bytes 86048 | tf_op jit(solution)/shard_map/ppermute | solution.py:534
  36.9 4.0 %shard_map.121 = (bf16[7,32,384]{2,1,0:T(8,128)(2,1)S(1)}, bf16[7,32,384]{2,1,0:T(8,128)(2,1)S(1)}, bf16[7,32,384]{2,1,0:T(8,128)(2,1)S(1)}, bf16[7,32,384]{2,1,0:T(8,128)(2,1)S(1)}) custom-call(s32[1]{0:T(128)S(6)} %copy.21.count_ref, bf16[192,576]{1,0:T(8,128)(2,1)S(1)} %copy-done.2, bf16[192,192]{1,0:T(8,128)(2,1)S(1)} %copy-done.3, ...), custom_call_target="tpu_custom_call" | custom-call | flops 100000000 | bytes 1000000 | tf_op jit(solution)/shard_map/pallas_call | solution.py:345
  41.1 1.7 %collective-permute-start.11 = (bf16[7,32,384]{2,1,0:T(8,128)(2,1)S(1)}, bf16[7,32,384]{2,1,0:T(8,128)(2,1)S(1)}, u32[]{:S(2)}, u32[]{:S(2)}) collective-permute-start(bf16[7,32,384]{2,1,0:T(8,128)(2,1)S(1)} %get-tuple-element.57), channel_id=1, source_target_pairs={{0,2},{1,3},{2,0},{3,1},{4,6},{5,7},{6,4},{7,5},{8,10},{9,11},{10,... | collective-permute-start | bytes 516104 | tf_op jit(solution)/shard_map/ppermute | solution.py:534
  42.9 1.4 %collective-permute-start.13 = (bf16[7,32,384]{2,1,0:T(8,128)(2,1)S(1)}, bf16[7,32,384]{2,1,0:T(8,128)(2,1)S(1)}, u32[]{:S(2)}, u32[]{:S(2)}) collective-permute-start(bf16[7,32,384]{2,1,0:T(8,128)(2,1)S(1)} %get-tuple-element.62), channel_id=1, source_target_pairs={{0,2},{1,3},{2,0},{3,1},{4,6},{5,7},{6,4},{7,5},{8,10},{9,11},{10,... | collective-permute-start | bytes 516104 | tf_op jit(solution)/shard_map/ppermute | solution.py:534
  44.6 1.0 %swap_cotangent.1.refs_6_.refs_4_ = bf16[112,32,192]{2,1,0:T(8,128)(2,1)S(1)} custom-call(bf16[32,192,112]{2,1,0:T(8,128)(2,1)S(1)} %get-tuple-element.55.in_ref), custom_call_target="tpu_custom_call" | custom-call | flops 100000000 | bytes 1000000 | tf_op jit(solution)/shard_map/swap_cotangent/pallas_call | solution.py:377
  45.7 7.0 %shard_map.123 = (bf16[4,448,192]{2,1,0:T(8,128)(2,1)S(1)}, f32[192,768]{1,0:T(8,128)S(1)}, f32[192,768]{1,0:T(8,128)S(1)}) custom-call(bf16[7,32,384]{2,1,0:T(8,128)(2,1)S(1)} %get-tuple-element.47.refs_0_, bf16[7,32,384]{2,1,0:T(8,128)(2,1)S(1)} %get-tuple-element.52.refs_1_, bf16[7,32,384]{2,1,0:T(8,128)(2,1)S(1)} %collective-permute-done.9.refs_2_, ...), custom_call_target="tpu_custom_call" | custom-call | flops 100000000 | bytes 1000000 | tf_op jit(solution)/shard_map/pallas_call | solution.py:503
  52.7 3.4 %shard_map.124 = (bf16[2,448,192]{2,1,0:T(8,128)(2,1)S(1)}, f32[192,768]{1,0:T(8,128)S(1)}, f32[192,768]{1,0:T(8,128)S(1)}) custom-call(bf16[7,32,384]{2,1,0:T(8,128)(2,1)S(1)} %collective-permute-done.11.refs_0_, bf16[7,32,384]{2,1,0:T(8,128)(2,1)S(1)} %collective-permute-done.12.refs_1_, ...), custom_call_target="tpu_custom_call", output_to_operand_aliasing={{1}: (5, {}), {2}: (6, {})} | custom-call | flops 100000000 | bytes 1000000 | tf_op jit(solution)/shard_map/pallas_call | solution.py:503
  56.1 2.2 %collective-permute-done.14.refs_1_ = bf16[7,32,384]{2,1,0:T(8,128)(2,1)S(1)} collective-permute-done((bf16[7,32,384]{2,1,0:T(8,128)(2,1)S(1)}, bf16[7,32,384]{2,1,0:T(8,128)(2,1)S(1)}, u32[]{:S(2)}, u32[]{:S(2)}) %collective-permute-start.14) | collective-permute-done | bytes 172064 | tf_op jit(solution)/shard_map/ppermute | solution.py:534
  58.3 3.8 %shard_map.125 = (bf16[2,448,192]{2,1,0:T(8,128)(2,1)S(1)}, f32[192,768]{1,0:T(8,128)S(1)}, f32[192,768]{1,0:T(8,128)S(1)}, bf16[16,24,384]{2,1,0:T(8,128)(2,1)S(1)}, bf16[16,24,384]{2,1,0:T(8,128)(2,1)S(1)}) custom-call(bf16[7,32,384]{2,1,0:T(8,128)(2,1)S(1)} %collective-permute-done.13.refs_0_, ...), custom_call_target="tpu_custom_call", output_to_operand_aliasing={{1}: (5, {}), {2}: (6, {})} | custom-call | flops 100000000 | bytes 1000000 | tf_op jit(solution)/shard_map/pallas_call | solution.py:503
  62.5 1.2 %collective-permute-done.15.b_ref = bf16[16,24,384]{2,1,0:T(8,128)(2,1)S(1)} collective-permute-done((bf16[16,24,384]{2,1,0:T(8,128)(2,1)S(1)}, bf16[16,24,384]{2,1,0:T(8,128)(2,1)S(1)}, u32[]{:S(2)}, u32[]{:S(2)}) %collective-permute-start.15) | collective-permute-done | bytes 294944 | tf_op jit(solution)/shard_map/ppermute | solution.py:586
  63.8 0.8 add_pair.1
  64.5 6.8 %all-to-all-start = ((bf16[16,24,384]{2,1,0:T(8,128)(2,1)}), bf16[16,24,384]{2,1,0:T(8,128)(2,1)S(1)}, u32[]{:S(2)}, u32[]{:S(2)}) async-start(bf16[16,24,384]{2,1,0:T(8,128)(2,1)} %add_pair.1), calls=%async_computation | async-start | bytes 589824 | tf_op jit(solution)/shard_map/all_to_all | solution.py:588
  71.3 2.4 %make_output.1 = bf16[32,192,112]{2,1,0:T(8,128)(2,1)} custom-call(bf16[4,448,192]{2,1,0:T(8,128)(2,1)S(1)} %get-tuple-element.56.refs_0_, bf16[2,448,192]{2,1,0:T(8,128)(2,1)S(1)} %get-tuple-element.61.refs_1_, bf16[2,448,192]{2,1,0:T(8,128)(2,1)S(1)} %get-tuple-element.66.refs_2_), custom_call_target="tpu_custom_call" | custom-call | flops 100000000 | bytes 1000000 | tf_op jit(solution)/shard_map/make_output/pallas_call | solution.py:418
  73.8 8.8 %all-to-all-done = bf16[16,24,384]{2,1,0:T(8,128)(2,1)S(1)} async-done(((bf16[16,24,384]{2,1,0:T(8,128)(2,1)}), bf16[16,24,384]{2,1,0:T(8,128)(2,1)S(1)}, u32[]{:S(2)}, u32[]{:S(2)}) %all-to-all-start) | async-done | bytes 294944 | tf_op jit(solution)/shard_map/all_to_all | solution.py:588
  82.7 0.6 maximum_bitcast_fusion
  (32 shorter events, 2.8 us)
Async XLA Ops:
  6.8 19.1 %copy-start.2 = (bf16[192,576]{1,0:T(8,128)(2,1)S(1)}, bf16[192,576]{1,0:T(8,128)(2,1)}, u32[]{:S(2)}) copy-start(bf16[192,576]{1,0:T(8,128)(2,1)} %wqkv_ref.3) | copy-start | bytes 663556
  6.8 19.1 %copy-start.3 = (bf16[192,192]{1,0:T(8,128)(2,1)S(1)}, bf16[192,192]{1,0:T(8,128)(2,1)}, u32[]{:S(2)}) copy-start(bf16[192,192]{1,0:T(8,128)(2,1)} %wproj_ref.3) | copy-start | bytes 221188
  11.0 5.0 %collective-permute-start.6 = (bf16[7,16,384]{2,1,0:T(8,128)(2,1)S(1)}, bf16[7,16,384]{2,1,0:T(8,128)(2,1)S(1)}, u32[]{:S(2)}, u32[]{:S(2)}) collective-permute-start(bf16[7,16,384]{2,1,0:T(8,128)(2,1)S(1)} %get-tuple-element.49), channel_id=1, source_target_pairs={{0,1},{1,0},{2,3},{3,2},{4,5},{5,4},{6,7},{7,6},{8,9},{9,8},{10,11... | collective-permute-start | bytes 258056 | tf_op jit(solution)/shard_map/ppermute | solution.py:534
  11.5 14.4 %collective-permute-start = (bf16[14,16,384]{2,1,0:T(8,128)(2,1)S(1)}, bf16[14,16,384]{2,1,0:T(8,128)(2,1)S(1)}, u32[]{:S(2)}, u32[]{:S(2)}) collective-permute-start(bf16[14,16,384]{2,1,0:T(8,128)(2,1)S(1)} %get-tuple-element.37), channel_id=1, source_target_pairs={{0,1},{1,0},{2,3},{3,2},{4,5},{5,4},{6,7},{7,6},{8,9},{9,8},{10,11... | collective-permute-start | bytes 516104 | tf_op jit(solution)/shard_map/ppermute | solution.py:534
  11.6 14.3 %collective-permute-start.1 = (bf16[14,16,384]{2,1,0:T(8,128)(2,1)S(1)}, bf16[14,16,384]{2,1,0:T(8,128)(2,1)S(1)}, u32[]{:S(2)}, u32[]{:S(2)}) collective-permute-start(bf16[14,16,384]{2,1,0:T(8,128)(2,1)S(1)} %get-tuple-element.38), channel_id=1, source_target_pairs={{0,2},{1,3},{2,0},{3,1},{4,6},{5,7},{6,4},{7,5},{8,10},{9,11},{10,... | collective-permute-start | bytes 516104 | tf_op jit(solution)/shard_map/ppermute | solution.py:534
  14.5 11.4 %collective-permute-start.2 = (bf16[14,16,384]{2,1,0:T(8,128)(2,1)S(1)}, bf16[14,16,384]{2,1,0:T(8,128)(2,1)S(1)}, u32[]{:S(2)}, u32[]{:S(2)}) collective-permute-start(bf16[14,16,384]{2,1,0:T(8,128)(2,1)S(1)} %get-tuple-element.39), channel_id=1, source_target_pairs={{0,3},{1,2},{2,1},{3,0},{4,7},{5,6},{6,5},{7,4},{8,11},{9,10},{10,... | collective-permute-start | bytes 516104 | tf_op jit(solution)/shard_map/ppermute | solution.py:534
  14.5 10.8 %collective-permute-start.7 = (bf16[7,16,384]{2,1,0:T(8,128)(2,1)S(1)}, bf16[7,16,384]{2,1,0:T(8,128)(2,1)S(1)}, u32[]{:S(2)}, u32[]{:S(2)}) collective-permute-start(bf16[7,16,384]{2,1,0:T(8,128)(2,1)S(1)} %get-tuple-element.50), channel_id=1, source_target_pairs={{0,2},{1,3},{2,0},{3,1},{4,6},{5,7},{6,4},{7,5},{8,10},{9,11},{10,... | collective-permute-start | bytes 258056 | tf_op jit(solution)/shard_map/ppermute | solution.py:534
  15.9 9.9 %collective-permute-start.8 = (bf16[7,16,384]{2,1,0:T(8,128)(2,1)S(1)}, bf16[7,16,384]{2,1,0:T(8,128)(2,1)S(1)}, u32[]{:S(2)}, u32[]{:S(2)}) collective-permute-start(bf16[7,16,384]{2,1,0:T(8,128)(2,1)S(1)} %get-tuple-element.51), channel_id=1, source_target_pairs={{0,3},{1,2},{2,1},{3,0},{4,7},{5,6},{6,5},{7,4},{8,11},{9,10},{10,... | collective-permute-start | bytes 258056 | tf_op jit(solution)/shard_map/ppermute | solution.py:534
  29.8 14.5 %collective-permute-start.10 = (bf16[7,32,384]{2,1,0:T(8,128)(2,1)S(1)}, bf16[7,32,384]{2,1,0:T(8,128)(2,1)S(1)}, u32[]{:S(2)}, u32[]{:S(2)}) collective-permute-start(bf16[7,32,384]{2,1,0:T(8,128)(2,1)S(1)} %get-tuple-element.54), channel_id=1, source_target_pairs={{0,1},{1,0},{2,3},{3,2},{4,5},{5,4},{6,7},{7,6},{8,9},{9,8},{10,11... | collective-permute-start | bytes 516104 | tf_op jit(solution)/shard_map/ppermute | solution.py:534
  30.3 1.9 %collective-permute-start.3 = (bf16[7,16,384]{2,1,0:T(8,128)(2,1)S(1)}, bf16[7,16,384]{2,1,0:T(8,128)(2,1)S(1)}, u32[]{:S(2)}, u32[]{:S(2)}) collective-permute-start(bf16[7,16,384]{2,1,0:T(8,128)(2,1)S(1)} %get-tuple-element.44), channel_id=1, source_target_pairs={{0,1},{1,0},{2,3},{3,2},{4,5},{5,4},{6,7},{7,6},{8,9},{9,8},{10,11... | collective-permute-start | bytes 258056 | tf_op jit(solution)/shard_map/ppermute | solution.py:534
  30.4 5.0 %collective-permute-start.4 = (bf16[7,16,384]{2,1,0:T(8,128)(2,1)S(1)}, bf16[7,16,384]{2,1,0:T(8,128)(2,1)S(1)}, u32[]{:S(2)}, u32[]{:S(2)}) collective-permute-start(bf16[7,16,384]{2,1,0:T(8,128)(2,1)S(1)} %get-tuple-element.45), channel_id=1, source_target_pairs={{0,2},{1,3},{2,0},{3,1},{4,6},{5,7},{6,4},{7,5},{8,10},{9,11},{10,... | collective-permute-start | bytes 258056 | tf_op jit(solution)/shard_map/ppermute | solution.py:534
  32.1 4.8 %collective-permute-start.5 = (bf16[7,16,384]{2,1,0:T(8,128)(2,1)S(1)}, bf16[7,16,384]{2,1,0:T(8,128)(2,1)S(1)}, u32[]{:S(2)}, u32[]{:S(2)}) collective-permute-start(bf16[7,16,384]{2,1,0:T(8,128)(2,1)S(1)} %get-tuple-element.46), channel_id=1, source_target_pairs={{0,3},{1,2},{2,1},{3,0},{4,7},{5,6},{6,5},{7,4},{8,11},{9,10},{10,... | collective-permute-start | bytes 258056 | tf_op jit(solution)/shard_map/ppermute | solution.py:534
  41.0 4.7 %collective-permute-start.9 = (bf16[7,32,384]{2,1,0:T(8,128)(2,1)S(1)}, bf16[7,32,384]{2,1,0:T(8,128)(2,1)S(1)}, u32[]{:S(2)}, u32[]{:S(2)}) collective-permute-start(bf16[7,32,384]{2,1,0:T(8,128)(2,1)S(1)} %get-tuple-element.53), channel_id=1, source_target_pairs={{0,1},{1,0},{2,3},{3,2},{4,5},{5,4},{6,7},{7,6},{8,9},{9,8},{10,11... | collective-permute-start | bytes 516104 | tf_op jit(solution)/shard_map/ppermute | solution.py:534
  41.1 11.5 %collective-permute-start.11 = (bf16[7,32,384]{2,1,0:T(8,128)(2,1)S(1)}, bf16[7,32,384]{2,1,0:T(8,128)(2,1)S(1)}, u32[]{:S(2)}, u32[]{:S(2)}) collective-permute-start(bf16[7,32,384]{2,1,0:T(8,128)(2,1)S(1)} %get-tuple-element.57), channel_id=1, source_target_pairs={{0,2},{1,3},{2,0},{3,1},{4,6},{5,7},{6,4},{7,5},{8,10},{9,11},{10,... | collective-permute-start | bytes 516104 | tf_op jit(solution)/shard_map/ppermute | solution.py:534
  42.8 9.9 %collective-permute-start.12 = (bf16[7,32,384]{2,1,0:T(8,128)(2,1)S(1)}, bf16[7,32,384]{2,1,0:T(8,128)(2,1)S(1)}, u32[]{:S(2)}, u32[]{:S(2)}) collective-permute-start(bf16[7,32,384]{2,1,0:T(8,128)(2,1)S(1)} %get-tuple-element.58), channel_id=1, source_target_pairs={{0,3},{1,2},{2,1},{3,0},{4,7},{5,6},{6,5},{7,4},{8,11},{9,10},{10,... | collective-permute-start | bytes 516104 | tf_op jit(solution)/shard_map/ppermute | solution.py:534
  42.9 13.2 %collective-permute-start.13 = (bf16[7,32,384]{2,1,0:T(8,128)(2,1)S(1)}, bf16[7,32,384]{2,1,0:T(8,128)(2,1)S(1)}, u32[]{:S(2)}, u32[]{:S(2)}) collective-permute-start(bf16[7,32,384]{2,1,0:T(8,128)(2,1)S(1)} %get-tuple-element.62), channel_id=1, source_target_pairs={{0,2},{1,3},{2,0},{3,1},{4,6},{5,7},{6,4},{7,5},{8,10},{9,11},{10,... | collective-permute-start | bytes 516104 | tf_op jit(solution)/shard_map/ppermute | solution.py:534
  44.3 14.0 %collective-permute-start.14 = (bf16[7,32,384]{2,1,0:T(8,128)(2,1)S(1)}, bf16[7,32,384]{2,1,0:T(8,128)(2,1)S(1)}, u32[]{:S(2)}, u32[]{:S(2)}) collective-permute-start(bf16[7,32,384]{2,1,0:T(8,128)(2,1)S(1)} %get-tuple-element.63), channel_id=1, source_target_pairs={{0,3},{1,2},{2,1},{3,0},{4,7},{5,6},{6,5},{7,4},{8,11},{9,10},{10,... | collective-permute-start | bytes 516104 | tf_op jit(solution)/shard_map/ppermute | solution.py:534
  44.6 1.0 %copy-start = (bf16[192,768]{1,0:T(8,128)(2,1)S(1)}, bf16[192,768]{1,0:T(8,128)(2,1)}, u32[]{:S(2)}) copy-start(bf16[192,768]{1,0:T(8,128)(2,1)} %refs_2_.5) | copy-start | bytes 884740
  44.6 1.0 %copy-start.1 = (bf16[768,192]{0,1:T(8,128)(2,1)S(1)}, bf16[768,192]{0,1:T(8,128)(2,1)}, u32[]{:S(2)}) copy-start(bf16[768,192]{0,1:T(8,128)(2,1)} %param.18) | copy-start | bytes 884740
  62.1 1.7 %collective-permute-start.15 = (bf16[16,24,384]{2,1,0:T(8,128)(2,1)S(1)}, bf16[16,24,384]{2,1,0:T(8,128)(2,1)S(1)}, u32[]{:S(2)}, u32[]{:S(2)}) collective-permute-start(bf16[16,24,384]{2,1,0:T(8,128)(2,1)S(1)} %get-tuple-element.68), channel_id=1, source_target_pairs={{0,1},{1,0},{2,3},{3,2},{4,5},{5,4},{6,7},{7,6},{8,9},{9,8},{10,11... | collective-permute-start | bytes 884744 | tf_op jit(solution)/shard_map/ppermute | solution.py:586
  64.5 18.0 %all-to-all-start = ((bf16[16,24,384]{2,1,0:T(8,128)(2,1)}), bf16[16,24,384]{2,1,0:T(8,128)(2,1)S(1)}, u32[]{:S(2)}, u32[]{:S(2)}) async-start(bf16[16,24,384]{2,1,0:T(8,128)(2,1)} %add_pair.1), calls=%async_computation | async-start | bytes 589824 | tf_op jit(solution)/shard_map/all_to_all | solution.py:588

commit v4 on v3

--- a/solution.py
+++ b/solution.py
@@ -165,8 +165,8 @@
     count = count_ref[0]
     first = base
     if lead:
-        outs = refs[: groups * cuts]
-        wqkv_buf, wproj_buf, rest_buf, *refs = refs[groups * cuts :]
+        outs = refs[: groups * len(cuts)]
+        wqkv_buf, wproj_buf, rest_buf, *refs = refs[groups * len(cuts) :]
         sems, cells_buf = refs[6:]
         moves = [(wqkv_ref, wqkv_buf), (wproj_ref, wproj_buf), (cells_ref.at[pl.ds(0, rows)], cells_buf)]
         late = (cells_ref.at[pl.ds(rows, rest_buf.shape[0])], rest_buf)
@@ -179,8 +179,8 @@
         wqkv_ref, wproj_ref, cells_ref = wqkv_buf, wproj_buf, cells_buf
     else:
         cot_ref, *refs = refs
-        outs = refs[: groups * cuts]
-        cot_buf, *refs = refs[groups * cuts :]
+        outs = refs[: groups * len(cuts)]
+        cot_buf, *refs = refs[groups * len(cuts) :]
         late = pltpu.make_async_copy(cot_ref, cot_buf, refs[6].at[0])
     late.start()
     refs = refs[:6]
@@ -219,10 +219,9 @@
         block = mid_ref[:, f * rows : (f + 1) * rows, :].reshape(rows * rows, width)
         swap_ref[f * rows : (f + 1) * rows] = dot(swap, block).astype(BF).reshape(rows, rows, width)
     here = cell_index()
-    size = half // cuts
-    for c in range(cuts):
+    for c, size in enumerate(cuts):
         for m in range(groups):
-            base = (here ^ m) * fg + c * size
+            base = (here ^ m) * fg + sum(cuts[:c])
             outs[c * groups + m][...] = pack([swap_ref[pl.ds(base + q * half, size)] for q in range(per)])
     late.wait()
 
@@ -258,11 +257,10 @@
 
 def feature_chunk(cells_t, count, wqkv, wproj, cot_t, groups, per, base, rows, cuts):
     whole, width, feats = cells_t.shape
-    half = feats // groups // per
     lanes = -(-feats // 128) * 128
     far = pl.BlockSpec(memory_space=pltpu.HBM)
     lead = cot_t is None
-    outs = [near((half // cuts, rows, per * width))] * (groups * cuts)
+    outs = [near((size, rows, per * width)) for size in cuts for _ in range(groups)]
     scratch = attention_scratch(rows, width, lanes, feats)
     scratch += [pltpu.VMEM((rows, feats, width), BF), pltpu.VMEM((feats, rows, width), BF)]
     operands = [cells_t, wqkv, wproj]
@@ -328,9 +326,9 @@
             y_ref[p] = pack(done[a * per : (a + 1) * per])
 
     most = max(1, 1024 // rows)
-    loop(items, min(2 * most, 14), project)
-    loop(items, min(most, 7), lambda ats: attend(kept, att_ref, ats, ones))
-    loop(pairs, min(most, 7), finish)
+    loop(items, min(2 * most, 16), project)
+    loop(items, min(most, 8), lambda ats: attend(kept, att_ref, ats, ones))
+    loop(pairs, min(most, 8), finish)
     for m in range(groups):
         at = pl.multiple_of((here ^ m) * local, local)
         outs[m][...] = y_ref[:, pl.ds(at, local), :]
@@ -386,17 +384,16 @@
     )(*bring(array_t))
 
 
-def output_kernel(groups, per, chunks, spots, *refs):
+def output_kernel(groups, per, spots, *refs):
     parts, (out_ref, f_ref, y_ref) = refs[:-3], refs[-3:]
     feats, local, width = f_ref.shape
     half = feats // groups // per
-    pairs = half // chunks
-    size = pairs * local
     lanes = -(-feats // 128) * 128
     here = cell_index()
-    for (first_m, some, first_j), part in zip(spots, parts):
+    for (first_m, start, pairs), part in zip(spots, parts):
+        size = pairs * local
         for b in range(part.shape[0]):
-            base = (here ^ (first_m + b // some)) * (half * per) + (first_j + b % some) * pairs
+            base = (here ^ (first_m + b)) * (half * per) + start
             for q in range(per):
                 rows = part[b, q * size : (q + 1) * size].reshape(pairs, local, width)
                 f_ref[pl.ds(base + q * half, pairs)] = rows
@@ -413,10 +410,10 @@
         out_ref[r] = y.T[:, :feats]
 
 
-def make_output(parts, spots, groups, per, chunks, feats, local):
+def make_output(parts, spots, groups, per, feats, local):
     width = parts[0].shape[-1]
     return pl.pallas_call(
-        functools.partial(output_kernel, groups, per, chunks, spots),
+        functools.partial(output_kernel, groups, per, spots),
         in_specs=[IN_VMEM] * len(parts),
         out_specs=IN_VMEM,
         out_shape=jax.ShapeDtypeStruct((local, width, feats), BF),
@@ -440,7 +437,7 @@
 
 
 def dense_kernel(groups, per, spot, fresh, factor, *refs):
-    first_m, chunks, first_j = spot
+    first_m, start, _ = spot
     last = factor is not None
     blocks = refs[-1].shape[0]
     ins = refs[:blocks]
@@ -466,8 +463,7 @@
     w_out_t = woutt_ref[...]
 
     def step(b):
-        group = here ^ (first_m + b // chunks)
-        feature = group * fg + (first_j + b % chunks) * pairs
+        feature = (here ^ (first_m + b)) * fg + start
         normed = n_ref[b]
         cot = [cot_ref[pl.ds(feature + q * half, pairs)].reshape(size, width) for q in range(per)]
         cot = jnp.concatenate(cot, axis=0)
@@ -547,38 +543,39 @@
     half = fg // per
     sub_rows = 16
     row_chunks = local // sub_rows
-    feat_chunks = 2 if half % 2 == 0 else 1
+    sizes = (half * 3 // 7, half - half * 3 // 7) if half % 2 == 0 else (half,)
+    offsets = [sum(sizes[:j]) for j in range(len(sizes))]
+    feat_chunks = len(sizes)
     factor = 1.0 / math.sqrt(tables * local * groups * feats)
-    pairs = half // feat_chunks
     pieces = [[] for _ in range(feat_chunks)]
     cot_t = jnp.swapaxes(cotangent[0], 1, 2)
     sent = feature_chunk(
-        block_t, feat_count, feat_qkv, feat_proj, None, groups, per, 0, sub_rows, 1
+        block_t, feat_count, feat_qkv, feat_proj, None, groups, per, 0, sub_rows, (half,)
     )
     *sent, wqkv_v, wproj_v, rest = sent
     come = exchange(sent, groups)
     for j in range(feat_chunks):
         pieces[j] += come
     *sent, cot_v = feature_chunk(
-        rest, feat_count, wqkv_v, wproj_v, cot_t, groups, per, 0, sub_rows, feat_chunks
+        rest, feat_count, wqkv_v, wproj_v, cot_t, groups, per, 0, sub_rows, sizes
     )
     for j in range(feat_chunks):
         pieces[j] += exchange(sent[j * groups : (j + 1) * groups], groups)
     cot_t = swap_cotangent(cot_v)
     back = []
     for j in range(feat_chunks):
-        starts = (j * pairs, 0)
-        done = row_chunk(pieces[j], train_count, row_qkv, row_proj, groups, per, row_chunks, pairs, starts)
+        starts = (offsets[j], 0)
+        done = row_chunk(pieces[j], train_count, row_qkv, row_proj, groups, per, row_chunks, sizes[j], starts)
         back.append(exchange(done, groups))
     w_out_t = w_out.T
     shares = tables * groups
     near_by = groups // 2
-    spots = [(0, feat_chunks, 0)] + [(near_by, 1, j) for j in range(feat_chunks)]
+    spots = [(m, offsets[j], sizes[j]) for m in (0, near_by) for j in range(feat_chunks)]
     parts = []
     grads = None
     for spot in spots:
-        first_m, some, first_j = spot
-        blocks = [back[first_j + j][first_m + m] for m in range(near_by) for j in range(some)]
+        first_m, start, _ = spot
+        blocks = [back[offsets.index(start)][first_m + m] for m in range(near_by)]
         scale = factor if spot == spots[-1] else None
         made, *grads = dense_part(blocks, cot_t, w_in, w_out_t, grads, groups, per, spot, scale, shares)
         parts.append(made)
@@ -587,7 +584,7 @@
     pieces = add_pair(keep, other)
     total = lax.all_to_all(pieces, ("tables", "chips"), split_axis=0, concat_axis=0, tiled=True)
     total = jnp.sum(total.astype(F32), axis=0)
-    output = make_output(parts, spots, groups, per, feat_chunks, feats, local)
+    output = make_output(parts, spots, groups, per, feats, local)
     grad_in, grad_out = unpack(total, 2, width)
     return (jnp.swapaxes(output, 1, 2)[None], grad_in.T, grad_out)
 

time: 83.6 us -> 78.5 us (0.939)
  waiting for transfers between devices: 25.9 us -> 20.5 us
  starting transfers between devices: 18.6 us -> 19.5 us
    ppermute x15, waiting for transfers between devices: 15.9 us -> 10.5 us  [exchange(): lax.ppermute(pieces[m], CELLS, [(s, s ^ m) for s in range(groups)])]
    pallas_call x3 -> x4, Pallas kernels: 14.2 us -> 13.7 us  [dense_part(): pl.pallas_call(functools.partial(dense_kernel, groups, per, spot, prev is...]
  transfers between devices with their start and end apart: 17 -> 17, of which waited for: 7 -> 7; matrix products, arithmetic and copies ran while one was open for 0% -> 0% of each run, Pallas kernels for 21% -> 32%
where the time goes in v4:
time: 78.5 us; the launch traced here: 78.3 us
  Pallas kernels  35.4 us (45%)
  waiting for transfers between devices  20.5 us (26%)
  starting transfers between devices  19.5 us (25%)
  between operations  2.1 us (3%)
    pallas_call x4, Pallas kernels, dense_part(): pl.pallas_call(functools.partial(dense_kernel, groups, per, spot, prev is...  13.7 us
    ppermute x15, starting transfers between devices, exchange(): lax.ppermute(pieces[m], CELLS, [(s, s ^ m) for s in range(groups)])  12.1 us
    ppermute x15, waiting for transfers between devices, exchange(): lax.ppermute(pieces[m], CELLS, [(s, s ^ m) for s in range(groups)])  10.5 us
    pallas_call x2, Pallas kernels, feature_chunk(): pl.pallas_call(functools.partial(feature_kernel, groups, per, base, rows,...  9.63 us
    all_to_all x1, waiting for transfers between devices, per_device(): lax.all_to_all(pieces, ('tables', 'chips'), split_axis=0, concat_axis=0,...  8.78 us
    pallas_call x2, Pallas kernels, row_chunk(): pl.pallas_call(functools.partial(row_kernel, groups, per, chunks, firsts)...  7.87 us
    all_to_all x1, starting transfers between devices, per_device(): lax.all_to_all(pieces, ('tables', 'chips'), split_axis=0, concat_axis=0,...  6.87 us
    pallas_call x1, Pallas kernels, make_output(): pl.pallas_call(functools.partial(output_kernel, groups, per, spots), in_s...  2.44 us
  transfers between devices with their start and end apart: 17, of which 7 were waited for; matrix products, arithmetic and copies ran while one was open for 0% of the time, Pallas kernels for 32%

profile of v4, /device:TPU:0, one launch (start us, length us, event | category | flops | bytes accessed | tf_op | source)
XLA Modules:
  0.0 78.3 jit_solution(1793537341675312279)
XLA Ops:
  1.3 5.5 %feature_0.1 = (bf16[14,16,384]{2,1,0:T(8,128)(2,1)S(1)}, bf16[14,16,384]{2,1,0:T(8,128)(2,1)S(1)}, bf16[14,16,384]{2,1,0:T(8,128)(2,1)S(1)}, bf16[14,16,384]{2,...) custom-call(s32[1]{0:T(128)S(6)} %copy.26.refs_0_, ...), custom_call_target="tpu_custom_call" | custom-call | flops 100000000 | bytes 1000000 | tf_op jit(solution)/shard_map/feature_0/pallas_call | solution.py:277
  7.3 2.5 %collective-permute-start.1 = (bf16[14,16,384]{2,1,0:T(8,128)(2,1)S(1)}, bf16[14,16,384]{2,1,0:T(8,128)(2,1)S(1)}, u32[]{:S(2)}, u32[]{:S(2)}) collective-permute-start(bf16[14,16,384]{2,1,0:T(8,128)(2,1)S(1)} %get-tuple-element.41), channel_id=1, source_target_pairs={{0,2},{1,3},{2,0},{3,1},{4,6},{5,7},{6,4},{7,5},{8,10},{9,11},{10,... | collective-permute-start | bytes 516104 | tf_op jit(solution)/shard_map/ppermute | solution.py:530
  9.9 4.2 %feature_1.1 = (bf16[6,16,384]{2,1,0:T(8,128)(2,1)S(1)}, bf16[6,16,384]{2,1,0:T(8,128)(2,1)S(1)}, bf16[6,16,384]{2,1,0:T(8,128)(2,1)S(1)}, bf16[6,16,384]{2,1,0:...) custom-call(s32[1]{0:T(128)S(6)} %copy.26.refs_0_, ...), custom_call_target="tpu_custom_call" | custom-call | flops 100000000 | bytes 1000000 | tf_op jit(solution)/shard_map/feature_1/pallas_call | solution.py:277
  14.3 2.0 %collective-permute-start.4 = (bf16[6,16,384]{2,1,0:T(8,128)(2,1)S(1)}, bf16[6,16,384]{2,1,0:T(8,128)(2,1)S(1)}, u32[]{:S(2)}, u32[]{:S(2)}) collective-permute-start(bf16[6,16,384]{2,1,0:T(8,128)(2,1)S(1)} %get-tuple-element.48), channel_id=1, source_target_pairs={{0,2},{1,3},{2,0},{3,1},{4,6},{5,7},{6,4},{7,5},{8,10},{9,11},{10,... | collective-permute-start | bytes 221192 | tf_op jit(solution)/shard_map/ppermute | solution.py:530
  16.3 0.9 %collective-permute-start.5 = (bf16[6,16,384]{2,1,0:T(8,128)(2,1)S(1)}, bf16[6,16,384]{2,1,0:T(8,128)(2,1)S(1)}, u32[]{:S(2)}, u32[]{:S(2)}) collective-permute-start(bf16[6,16,384]{2,1,0:T(8,128)(2,1)S(1)} %get-tuple-element.49), channel_id=1, source_target_pairs={{0,3},{1,2},{2,1},{3,0},{4,7},{5,6},{6,5},{7,4},{8,11},{9,10},{10,... | collective-permute-start | bytes 221192 | tf_op jit(solution)/shard_map/ppermute | solution.py:530
  17.1 3.2 %collective-permute-done.4.refs_6_ = bf16[6,16,384]{2,1,0:T(8,128)(2,1)S(1)} collective-permute-done((bf16[6,16,384]{2,1,0:T(8,128)(2,1)S(1)}, bf16[6,16,384]{2,1,0:T(8,128)(2,1)S(1)}, u32[]{:S(2)}, u32[]{:S(2)}) %collective-permute-start.4) | collective-permute-done | bytes 73760 | tf_op jit(solution)/shard_map/ppermute | solution.py:530
  20.4 1.1 %collective-permute-done.5.refs_7_ = bf16[6,16,384]{2,1,0:T(8,128)(2,1)S(1)} collective-permute-done((bf16[6,16,384]{2,1,0:T(8,128)(2,1)S(1)}, bf16[6,16,384]{2,1,0:T(8,128)(2,1)S(1)}, u32[]{:S(2)}, u32[]{:S(2)}) %collective-permute-start.5) | collective-permute-done | bytes 73760 | tf_op jit(solution)/shard_map/ppermute | solution.py:530
  21.4 1.5 %collective-permute-start.8 = (bf16[8,16,384]{2,1,0:T(8,128)(2,1)S(1)}, bf16[8,16,384]{2,1,0:T(8,128)(2,1)S(1)}, u32[]{:S(2)}, u32[]{:S(2)}) collective-permute-start(bf16[8,16,384]{2,1,0:T(8,128)(2,1)S(1)} %get-tuple-element.56), channel_id=1, source_target_pairs={{0,2},{1,3},{2,0},{3,1},{4,6},{5,7},{6,4},{7,5},{8,10},{9,11},{10,... | collective-permute-start | bytes 294920 | tf_op jit(solution)/shard_map/ppermute | solution.py:530
  23.6 3.4 %shard_map.121 = (bf16[6,32,384]{2,1,0:T(8,128)(2,1)S(1)}, bf16[6,32,384]{2,1,0:T(8,128)(2,1)S(1)}, bf16[6,32,384]{2,1,0:T(8,128)(2,1)S(1)}, bf16[6,32,384]{2,1,0:T(8,128)(2,1)S(1)}) custom-call(s32[1]{0:T(128)S(6)} %copy.25.count_ref, bf16[192,576]{1,0:T(8,128)(2,1)S(1)} %copy-done.2, bf16[192,192]{1,0:T(8,128)(2,1)S(1)} %copy-done.3, ...), custom_call_target="tpu_custom_call" | custom-call | flops 100000000 | bytes 1000000 | tf_op jit(solution)/shard_map/pallas_call | solution.py:343
  28.0 4.4 %shard_map.123 = (bf16[8,32,384]{2,1,0:T(8,128)(2,1)S(1)}, bf16[8,32,384]{2,1,0:T(8,128)(2,1)S(1)}, bf16[8,32,384]{2,1,0:T(8,128)(2,1)S(1)}, bf16[8,32,384]{2,1,0:T(8,128)(2,1)S(1)}) custom-call(s32[1]{0:T(128)S(6)} %copy.25.count_ref, bf16[192,576]{1,0:T(8,128)(2,1)S(1)} %copy-done.2, bf16[192,192]{1,0:T(8,128)(2,1)S(1)} %copy-done.3, ...), custom_call_target="tpu_custom_call" | custom-call | flops 100000000 | bytes 1000000 | tf_op jit(solution)/shard_map/pallas_call | solution.py:343
  32.7 1.8 %collective-permute-start.13 = (bf16[8,32,384]{2,1,0:T(8,128)(2,1)S(1)}, bf16[8,32,384]{2,1,0:T(8,128)(2,1)S(1)}, u32[]{:S(2)}, u32[]{:S(2)}) collective-permute-start(bf16[8,32,384]{2,1,0:T(8,128)(2,1)S(1)} %get-tuple-element.68), channel_id=1, source_target_pairs={{0,2},{1,3},{2,0},{3,1},{4,6},{5,7},{6,4},{7,5},{8,10},{9,11},{10,... | collective-permute-start | bytes 589832 | tf_op jit(solution)/shard_map/ppermute | solution.py:530
  34.4 1.4 %collective-permute-start.11 = (bf16[6,32,384]{2,1,0:T(8,128)(2,1)S(1)}, bf16[6,32,384]{2,1,0:T(8,128)(2,1)S(1)}, u32[]{:S(2)}, u32[]{:S(2)}) collective-permute-start(bf16[6,32,384]{2,1,0:T(8,128)(2,1)S(1)} %get-tuple-element.63), channel_id=1, source_target_pairs={{0,2},{1,3},{2,0},{3,1},{4,6},{5,7},{6,4},{7,5},{8,10},{9,11},{10,... | collective-permute-start | bytes 442376 | tf_op jit(solution)/shard_map/ppermute | solution.py:530
  36.2 1.0 %swap_cotangent.1.refs_4_ = bf16[112,32,192]{2,1,0:T(8,128)(2,1)S(1)} custom-call(bf16[32,192,112]{2,1,0:T(8,128)(2,1)S(1)} %get-tuple-element.52.in_ref), custom_call_target="tpu_custom_call" | custom-call | flops 100000000 | bytes 1000000 | tf_op jit(solution)/shard_map/swap_cotangent/pallas_call | solution.py:375
  37.2 2.9 %shard_map.122 = (bf16[2,384,192]{2,1,0:T(8,128)(2,1)S(1)}, f32[192,768]{1,0:T(8,128)S(1)}, f32[192,768]{1,0:T(8,128)S(1)}) custom-call(bf16[6,32,384]{2,1,0:T(8,128)(2,1)S(1)} %get-tuple-element.50.refs_0_, bf16[6,32,384]{2,1,0:T(8,128)(2,1)S(1)} %collective-permute-done.6.refs_1_, bf16[192,768]{1,0:T(8,128)(2,1)S(1)} %copy-done, ...), custom_call_target="tpu_custom_call" | custom-call | flops 100000000 | bytes 1000000 | tf_op jit(solution)/shard_map/pallas_call | solution.py:499
  40.2 3.6 %shard_map.124 = (bf16[2,512,192]{2,1,0:T(8,128)(2,1)S(1)}, f32[192,768]{1,0:T(8,128)S(1)}, f32[192,768]{1,0:T(8,128)S(1)}) custom-call(bf16[8,32,384]{2,1,0:T(8,128)(2,1)S(1)} %get-tuple-element.58.refs_0_, bf16[8,32,384]{2,1,0:T(8,128)(2,1)S(1)} %collective-permute-done.10.refs_1_, ...), custom_call_target="tpu_custom_call", output_to_operand_aliasing={{1}: (5, {}), {2}: (6, {})} | custom-call | flops 100000000 | bytes 1000000 | tf_op jit(solution)/shard_map/pallas_call | solution.py:499
  43.8 4.0 %collective-permute-done.11.refs_0_ = bf16[6,32,384]{2,1,0:T(8,128)(2,1)S(1)} collective-permute-done((bf16[6,32,384]{2,1,0:T(8,128)(2,1)S(1)}, bf16[6,32,384]{2,1,0:T(8,128)(2,1)S(1)}, u32[]{:S(2)}, u32[]{:S(2)}) %collective-permute-start.11) | collective-permute-done | bytes 147488 | tf_op jit(solution)/shard_map/ppermute | solution.py:530
  47.8 1.9 %collective-permute-done.12.refs_1_ = bf16[6,32,384]{2,1,0:T(8,128)(2,1)S(1)} collective-permute-done((bf16[6,32,384]{2,1,0:T(8,128)(2,1)S(1)}, bf16[6,32,384]{2,1,0:T(8,128)(2,1)S(1)}, u32[]{:S(2)}, u32[]{:S(2)}) %collective-permute-start.12) | collective-permute-done | bytes 147488 | tf_op jit(solution)/shard_map/ppermute | solution.py:530
  49.7 2.9 %shard_map.125 = (bf16[2,384,192]{2,1,0:T(8,128)(2,1)S(1)}, f32[192,768]{1,0:T(8,128)S(1)}, f32[192,768]{1,0:T(8,128)S(1)}) custom-call(bf16[6,32,384]{2,1,0:T(8,128)(2,1)S(1)} %collective-permute-done.11.refs_0_, bf16[6,32,384]{2,1,0:T(8,128)(2,1)S(1)} %collective-permute-done.12.refs_1_, ...), custom_call_target="tpu_custom_call", output_to_operand_aliasing={{1}: (5, {}), {2}: (6, {})} | custom-call | flops 100000000 | bytes 1000000 | tf_op jit(solution)/shard_map/pallas_call | solution.py:499
  52.7 4.2 %shard_map.126 = (bf16[2,512,192]{2,1,0:T(8,128)(2,1)S(1)}, f32[192,768]{1,0:T(8,128)S(1)}, f32[192,768]{1,0:T(8,128)S(1)}, bf16[16,24,384]{2,1,0:T(8,128)(2,1)S(1)}, bf16[16,24,384]{2,1,0:T(8,128)(2,1)S(1)}) custom-call(bf16[8,32,384]{2,1,0:T(8,128)(2,1)S(1)} %collective-permute-done.13.refs_0_, ...), custom_call_target="tpu_custom_call", output_to_operand_aliasing={{1}: (5, {}), {2}: (6, {})} | custom-call | flops 100000000 | bytes 1000000 | tf_op jit(solution)/shard_map/pallas_call | solution.py:499
  57.4 1.2 %collective-permute-done.15.b_ref = bf16[16,24,384]{2,1,0:T(8,128)(2,1)S(1)} collective-permute-done((bf16[16,24,384]{2,1,0:T(8,128)(2,1)S(1)}, bf16[16,24,384]{2,1,0:T(8,128)(2,1)S(1)}, u32[]{:S(2)}, u32[]{:S(2)}) %collective-permute-start.15) | collective-permute-done | bytes 294944 | tf_op jit(solution)/shard_map/ppermute | solution.py:583
  58.6 0.8 add_pair.1
  59.4 6.9 %all-to-all-start = ((bf16[16,24,384]{2,1,0:T(8,128)(2,1)}), bf16[16,24,384]{2,1,0:T(8,128)(2,1)S(1)}, u32[]{:S(2)}, u32[]{:S(2)}) async-start(bf16[16,24,384]{2,1,0:T(8,128)(2,1)} %add_pair.1), calls=%async_computation | async-start | bytes 589824 | tf_op jit(solution)/shard_map/all_to_all | solution.py:585
  66.3 2.4 %make_output.1 = bf16[32,192,112]{2,1,0:T(8,128)(2,1)} custom-call(bf16[2,384,192]{2,1,0:T(8,128)(2,1)S(1)} %get-tuple-element.53.refs_0_, bf16[2,512,192]{2,1,0:T(8,128)(2,1)S(1)} %get-tuple-element.62.refs_1_, bf16[2,384,192]{2,1,0:T(8,128)(2,1)S(1)} %get-tuple-element.67.refs_2_, bf16[2,512,192]{2,1,0:T(8,128)(2,1)S(1)} %get-tuple-element.72.refs_3_), custom_call_target="tpu_custom_call" | custom-call | flops 100000000 | bytes 1000000 | tf_op jit(solution)/shard_map/make_output/pallas_call | solution.py:415
  68.7 8.8 %all-to-all-done = bf16[16,24,384]{2,1,0:T(8,128)(2,1)S(1)} async-done(((bf16[16,24,384]{2,1,0:T(8,128)(2,1)}), bf16[16,24,384]{2,1,0:T(8,128)(2,1)S(1)}, u32[]{:S(2)}, u32[]{:S(2)}) %all-to-all-start) | async-done | bytes 294944 | tf_op jit(solution)/shard_map/all_to_all | solution.py:585
  (33 shorter events, 3.6 us)
Async XLA Ops:
  6.8 16.8 %copy-start.2 = (bf16[192,576]{1,0:T(8,128)(2,1)S(1)}, bf16[192,576]{1,0:T(8,128)(2,1)}, u32[]{:S(2)}) copy-start(bf16[192,576]{1,0:T(8,128)(2,1)} %wqkv_ref.3) | copy-start | bytes 663556
  6.8 16.8 %copy-start.3 = (bf16[192,192]{1,0:T(8,128)(2,1)S(1)}, bf16[192,192]{1,0:T(8,128)(2,1)}, u32[]{:S(2)}) copy-start(bf16[192,192]{1,0:T(8,128)(2,1)} %wproj_ref.3) | copy-start | bytes 221188
  6.8 16.1 %collective-permute-start = (bf16[14,16,384]{2,1,0:T(8,128)(2,1)S(1)}, bf16[14,16,384]{2,1,0:T(8,128)(2,1)S(1)}, u32[]{:S(2)}, u32[]{:S(2)}) collective-permute-start(bf16[14,16,384]{2,1,0:T(8,128)(2,1)S(1)} %get-tuple-element.40), channel_id=1, source_target_pairs={{0,1},{1,0},{2,3},{3,2},{4,5},{5,4},{6,7},{7,6},{8,9},{9,8},{10,11... | collective-permute-start | bytes 516104 | tf_op jit(solution)/shard_map/ppermute | solution.py:530
  7.3 16.2 %collective-permute-start.1 = (bf16[14,16,384]{2,1,0:T(8,128)(2,1)S(1)}, bf16[14,16,384]{2,1,0:T(8,128)(2,1)S(1)}, u32[]{:S(2)}, u32[]{:S(2)}) collective-permute-start(bf16[14,16,384]{2,1,0:T(8,128)(2,1)S(1)} %get-tuple-element.41), channel_id=1, source_target_pairs={{0,2},{1,3},{2,0},{3,1},{4,6},{5,7},{6,4},{7,5},{8,10},{9,11},{10,... | collective-permute-start | bytes 516104 | tf_op jit(solution)/shard_map/ppermute | solution.py:530
  9.9 13.7 %collective-permute-start.2 = (bf16[14,16,384]{2,1,0:T(8,128)(2,1)S(1)}, bf16[14,16,384]{2,1,0:T(8,128)(2,1)S(1)}, u32[]{:S(2)}, u32[]{:S(2)}) collective-permute-start(bf16[14,16,384]{2,1,0:T(8,128)(2,1)S(1)} %get-tuple-element.42), channel_id=1, source_target_pairs={{0,3},{1,2},{2,1},{3,0},{4,7},{5,6},{6,5},{7,4},{8,11},{9,10},{10,... | collective-permute-start | bytes 516104 | tf_op jit(solution)/shard_map/ppermute | solution.py:530
  14.1 2.2 %collective-permute-start.3 = (bf16[6,16,384]{2,1,0:T(8,128)(2,1)S(1)}, bf16[6,16,384]{2,1,0:T(8,128)(2,1)S(1)}, u32[]{:S(2)}, u32[]{:S(2)}) collective-permute-start(bf16[6,16,384]{2,1,0:T(8,128)(2,1)S(1)} %get-tuple-element.47), channel_id=1, source_target_pairs={{0,1},{1,0},{2,3},{3,2},{4,5},{5,4},{6,7},{7,6},{8,9},{9,8},{10,11... | collective-permute-start | bytes 221192 | tf_op jit(solution)/shard_map/ppermute | solution.py:530
  14.3 6.1 %collective-permute-start.4 = (bf16[6,16,384]{2,1,0:T(8,128)(2,1)S(1)}, bf16[6,16,384]{2,1,0:T(8,128)(2,1)S(1)}, u32[]{:S(2)}, u32[]{:S(2)}) collective-permute-start(bf16[6,16,384]{2,1,0:T(8,128)(2,1)S(1)} %get-tuple-element.48), channel_id=1, source_target_pairs={{0,2},{1,3},{2,0},{3,1},{4,6},{5,7},{6,4},{7,5},{8,10},{9,11},{10,... | collective-permute-start | bytes 221192 | tf_op jit(solution)/shard_map/ppermute | solution.py:530
  16.3 5.2 %collective-permute-start.5 = (bf16[6,16,384]{2,1,0:T(8,128)(2,1)S(1)}, bf16[6,16,384]{2,1,0:T(8,128)(2,1)S(1)}, u32[]{:S(2)}, u32[]{:S(2)}) collective-permute-start(bf16[6,16,384]{2,1,0:T(8,128)(2,1)S(1)} %get-tuple-element.49), channel_id=1, source_target_pairs={{0,3},{1,2},{2,1},{3,0},{4,7},{5,6},{6,5},{7,4},{8,11},{9,10},{10,... | collective-permute-start | bytes 221192 | tf_op jit(solution)/shard_map/ppermute | solution.py:530
  20.4 7.4 %collective-permute-start.7 = (bf16[8,16,384]{2,1,0:T(8,128)(2,1)S(1)}, bf16[8,16,384]{2,1,0:T(8,128)(2,1)S(1)}, u32[]{:S(2)}, u32[]{:S(2)}) collective-permute-start(bf16[8,16,384]{2,1,0:T(8,128)(2,1)S(1)} %get-tuple-element.55), channel_id=1, source_target_pairs={{0,1},{1,0},{2,3},{3,2},{4,5},{5,4},{6,7},{7,6},{8,9},{9,8},{10,11... | collective-permute-start | bytes 294920 | tf_op jit(solution)/shard_map/ppermute | solution.py:530
  21.4 6.3 %collective-permute-start.8 = (bf16[8,16,384]{2,1,0:T(8,128)(2,1)S(1)}, bf16[8,16,384]{2,1,0:T(8,128)(2,1)S(1)}, u32[]{:S(2)}, u32[]{:S(2)}) collective-permute-start(bf16[8,16,384]{2,1,0:T(8,128)(2,1)S(1)} %get-tuple-element.56), channel_id=1, source_target_pairs={{0,2},{1,3},{2,0},{3,1},{4,6},{5,7},{6,4},{7,5},{8,10},{9,11},{10,... | collective-permute-start | bytes 294920 | tf_op jit(solution)/shard_map/ppermute | solution.py:530
  22.9 5.1 %collective-permute-start.9 = (bf16[8,16,384]{2,1,0:T(8,128)(2,1)S(1)}, bf16[8,16,384]{2,1,0:T(8,128)(2,1)S(1)}, u32[]{:S(2)}, u32[]{:S(2)}) collective-permute-start(bf16[8,16,384]{2,1,0:T(8,128)(2,1)S(1)} %get-tuple-element.57), channel_id=1, source_target_pairs={{0,3},{1,2},{2,1},{3,0},{4,7},{5,6},{6,5},{7,4},{8,11},{9,10},{10,... | collective-permute-start | bytes 294920 | tf_op jit(solution)/shard_map/ppermute | solution.py:530
  27.1 8.8 %collective-permute-start.6 = (bf16[6,32,384]{2,1,0:T(8,128)(2,1)S(1)}, bf16[6,32,384]{2,1,0:T(8,128)(2,1)S(1)}, u32[]{:S(2)}, u32[]{:S(2)}) collective-permute-start(bf16[6,32,384]{2,1,0:T(8,128)(2,1)S(1)} %get-tuple-element.51), channel_id=1, source_target_pairs={{0,1},{1,0},{2,3},{3,2},{4,5},{5,4},{6,7},{7,6},{8,9},{9,8},{10,11... | collective-permute-start | bytes 442376 | tf_op jit(solution)/shard_map/ppermute | solution.py:530
  32.5 7.7 %collective-permute-start.10 = (bf16[8,32,384]{2,1,0:T(8,128)(2,1)S(1)}, bf16[8,32,384]{2,1,0:T(8,128)(2,1)S(1)}, u32[]{:S(2)}, u32[]{:S(2)}) collective-permute-start(bf16[8,32,384]{2,1,0:T(8,128)(2,1)S(1)} %get-tuple-element.59), channel_id=1, source_target_pairs={{0,1},{1,0},{2,3},{3,2},{4,5},{5,4},{6,7},{7,6},{8,9},{9,8},{10,11... | collective-permute-start | bytes 589832 | tf_op jit(solution)/shard_map/ppermute | solution.py:530
  32.7 20.0 %collective-permute-start.13 = (bf16[8,32,384]{2,1,0:T(8,128)(2,1)S(1)}, bf16[8,32,384]{2,1,0:T(8,128)(2,1)S(1)}, u32[]{:S(2)}, u32[]{:S(2)}) collective-permute-start(bf16[8,32,384]{2,1,0:T(8,128)(2,1)S(1)} %get-tuple-element.68), channel_id=1, source_target_pairs={{0,2},{1,3},{2,0},{3,1},{4,6},{5,7},{6,4},{7,5},{8,10},{9,11},{10,... | collective-permute-start | bytes 589832 | tf_op jit(solution)/shard_map/ppermute | solution.py:530
  34.4 18.2 %collective-permute-start.14 = (bf16[8,32,384]{2,1,0:T(8,128)(2,1)S(1)}, bf16[8,32,384]{2,1,0:T(8,128)(2,1)S(1)}, u32[]{:S(2)}, u32[]{:S(2)}) collective-permute-start(bf16[8,32,384]{2,1,0:T(8,128)(2,1)S(1)} %get-tuple-element.69), channel_id=1, source_target_pairs={{0,3},{1,2},{2,1},{3,0},{4,7},{5,6},{6,5},{7,4},{8,11},{9,10},{10,... | collective-permute-start | bytes 589832 | tf_op jit(solution)/shard_map/ppermute | solution.py:530
  34.4 13.4 %collective-permute-start.11 = (bf16[6,32,384]{2,1,0:T(8,128)(2,1)S(1)}, bf16[6,32,384]{2,1,0:T(8,128)(2,1)S(1)}, u32[]{:S(2)}, u32[]{:S(2)}) collective-permute-start(bf16[6,32,384]{2,1,0:T(8,128)(2,1)S(1)} %get-tuple-element.63), channel_id=1, source_target_pairs={{0,2},{1,3},{2,0},{3,1},{4,6},{5,7},{6,4},{7,5},{8,10},{9,11},{10,... | collective-permute-start | bytes 442376 | tf_op jit(solution)/shard_map/ppermute | solution.py:530
  35.9 13.9 %collective-permute-start.12 = (bf16[6,32,384]{2,1,0:T(8,128)(2,1)S(1)}, bf16[6,32,384]{2,1,0:T(8,128)(2,1)S(1)}, u32[]{:S(2)}, u32[]{:S(2)}) collective-permute-start(bf16[6,32,384]{2,1,0:T(8,128)(2,1)S(1)} %get-tuple-element.64), channel_id=1, source_target_pairs={{0,3},{1,2},{2,1},{3,0},{4,7},{5,6},{6,5},{7,4},{8,11},{9,10},{10,... | collective-permute-start | bytes 442376 | tf_op jit(solution)/shard_map/ppermute | solution.py:530
  36.2 1.0 %copy-start = (bf16[192,768]{1,0:T(8,128)(2,1)S(1)}, bf16[192,768]{1,0:T(8,128)(2,1)}, u32[]{:S(2)}) copy-start(bf16[192,768]{1,0:T(8,128)(2,1)} %refs_2_.9) | copy-start | bytes 884740
  36.2 1.0 %copy-start.1 = (bf16[768,192]{0,1:T(8,128)(2,1)S(1)}, bf16[768,192]{0,1:T(8,128)(2,1)}, u32[]{:S(2)}) copy-start(bf16[768,192]{0,1:T(8,128)(2,1)} %param.18) | copy-start | bytes 884740
  56.9 1.7 %collective-permute-start.15 = (bf16[16,24,384]{2,1,0:T(8,128)(2,1)S(1)}, bf16[16,24,384]{2,1,0:T(8,128)(2,1)S(1)}, u32[]{:S(2)}, u32[]{:S(2)}) collective-permute-start(bf16[16,24,384]{2,1,0:T(8,128)(2,1)S(1)} %get-tuple-element.74), channel_id=1, source_target_pairs={{0,1},{1,0},{2,3},{3,2},{4,5},{5,4},{6,7},{7,6},{8,9},{9,8},{10,11... | collective-permute-start | bytes 884744 | tf_op jit(solution)/shard_map/ppermute | solution.py:583
  59.4 18.1 %all-to-all-start = ((bf16[16,24,384]{2,1,0:T(8,128)(2,1)}), bf16[16,24,384]{2,1,0:T(8,128)(2,1)S(1)}, u32[]{:S(2)}, u32[]{:S(2)}) async-start(bf16[16,24,384]{2,1,0:T(8,128)(2,1)} %add_pair.1), calls=%async_computation | async-start | bytes 589824 | tf_op jit(solution)/shard_map/all_to_all | solution.py:585

commit v5 on v4

--- a/solution.py
+++ b/solution.py
@@ -168,10 +168,13 @@
         outs = refs[: groups * len(cuts)]
         wqkv_buf, wproj_buf, rest_buf, *refs = refs[groups * len(cuts) :]
         sems, cells_buf = refs[6:]
-        moves = [(wqkv_ref, wqkv_buf), (wproj_ref, wproj_buf), (cells_ref.at[pl.ds(0, rows)], cells_buf)]
+        moves = [(wqkv_ref, wqkv_buf)]
+        for n in range(0, rows, 4):
+            moves.append((cells_ref.at[pl.ds(n, 4)], cells_buf.at[pl.ds(n, 4)]))
+        moves.append((wproj_ref, wproj_buf))
         late = (cells_ref.at[pl.ds(rows, rest_buf.shape[0])], rest_buf)
         moves = [pltpu.make_async_copy(a, b, sems.at[n]) for n, (a, b) in enumerate(moves)]
-        late = pltpu.make_async_copy(*late, sems.at[3])
+        late = pltpu.make_async_copy(*late, sems.at[len(moves)])
         for move in moves:
             move.start()
         for move in moves:
@@ -268,7 +271,7 @@
         operands = [pltpu.with_memory_space_constraint(x, pltpu.HBM) for x in operands]
         specs = [far] * 3
         outs += [near(wqkv.shape), near(wproj.shape), near((whole - rows, width, feats))]
-        scratch += [pltpu.SemaphoreType.DMA((4,)), pltpu.VMEM((rows, width, feats), BF)]
+        scratch += [pltpu.SemaphoreType.DMA((3 + rows // 4,)), pltpu.VMEM((rows, width, feats), BF)]
     else:
         operands = bring(*operands) + [pltpu.with_memory_space_constraint(cot_t, pltpu.HBM)]
         specs = [IN_VMEM] * 3 + [far]

time: 78.5 us -> 78.6 us (level)
  no operation moved by 1% of the time
where the time goes in v5:
time: 78.6 us; the launch traced here: 78.3 us
  Pallas kernels  35.4 us (45%)
  waiting for transfers between devices  20.4 us (26%)
  starting transfers between devices  19.5 us (25%)
  between operations  2.1 us (3%)
    pallas_call x4, Pallas kernels, dense_part(): pl.pallas_call(functools.partial(dense_kernel, groups, per, spot, prev is...  13.7 us
    ppermute x15, starting transfers between devices, exchange(): lax.ppermute(pieces[m], CELLS, [(s, s ^ m) for s in range(groups)])  12.2 us
    ppermute x15, waiting for transfers between devices, exchange(): lax.ppermute(pieces[m], CELLS, [(s, s ^ m) for s in range(groups)])  10.4 us
    pallas_call x2, Pallas kernels, feature_chunk(): pl.pallas_call(functools.partial(feature_kernel, groups, per, base, rows,...  9.67 us
    all_to_all x1, waiting for transfers between devices, per_device(): lax.all_to_all(pieces, ('tables', 'chips'), split_axis=0, concat_axis=0,...  8.78 us
    pallas_call x2, Pallas kernels, row_chunk(): pl.pallas_call(functools.partial(row_kernel, groups, per, chunks, firsts)...  7.86 us
    all_to_all x1, starting transfers between devices, per_device(): lax.all_to_all(pieces, ('tables', 'chips'), split_axis=0, concat_axis=0,...  6.86 us
    pallas_call x1, Pallas kernels, make_output(): pl.pallas_call(functools.partial(output_kernel, groups, per, spots), in_s...  2.44 us
  transfers between devices with their start and end apart: 17, of which 7 were waited for; matrix products, arithmetic and copies ran while one was open for 0% of the time, Pallas kernels for 32%

profile of v5, /device:TPU:0, one launch (start us, length us, event | category | flops | bytes accessed | tf_op | source)
XLA Modules:
  0.0 78.3 jit_solution(594180145608226897)
XLA Ops:
  1.3 5.5 %feature_0.1 = (bf16[14,16,384]{2,1,0:T(8,128)(2,1)S(1)}, bf16[14,16,384]{2,1,0:T(8,128)(2,1)S(1)}, bf16[14,16,384]{2,1,0:T(8,128)(2,1)S(1)}, bf16[14,16,384]{2,...) custom-call(s32[1]{0:T(128)S(6)} %copy.26.refs_0_, ...), custom_call_target="tpu_custom_call" | custom-call | flops 100000000 | bytes 1000000 | tf_op jit(solution)/shard_map/feature_0/pallas_call | solution.py:280
  7.4 2.6 %collective-permute-start.1 = (bf16[14,16,384]{2,1,0:T(8,128)(2,1)S(1)}, bf16[14,16,384]{2,1,0:T(8,128)(2,1)S(1)}, u32[]{:S(2)}, u32[]{:S(2)}) collective-permute-start(bf16[14,16,384]{2,1,0:T(8,128)(2,1)S(1)} %get-tuple-element.41), channel_id=1, source_target_pairs={{0,2},{1,3},{2,0},{3,1},{4,6},{5,7},{6,4},{7,5},{8,10},{9,11},{10,... | collective-permute-start | bytes 516104 | tf_op jit(solution)/shard_map/ppermute | solution.py:533
  10.0 4.2 %feature_1.1 = (bf16[6,16,384]{2,1,0:T(8,128)(2,1)S(1)}, bf16[6,16,384]{2,1,0:T(8,128)(2,1)S(1)}, bf16[6,16,384]{2,1,0:T(8,128)(2,1)S(1)}, bf16[6,16,384]{2,1,0:...) custom-call(s32[1]{0:T(128)S(6)} %copy.26.refs_0_, ...), custom_call_target="tpu_custom_call" | custom-call | flops 100000000 | bytes 1000000 | tf_op jit(solution)/shard_map/feature_1/pallas_call | solution.py:280
  14.4 1.9 %collective-permute-start.4 = (bf16[6,16,384]{2,1,0:T(8,128)(2,1)S(1)}, bf16[6,16,384]{2,1,0:T(8,128)(2,1)S(1)}, u32[]{:S(2)}, u32[]{:S(2)}) collective-permute-start(bf16[6,16,384]{2,1,0:T(8,128)(2,1)S(1)} %get-tuple-element.48), channel_id=1, source_target_pairs={{0,2},{1,3},{2,0},{3,1},{4,6},{5,7},{6,4},{7,5},{8,10},{9,11},{10,... | collective-permute-start | bytes 221192 | tf_op jit(solution)/shard_map/ppermute | solution.py:533
  16.3 0.9 %collective-permute-start.5 = (bf16[6,16,384]{2,1,0:T(8,128)(2,1)S(1)}, bf16[6,16,384]{2,1,0:T(8,128)(2,1)S(1)}, u32[]{:S(2)}, u32[]{:S(2)}) collective-permute-start(bf16[6,16,384]{2,1,0:T(8,128)(2,1)S(1)} %get-tuple-element.49), channel_id=1, source_target_pairs={{0,3},{1,2},{2,1},{3,0},{4,7},{5,6},{6,5},{7,4},{8,11},{9,10},{10,... | collective-permute-start | bytes 221192 | tf_op jit(solution)/shard_map/ppermute | solution.py:533
  17.2 3.2 %collective-permute-done.4.refs_6_ = bf16[6,16,384]{2,1,0:T(8,128)(2,1)S(1)} collective-permute-done((bf16[6,16,384]{2,1,0:T(8,128)(2,1)S(1)}, bf16[6,16,384]{2,1,0:T(8,128)(2,1)S(1)}, u32[]{:S(2)}, u32[]{:S(2)}) %collective-permute-start.4) | collective-permute-done | bytes 73760 | tf_op jit(solution)/shard_map/ppermute | solution.py:533
  20.4 1.1 %collective-permute-done.5.refs_7_ = bf16[6,16,384]{2,1,0:T(8,128)(2,1)S(1)} collective-permute-done((bf16[6,16,384]{2,1,0:T(8,128)(2,1)S(1)}, bf16[6,16,384]{2,1,0:T(8,128)(2,1)S(1)}, u32[]{:S(2)}, u32[]{:S(2)}) %collective-permute-start.5) | collective-permute-done | bytes 73760 | tf_op jit(solution)/shard_map/ppermute | solution.py:533
  21.5 1.5 %collective-permute-start.8 = (bf16[8,16,384]{2,1,0:T(8,128)(2,1)S(1)}, bf16[8,16,384]{2,1,0:T(8,128)(2,1)S(1)}, u32[]{:S(2)}, u32[]{:S(2)}) collective-permute-start(bf16[8,16,384]{2,1,0:T(8,128)(2,1)S(1)} %get-tuple-element.56), channel_id=1, source_target_pairs={{0,2},{1,3},{2,0},{3,1},{4,6},{5,7},{6,4},{7,5},{8,10},{9,11},{10,... | collective-permute-start | bytes 294920 | tf_op jit(solution)/shard_map/ppermute | solution.py:533
  23.7 3.4 %shard_map.121 = (bf16[6,32,384]{2,1,0:T(8,128)(2,1)S(1)}, bf16[6,32,384]{2,1,0:T(8,128)(2,1)S(1)}, bf16[6,32,384]{2,1,0:T(8,128)(2,1)S(1)}, bf16[6,32,384]{2,1,0:T(8,128)(2,1)S(1)}) custom-call(s32[1]{0:T(128)S(6)} %copy.25.count_ref, bf16[192,576]{1,0:T(8,128)(2,1)S(1)} %copy-done.2, bf16[192,192]{1,0:T(8,128)(2,1)S(1)} %copy-done.3, ...), custom_call_target="tpu_custom_call" | custom-call | flops 100000000 | bytes 1000000 | tf_op jit(solution)/shard_map/pallas_call | solution.py:346
  28.1 4.4 %shard_map.123 = (bf16[8,32,384]{2,1,0:T(8,128)(2,1)S(1)}, bf16[8,32,384]{2,1,0:T(8,128)(2,1)S(1)}, bf16[8,32,384]{2,1,0:T(8,128)(2,1)S(1)}, bf16[8,32,384]{2,1,0:T(8,128)(2,1)S(1)}) custom-call(s32[1]{0:T(128)S(6)} %copy.25.count_ref, bf16[192,576]{1,0:T(8,128)(2,1)S(1)} %copy-done.2, bf16[192,192]{1,0:T(8,128)(2,1)S(1)} %copy-done.3, ...), custom_call_target="tpu_custom_call" | custom-call | flops 100000000 | bytes 1000000 | tf_op jit(solution)/shard_map/pallas_call | solution.py:346
  32.7 1.7 %collective-permute-start.13 = (bf16[8,32,384]{2,1,0:T(8,128)(2,1)S(1)}, bf16[8,32,384]{2,1,0:T(8,128)(2,1)S(1)}, u32[]{:S(2)}, u32[]{:S(2)}) collective-permute-start(bf16[8,32,384]{2,1,0:T(8,128)(2,1)S(1)} %get-tuple-element.68), channel_id=1, source_target_pairs={{0,2},{1,3},{2,0},{3,1},{4,6},{5,7},{6,4},{7,5},{8,10},{9,11},{10,... | collective-permute-start | bytes 589832 | tf_op jit(solution)/shard_map/ppermute | solution.py:533
  34.5 1.4 %collective-permute-start.11 = (bf16[6,32,384]{2,1,0:T(8,128)(2,1)S(1)}, bf16[6,32,384]{2,1,0:T(8,128)(2,1)S(1)}, u32[]{:S(2)}, u32[]{:S(2)}) collective-permute-start(bf16[6,32,384]{2,1,0:T(8,128)(2,1)S(1)} %get-tuple-element.63), channel_id=1, source_target_pairs={{0,2},{1,3},{2,0},{3,1},{4,6},{5,7},{6,4},{7,5},{8,10},{9,11},{10,... | collective-permute-start | bytes 442376 | tf_op jit(solution)/shard_map/ppermute | solution.py:533
  36.2 1.0 %swap_cotangent.1.refs_4_ = bf16[112,32,192]{2,1,0:T(8,128)(2,1)S(1)} custom-call(bf16[32,192,112]{2,1,0:T(8,128)(2,1)S(1)} %get-tuple-element.52.in_ref), custom_call_target="tpu_custom_call" | custom-call | flops 100000000 | bytes 1000000 | tf_op jit(solution)/shard_map/swap_cotangent/pallas_call | solution.py:378
  37.3 2.9 %shard_map.122 = (bf16[2,384,192]{2,1,0:T(8,128)(2,1)S(1)}, f32[192,768]{1,0:T(8,128)S(1)}, f32[192,768]{1,0:T(8,128)S(1)}) custom-call(bf16[6,32,384]{2,1,0:T(8,128)(2,1)S(1)} %get-tuple-element.50.refs_0_, bf16[6,32,384]{2,1,0:T(8,128)(2,1)S(1)} %collective-permute-done.6.refs_1_, bf16[192,768]{1,0:T(8,128)(2,1)S(1)} %copy-done, ...), custom_call_target="tpu_custom_call" | custom-call | flops 100000000 | bytes 1000000 | tf_op jit(solution)/shard_map/pallas_call | solution.py:502
  40.2 3.6 %shard_map.124 = (bf16[2,512,192]{2,1,0:T(8,128)(2,1)S(1)}, f32[192,768]{1,0:T(8,128)S(1)}, f32[192,768]{1,0:T(8,128)S(1)}) custom-call(bf16[8,32,384]{2,1,0:T(8,128)(2,1)S(1)} %get-tuple-element.58.refs_0_, bf16[8,32,384]{2,1,0:T(8,128)(2,1)S(1)} %collective-permute-done.10.refs_1_, ...), custom_call_target="tpu_custom_call", output_to_operand_aliasing={{1}: (5, {}), {2}: (6, {})} | custom-call | flops 100000000 | bytes 1000000 | tf_op jit(solution)/shard_map/pallas_call | solution.py:502
  43.9 4.0 %collective-permute-done.11.refs_0_ = bf16[6,32,384]{2,1,0:T(8,128)(2,1)S(1)} collective-permute-done((bf16[6,32,384]{2,1,0:T(8,128)(2,1)S(1)}, bf16[6,32,384]{2,1,0:T(8,128)(2,1)S(1)}, u32[]{:S(2)}, u32[]{:S(2)}) %collective-permute-start.11) | collective-permute-done | bytes 147488 | tf_op jit(solution)/shard_map/ppermute | solution.py:533
  47.9 1.9 %collective-permute-done.12.refs_1_ = bf16[6,32,384]{2,1,0:T(8,128)(2,1)S(1)} collective-permute-done((bf16[6,32,384]{2,1,0:T(8,128)(2,1)S(1)}, bf16[6,32,384]{2,1,0:T(8,128)(2,1)S(1)}, u32[]{:S(2)}, u32[]{:S(2)}) %collective-permute-start.12) | collective-permute-done | bytes 147488 | tf_op jit(solution)/shard_map/ppermute | solution.py:533
  49.8 2.9 %shard_map.125 = (bf16[2,384,192]{2,1,0:T(8,128)(2,1)S(1)}, f32[192,768]{1,0:T(8,128)S(1)}, f32[192,768]{1,0:T(8,128)S(1)}) custom-call(bf16[6,32,384]{2,1,0:T(8,128)(2,1)S(1)} %collective-permute-done.11.refs_0_, bf16[6,32,384]{2,1,0:T(8,128)(2,1)S(1)} %collective-permute-done.12.refs_1_, ...), custom_call_target="tpu_custom_call", output_to_operand_aliasing={{1}: (5, {}), {2}: (6, {})} | custom-call | flops 100000000 | bytes 1000000 | tf_op jit(solution)/shard_map/pallas_call | solution.py:502
  52.7 4.2 %shard_map.126 = (bf16[2,512,192]{2,1,0:T(8,128)(2,1)S(1)}, f32[192,768]{1,0:T(8,128)S(1)}, f32[192,768]{1,0:T(8,128)S(1)}, bf16[16,24,384]{2,1,0:T(8,128)(2,1)S(1)}, bf16[16,24,384]{2,1,0:T(8,128)(2,1)S(1)}) custom-call(bf16[8,32,384]{2,1,0:T(8,128)(2,1)S(1)} %collective-permute-done.13.refs_0_, ...), custom_call_target="tpu_custom_call", output_to_operand_aliasing={{1}: (5, {}), {2}: (6, {})} | custom-call | flops 100000000 | bytes 1000000 | tf_op jit(solution)/shard_map/pallas_call | solution.py:502
  57.5 1.2 %collective-permute-done.15.b_ref = bf16[16,24,384]{2,1,0:T(8,128)(2,1)S(1)} collective-permute-done((bf16[16,24,384]{2,1,0:T(8,128)(2,1)S(1)}, bf16[16,24,384]{2,1,0:T(8,128)(2,1)S(1)}, u32[]{:S(2)}, u32[]{:S(2)}) %collective-permute-start.15) | collective-permute-done | bytes 294944 | tf_op jit(solution)/shard_map/ppermute | solution.py:586
  58.7 0.8 add_pair.1
  59.5 6.9 %all-to-all-start = ((bf16[16,24,384]{2,1,0:T(8,128)(2,1)}), bf16[16,24,384]{2,1,0:T(8,128)(2,1)S(1)}, u32[]{:S(2)}, u32[]{:S(2)}) async-start(bf16[16,24,384]{2,1,0:T(8,128)(2,1)} %add_pair.1), calls=%async_computation | async-start | bytes 589824 | tf_op jit(solution)/shard_map/all_to_all | solution.py:588
  66.3 2.4 %make_output.1 = bf16[32,192,112]{2,1,0:T(8,128)(2,1)} custom-call(bf16[2,384,192]{2,1,0:T(8,128)(2,1)S(1)} %get-tuple-element.53.refs_0_, bf16[2,512,192]{2,1,0:T(8,128)(2,1)S(1)} %get-tuple-element.62.refs_1_, bf16[2,384,192]{2,1,0:T(8,128)(2,1)S(1)} %get-tuple-element.67.refs_2_, bf16[2,512,192]{2,1,0:T(8,128)(2,1)S(1)} %get-tuple-element.72.refs_3_), custom_call_target="tpu_custom_call" | custom-call | flops 100000000 | bytes 1000000 | tf_op jit(solution)/shard_map/make_output/pallas_call | solution.py:418
  68.8 8.8 %all-to-all-done = bf16[16,24,384]{2,1,0:T(8,128)(2,1)S(1)} async-done(((bf16[16,24,384]{2,1,0:T(8,128)(2,1)}), bf16[16,24,384]{2,1,0:T(8,128)(2,1)S(1)}, u32[]{:S(2)}, u32[]{:S(2)}) %all-to-all-start) | async-done | bytes 294944 | tf_op jit(solution)/shard_map/all_to_all | solution.py:588
  (33 shorter events, 3.7 us)
Async XLA Ops:
  6.8 16.8 %copy-start.2 = (bf16[192,576]{1,0:T(8,128)(2,1)S(1)}, bf16[192,576]{1,0:T(8,128)(2,1)}, u32[]{:S(2)}) copy-start(bf16[192,576]{1,0:T(8,128)(2,1)} %wqkv_ref.3) | copy-start | bytes 663556
  6.8 16.8 %copy-start.3 = (bf16[192,192]{1,0:T(8,128)(2,1)S(1)}, bf16[192,192]{1,0:T(8,128)(2,1)}, u32[]{:S(2)}) copy-start(bf16[192,192]{1,0:T(8,128)(2,1)} %wproj_ref.3) | copy-start | bytes 221188
  6.8 16.1 %collective-permute-start = (bf16[14,16,384]{2,1,0:T(8,128)(2,1)S(1)}, bf16[14,16,384]{2,1,0:T(8,128)(2,1)S(1)}, u32[]{:S(2)}, u32[]{:S(2)}) collective-permute-start(bf16[14,16,384]{2,1,0:T(8,128)(2,1)S(1)} %get-tuple-element.40), channel_id=1, source_target_pairs={{0,1},{1,0},{2,3},{3,2},{4,5},{5,4},{6,7},{7,6},{8,9},{9,8},{10,11... | collective-permute-start | bytes 516104 | tf_op jit(solution)/shard_map/ppermute | solution.py:533
  7.4 16.2 %collective-permute-start.1 = (bf16[14,16,384]{2,1,0:T(8,128)(2,1)S(1)}, bf16[14,16,384]{2,1,0:T(8,128)(2,1)S(1)}, u32[]{:S(2)}, u32[]{:S(2)}) collective-permute-start(bf16[14,16,384]{2,1,0:T(8,128)(2,1)S(1)} %get-tuple-element.41), channel_id=1, source_target_pairs={{0,2},{1,3},{2,0},{3,1},{4,6},{5,7},{6,4},{7,5},{8,10},{9,11},{10,... | collective-permute-start | bytes 516104 | tf_op jit(solution)/shard_map/ppermute | solution.py:533
  9.9 13.7 %collective-permute-start.2 = (bf16[14,16,384]{2,1,0:T(8,128)(2,1)S(1)}, bf16[14,16,384]{2,1,0:T(8,128)(2,1)S(1)}, u32[]{:S(2)}, u32[]{:S(2)}) collective-permute-start(bf16[14,16,384]{2,1,0:T(8,128)(2,1)S(1)} %get-tuple-element.42), channel_id=1, source_target_pairs={{0,3},{1,2},{2,1},{3,0},{4,7},{5,6},{6,5},{7,4},{8,11},{9,10},{10,... | collective-permute-start | bytes 516104 | tf_op jit(solution)/shard_map/ppermute | solution.py:533
  14.1 2.2 %collective-permute-start.3 = (bf16[6,16,384]{2,1,0:T(8,128)(2,1)S(1)}, bf16[6,16,384]{2,1,0:T(8,128)(2,1)S(1)}, u32[]{:S(2)}, u32[]{:S(2)}) collective-permute-start(bf16[6,16,384]{2,1,0:T(8,128)(2,1)S(1)} %get-tuple-element.47), channel_id=1, source_target_pairs={{0,1},{1,0},{2,3},{3,2},{4,5},{5,4},{6,7},{7,6},{8,9},{9,8},{10,11... | collective-permute-start | bytes 221192 | tf_op jit(solution)/shard_map/ppermute | solution.py:533
  14.4 6.1 %collective-permute-start.4 = (bf16[6,16,384]{2,1,0:T(8,128)(2,1)S(1)}, bf16[6,16,384]{2,1,0:T(8,128)(2,1)S(1)}, u32[]{:S(2)}, u32[]{:S(2)}) collective-permute-start(bf16[6,16,384]{2,1,0:T(8,128)(2,1)S(1)} %get-tuple-element.48), channel_id=1, source_target_pairs={{0,2},{1,3},{2,0},{3,1},{4,6},{5,7},{6,4},{7,5},{8,10},{9,11},{10,... | collective-permute-start | bytes 221192 | tf_op jit(solution)/shard_map/ppermute | solution.py:533
  16.3 5.2 %collective-permute-start.5 = (bf16[6,16,384]{2,1,0:T(8,128)(2,1)S(1)}, bf16[6,16,384]{2,1,0:T(8,128)(2,1)S(1)}, u32[]{:S(2)}, u32[]{:S(2)}) collective-permute-start(bf16[6,16,384]{2,1,0:T(8,128)(2,1)S(1)} %get-tuple-element.49), channel_id=1, source_target_pairs={{0,3},{1,2},{2,1},{3,0},{4,7},{5,6},{6,5},{7,4},{8,11},{9,10},{10,... | collective-permute-start | bytes 221192 | tf_op jit(solution)/shard_map/ppermute | solution.py:533
  20.4 7.4 %collective-permute-start.7 = (bf16[8,16,384]{2,1,0:T(8,128)(2,1)S(1)}, bf16[8,16,384]{2,1,0:T(8,128)(2,1)S(1)}, u32[]{:S(2)}, u32[]{:S(2)}) collective-permute-start(bf16[8,16,384]{2,1,0:T(8,128)(2,1)S(1)} %get-tuple-element.55), channel_id=1, source_target_pairs={{0,1},{1,0},{2,3},{3,2},{4,5},{5,4},{6,7},{7,6},{8,9},{9,8},{10,11... | collective-permute-start | bytes 294920 | tf_op jit(solution)/shard_map/ppermute | solution.py:533
  21.5 6.4 %collective-permute-start.8 = (bf16[8,16,384]{2,1,0:T(8,128)(2,1)S(1)}, bf16[8,16,384]{2,1,0:T(8,128)(2,1)S(1)}, u32[]{:S(2)}, u32[]{:S(2)}) collective-permute-start(bf16[8,16,384]{2,1,0:T(8,128)(2,1)S(1)} %get-tuple-element.56), channel_id=1, source_target_pairs={{0,2},{1,3},{2,0},{3,1},{4,6},{5,7},{6,4},{7,5},{8,10},{9,11},{10,... | collective-permute-start | bytes 294920 | tf_op jit(solution)/shard_map/ppermute | solution.py:533
  23.0 5.1 %collective-permute-start.9 = (bf16[8,16,384]{2,1,0:T(8,128)(2,1)S(1)}, bf16[8,16,384]{2,1,0:T(8,128)(2,1)S(1)}, u32[]{:S(2)}, u32[]{:S(2)}) collective-permute-start(bf16[8,16,384]{2,1,0:T(8,128)(2,1)S(1)} %get-tuple-element.57), channel_id=1, source_target_pairs={{0,3},{1,2},{2,1},{3,0},{4,7},{5,6},{6,5},{7,4},{8,11},{9,10},{10,... | collective-permute-start | bytes 294920 | tf_op jit(solution)/shard_map/ppermute | solution.py:533
  27.1 8.8 %collective-permute-start.6 = (bf16[6,32,384]{2,1,0:T(8,128)(2,1)S(1)}, bf16[6,32,384]{2,1,0:T(8,128)(2,1)S(1)}, u32[]{:S(2)}, u32[]{:S(2)}) collective-permute-start(bf16[6,32,384]{2,1,0:T(8,128)(2,1)S(1)} %get-tuple-element.51), channel_id=1, source_target_pairs={{0,1},{1,0},{2,3},{3,2},{4,5},{5,4},{6,7},{7,6},{8,9},{9,8},{10,11... | collective-permute-start | bytes 442376 | tf_op jit(solution)/shard_map/ppermute | solution.py:533
  32.5 7.7 %collective-permute-start.10 = (bf16[8,32,384]{2,1,0:T(8,128)(2,1)S(1)}, bf16[8,32,384]{2,1,0:T(8,128)(2,1)S(1)}, u32[]{:S(2)}, u32[]{:S(2)}) collective-permute-start(bf16[8,32,384]{2,1,0:T(8,128)(2,1)S(1)} %get-tuple-element.59), channel_id=1, source_target_pairs={{0,1},{1,0},{2,3},{3,2},{4,5},{5,4},{6,7},{7,6},{8,9},{9,8},{10,11... | collective-permute-start | bytes 589832 | tf_op jit(solution)/shard_map/ppermute | solution.py:533
  32.7 19.9 %collective-permute-start.13 = (bf16[8,32,384]{2,1,0:T(8,128)(2,1)S(1)}, bf16[8,32,384]{2,1,0:T(8,128)(2,1)S(1)}, u32[]{:S(2)}, u32[]{:S(2)}) collective-permute-start(bf16[8,32,384]{2,1,0:T(8,128)(2,1)S(1)} %get-tuple-element.68), channel_id=1, source_target_pairs={{0,2},{1,3},{2,0},{3,1},{4,6},{5,7},{6,4},{7,5},{8,10},{9,11},{10,... | collective-permute-start | bytes 589832 | tf_op jit(solution)/shard_map/ppermute | solution.py:533
  34.5 18.2 %collective-permute-start.14 = (bf16[8,32,384]{2,1,0:T(8,128)(2,1)S(1)}, bf16[8,32,384]{2,1,0:T(8,128)(2,1)S(1)}, u32[]{:S(2)}, u32[]{:S(2)}) collective-permute-start(bf16[8,32,384]{2,1,0:T(8,128)(2,1)S(1)} %get-tuple-element.69), channel_id=1, source_target_pairs={{0,3},{1,2},{2,1},{3,0},{4,7},{5,6},{6,5},{7,4},{8,11},{9,10},{10,... | collective-permute-start | bytes 589832 | tf_op jit(solution)/shard_map/ppermute | solution.py:533
  34.5 13.4 %collective-permute-start.11 = (bf16[6,32,384]{2,1,0:T(8,128)(2,1)S(1)}, bf16[6,32,384]{2,1,0:T(8,128)(2,1)S(1)}, u32[]{:S(2)}, u32[]{:S(2)}) collective-permute-start(bf16[6,32,384]{2,1,0:T(8,128)(2,1)S(1)} %get-tuple-element.63), channel_id=1, source_target_pairs={{0,2},{1,3},{2,0},{3,1},{4,6},{5,7},{6,4},{7,5},{8,10},{9,11},{10,... | collective-permute-start | bytes 442376 | tf_op jit(solution)/shard_map/ppermute | solution.py:533
  35.9 13.9 %collective-permute-start.12 = (bf16[6,32,384]{2,1,0:T(8,128)(2,1)S(1)}, bf16[6,32,384]{2,1,0:T(8,128)(2,1)S(1)}, u32[]{:S(2)}, u32[]{:S(2)}) collective-permute-start(bf16[6,32,384]{2,1,0:T(8,128)(2,1)S(1)} %get-tuple-element.64), channel_id=1, source_target_pairs={{0,3},{1,2},{2,1},{3,0},{4,7},{5,6},{6,5},{7,4},{8,11},{9,10},{10,... | collective-permute-start | bytes 442376 | tf_op jit(solution)/shard_map/ppermute | solution.py:533
  36.2 1.0 %copy-start = (bf16[192,768]{1,0:T(8,128)(2,1)S(1)}, bf16[192,768]{1,0:T(8,128)(2,1)}, u32[]{:S(2)}) copy-start(bf16[192,768]{1,0:T(8,128)(2,1)} %refs_2_.9) | copy-start | bytes 884740
  36.2 1.0 %copy-start.1 = (bf16[768,192]{0,1:T(8,128)(2,1)S(1)}, bf16[768,192]{0,1:T(8,128)(2,1)}, u32[]{:S(2)}) copy-start(bf16[768,192]{0,1:T(8,128)(2,1)} %param.18) | copy-start | bytes 884740
  56.9 1.7 %collective-permute-start.15 = (bf16[16,24,384]{2,1,0:T(8,128)(2,1)S(1)}, bf16[16,24,384]{2,1,0:T(8,128)(2,1)S(1)}, u32[]{:S(2)}, u32[]{:S(2)}) collective-permute-start(bf16[16,24,384]{2,1,0:T(8,128)(2,1)S(1)} %get-tuple-element.74), channel_id=1, source_target_pairs={{0,1},{1,0},{2,3},{3,2},{4,5},{5,4},{6,7},{7,6},{8,9},{9,8},{10,11... | collective-permute-start | bytes 884744 | tf_op jit(solution)/shard_map/ppermute | solution.py:586
  59.5 18.1 %all-to-all-start = ((bf16[16,24,384]{2,1,0:T(8,128)(2,1)}), bf16[16,24,384]{2,1,0:T(8,128)(2,1)S(1)}, u32[]{:S(2)}, u32[]{:S(2)}) async-start(bf16[16,24,384]{2,1,0:T(8,128)(2,1)} %add_pair.1), calls=%async_computation | async-start | bytes 589824 | tf_op jit(solution)/shard_map/all_to_all | solution.py:588

commit v6 on v4

--- a/solution.py
+++ b/solution.py
@@ -476,7 +476,8 @@
 
     loop(blocks, BLOCKS, lambda bs: [step(b) for b in bs])
     if last:
-        both = pack([(gin_ref[...].T * F32(factor)).astype(BF), (gout_ref[...].T * F32(factor)).astype(BF)])
+        both = [(ref[...].T * F32(factor)).astype(BF) for ref in (gin_ref, gout_ref)]
+        both = jnp.concatenate(both, axis=1)
         both = both.reshape(keep_ref.shape[0], 2, *keep_ref.shape[1:])
         even = here % 2 == 0
         keep_ref[...] = jnp.where(even, both[:, 0], both[:, 1])
@@ -585,7 +586,7 @@
     total = lax.all_to_all(pieces, ("tables", "chips"), split_axis=0, concat_axis=0, tiled=True)
     total = jnp.sum(total.astype(F32), axis=0)
     output = make_output(parts, spots, groups, per, feats, local)
-    grad_in, grad_out = unpack(total, 2, width)
+    grad_in, grad_out = total[:, :width], total[:, width:]
     return (jnp.swapaxes(output, 1, 2)[None], grad_in.T, grad_out)
 
 

time: 78.5 us -> 78.6 us (level)
  no operation moved by 1% of the time
where the time goes in v6:
time: 78.6 us; the launch traced here: 78.3 us
  Pallas kernels  35.5 us (45%)
  waiting for transfers between devices  20.5 us (26%)
  starting transfers between devices  19.5 us (25%)
  between operations  2.1 us (3%)
    pallas_call x4, Pallas kernels, dense_part(): pl.pallas_call(functools.partial(dense_kernel, groups, per, spot, prev is...  13.7 us
    ppermute x15, starting transfers between devices, exchange(): lax.ppermute(pieces[m], CELLS, [(s, s ^ m) for s in range(groups)])  12.1 us
    ppermute x15, waiting for transfers between devices, exchange(): lax.ppermute(pieces[m], CELLS, [(s, s ^ m) for s in range(groups)])  10.5 us
    pallas_call x2, Pallas kernels, feature_chunk(): pl.pallas_call(functools.partial(feature_kernel, groups, per, base, rows,...  9.63 us
    all_to_all x1, waiting for transfers between devices, per_device(): lax.all_to_all(pieces, ('tables', 'chips'), split_axis=0, concat_axis=0,...  8.78 us
    pallas_call x2, Pallas kernels, row_chunk(): pl.pallas_call(functools.partial(row_kernel, groups, per, chunks, firsts)...  7.87 us
    all_to_all x1, starting transfers between devices, per_device(): lax.all_to_all(pieces, ('tables', 'chips'), split_axis=0, concat_axis=0,...  6.88 us
    pallas_call x1, Pallas kernels, make_output(): pl.pallas_call(functools.partial(output_kernel, groups, per, spots), in_s...  2.44 us
  transfers between devices with their start and end apart: 17, of which 7 were waited for; matrix products, arithmetic and copies ran while one was open for 0% of the time, Pallas kernels for 32%

profile of v6, /device:TPU:0, one launch (start us, length us, event | category | flops | bytes accessed | tf_op | source)
XLA Modules:
  0.0 78.3 jit_solution(9782617694090894838)
XLA Ops:
  1.3 5.5 %feature_0.1 = (bf16[14,16,384]{2,1,0:T(8,128)(2,1)S(1)}, bf16[14,16,384]{2,1,0:T(8,128)(2,1)S(1)}, bf16[14,16,384]{2,1,0:T(8,128)(2,1)S(1)}, bf16[14,16,384]{2,...) custom-call(s32[1]{0:T(128)S(6)} %copy.26.refs_0_, ...), custom_call_target="tpu_custom_call" | custom-call | flops 100000000 | bytes 1000000 | tf_op jit(solution)/shard_map/feature_0/pallas_call | solution.py:277
  7.3 2.5 %collective-permute-start.1 = (bf16[14,16,384]{2,1,0:T(8,128)(2,1)S(1)}, bf16[14,16,384]{2,1,0:T(8,128)(2,1)S(1)}, u32[]{:S(2)}, u32[]{:S(2)}) collective-permute-start(bf16[14,16,384]{2,1,0:T(8,128)(2,1)S(1)} %get-tuple-element.41), channel_id=1, source_target_pairs={{0,2},{1,3},{2,0},{3,1},{4,6},{5,7},{6,4},{7,5},{8,10},{9,11},{10,... | collective-permute-start | bytes 516104 | tf_op jit(solution)/shard_map/ppermute | solution.py:531
  9.9 4.2 %feature_1.1 = (bf16[6,16,384]{2,1,0:T(8,128)(2,1)S(1)}, bf16[6,16,384]{2,1,0:T(8,128)(2,1)S(1)}, bf16[6,16,384]{2,1,0:T(8,128)(2,1)S(1)}, bf16[6,16,384]{2,1,0:...) custom-call(s32[1]{0:T(128)S(6)} %copy.26.refs_0_, ...), custom_call_target="tpu_custom_call" | custom-call | flops 100000000 | bytes 1000000 | tf_op jit(solution)/shard_map/feature_1/pallas_call | solution.py:277
  14.3 2.0 %collective-permute-start.4 = (bf16[6,16,384]{2,1,0:T(8,128)(2,1)S(1)}, bf16[6,16,384]{2,1,0:T(8,128)(2,1)S(1)}, u32[]{:S(2)}, u32[]{:S(2)}) collective-permute-start(bf16[6,16,384]{2,1,0:T(8,128)(2,1)S(1)} %get-tuple-element.48), channel_id=1, source_target_pairs={{0,2},{1,3},{2,0},{3,1},{4,6},{5,7},{6,4},{7,5},{8,10},{9,11},{10,... | collective-permute-start | bytes 221192 | tf_op jit(solution)/shard_map/ppermute | solution.py:531
  16.3 0.9 %collective-permute-start.5 = (bf16[6,16,384]{2,1,0:T(8,128)(2,1)S(1)}, bf16[6,16,384]{2,1,0:T(8,128)(2,1)S(1)}, u32[]{:S(2)}, u32[]{:S(2)}) collective-permute-start(bf16[6,16,384]{2,1,0:T(8,128)(2,1)S(1)} %get-tuple-element.49), channel_id=1, source_target_pairs={{0,3},{1,2},{2,1},{3,0},{4,7},{5,6},{6,5},{7,4},{8,11},{9,10},{10,... | collective-permute-start | bytes 221192 | tf_op jit(solution)/shard_map/ppermute | solution.py:531
  17.1 3.2 %collective-permute-done.4.refs_6_ = bf16[6,16,384]{2,1,0:T(8,128)(2,1)S(1)} collective-permute-done((bf16[6,16,384]{2,1,0:T(8,128)(2,1)S(1)}, bf16[6,16,384]{2,1,0:T(8,128)(2,1)S(1)}, u32[]{:S(2)}, u32[]{:S(2)}) %collective-permute-start.4) | collective-permute-done | bytes 73760 | tf_op jit(solution)/shard_map/ppermute | solution.py:531
  20.4 1.1 %collective-permute-done.5.refs_7_ = bf16[6,16,384]{2,1,0:T(8,128)(2,1)S(1)} collective-permute-done((bf16[6,16,384]{2,1,0:T(8,128)(2,1)S(1)}, bf16[6,16,384]{2,1,0:T(8,128)(2,1)S(1)}, u32[]{:S(2)}, u32[]{:S(2)}) %collective-permute-start.5) | collective-permute-done | bytes 73760 | tf_op jit(solution)/shard_map/ppermute | solution.py:531
  21.4 1.5 %collective-permute-start.8 = (bf16[8,16,384]{2,1,0:T(8,128)(2,1)S(1)}, bf16[8,16,384]{2,1,0:T(8,128)(2,1)S(1)}, u32[]{:S(2)}, u32[]{:S(2)}) collective-permute-start(bf16[8,16,384]{2,1,0:T(8,128)(2,1)S(1)} %get-tuple-element.56), channel_id=1, source_target_pairs={{0,2},{1,3},{2,0},{3,1},{4,6},{5,7},{6,4},{7,5},{8,10},{9,11},{10,... | collective-permute-start | bytes 294920 | tf_op jit(solution)/shard_map/ppermute | solution.py:531
  23.6 3.4 %shard_map.121 = (bf16[6,32,384]{2,1,0:T(8,128)(2,1)S(1)}, bf16[6,32,384]{2,1,0:T(8,128)(2,1)S(1)}, bf16[6,32,384]{2,1,0:T(8,128)(2,1)S(1)}, bf16[6,32,384]{2,1,0:T(8,128)(2,1)S(1)}) custom-call(s32[1]{0:T(128)S(6)} %copy.25.count_ref, bf16[192,576]{1,0:T(8,128)(2,1)S(1)} %copy-done.2, bf16[192,192]{1,0:T(8,128)(2,1)S(1)} %copy-done.3, ...), custom_call_target="tpu_custom_call" | custom-call | flops 100000000 | bytes 1000000 | tf_op jit(solution)/shard_map/pallas_call | solution.py:343
  28.0 4.4 %shard_map.123 = (bf16[8,32,384]{2,1,0:T(8,128)(2,1)S(1)}, bf16[8,32,384]{2,1,0:T(8,128)(2,1)S(1)}, bf16[8,32,384]{2,1,0:T(8,128)(2,1)S(1)}, bf16[8,32,384]{2,1,0:T(8,128)(2,1)S(1)}) custom-call(s32[1]{0:T(128)S(6)} %copy.25.count_ref, bf16[192,576]{1,0:T(8,128)(2,1)S(1)} %copy-done.2, bf16[192,192]{1,0:T(8,128)(2,1)S(1)} %copy-done.3, ...), custom_call_target="tpu_custom_call" | custom-call | flops 100000000 | bytes 1000000 | tf_op jit(solution)/shard_map/pallas_call | solution.py:343
  32.7 1.8 %collective-permute-start.13 = (bf16[8,32,384]{2,1,0:T(8,128)(2,1)S(1)}, bf16[8,32,384]{2,1,0:T(8,128)(2,1)S(1)}, u32[]{:S(2)}, u32[]{:S(2)}) collective-permute-start(bf16[8,32,384]{2,1,0:T(8,128)(2,1)S(1)} %get-tuple-element.68), channel_id=1, source_target_pairs={{0,2},{1,3},{2,0},{3,1},{4,6},{5,7},{6,4},{7,5},{8,10},{9,11},{10,... | collective-permute-start | bytes 589832 | tf_op jit(solution)/shard_map/ppermute | solution.py:531
  34.4 1.4 %collective-permute-start.11 = (bf16[6,32,384]{2,1,0:T(8,128)(2,1)S(1)}, bf16[6,32,384]{2,1,0:T(8,128)(2,1)S(1)}, u32[]{:S(2)}, u32[]{:S(2)}) collective-permute-start(bf16[6,32,384]{2,1,0:T(8,128)(2,1)S(1)} %get-tuple-element.63), channel_id=1, source_target_pairs={{0,2},{1,3},{2,0},{3,1},{4,6},{5,7},{6,4},{7,5},{8,10},{9,11},{10,... | collective-permute-start | bytes 442376 | tf_op jit(solution)/shard_map/ppermute | solution.py:531
  36.2 1.0 %swap_cotangent.1.refs_4_ = bf16[112,32,192]{2,1,0:T(8,128)(2,1)S(1)} custom-call(bf16[32,192,112]{2,1,0:T(8,128)(2,1)S(1)} %get-tuple-element.52.in_ref), custom_call_target="tpu_custom_call" | custom-call | flops 100000000 | bytes 1000000 | tf_op jit(solution)/shard_map/swap_cotangent/pallas_call | solution.py:375
  37.2 2.9 %shard_map.122 = (bf16[2,384,192]{2,1,0:T(8,128)(2,1)S(1)}, f32[192,768]{1,0:T(8,128)S(1)}, f32[192,768]{1,0:T(8,128)S(1)}) custom-call(bf16[6,32,384]{2,1,0:T(8,128)(2,1)S(1)} %get-tuple-element.50.refs_0_, bf16[6,32,384]{2,1,0:T(8,128)(2,1)S(1)} %collective-permute-done.6.refs_1_, bf16[192,768]{1,0:T(8,128)(2,1)S(1)} %copy-done, ...), custom_call_target="tpu_custom_call" | custom-call | flops 100000000 | bytes 1000000 | tf_op jit(solution)/shard_map/pallas_call | solution.py:500
  40.2 3.6 %shard_map.124 = (bf16[2,512,192]{2,1,0:T(8,128)(2,1)S(1)}, f32[192,768]{1,0:T(8,128)S(1)}, f32[192,768]{1,0:T(8,128)S(1)}) custom-call(bf16[8,32,384]{2,1,0:T(8,128)(2,1)S(1)} %get-tuple-element.58.refs_0_, bf16[8,32,384]{2,1,0:T(8,128)(2,1)S(1)} %collective-permute-done.10.refs_1_, ...), custom_call_target="tpu_custom_call", output_to_operand_aliasing={{1}: (5, {}), {2}: (6, {})} | custom-call | flops 100000000 | bytes 1000000 | tf_op jit(solution)/shard_map/pallas_call | solution.py:500
  43.8 4.0 %collective-permute-done.11.refs_0_ = bf16[6,32,384]{2,1,0:T(8,128)(2,1)S(1)} collective-permute-done((bf16[6,32,384]{2,1,0:T(8,128)(2,1)S(1)}, bf16[6,32,384]{2,1,0:T(8,128)(2,1)S(1)}, u32[]{:S(2)}, u32[]{:S(2)}) %collective-permute-start.11) | collective-permute-done | bytes 147488 | tf_op jit(solution)/shard_map/ppermute | solution.py:531
  47.8 1.9 %collective-permute-done.12.refs_1_ = bf16[6,32,384]{2,1,0:T(8,128)(2,1)S(1)} collective-permute-done((bf16[6,32,384]{2,1,0:T(8,128)(2,1)S(1)}, bf16[6,32,384]{2,1,0:T(8,128)(2,1)S(1)}, u32[]{:S(2)}, u32[]{:S(2)}) %collective-permute-start.12) | collective-permute-done | bytes 147488 | tf_op jit(solution)/shard_map/ppermute | solution.py:531
  49.7 2.9 %shard_map.125 = (bf16[2,384,192]{2,1,0:T(8,128)(2,1)S(1)}, f32[192,768]{1,0:T(8,128)S(1)}, f32[192,768]{1,0:T(8,128)S(1)}) custom-call(bf16[6,32,384]{2,1,0:T(8,128)(2,1)S(1)} %collective-permute-done.11.refs_0_, bf16[6,32,384]{2,1,0:T(8,128)(2,1)S(1)} %collective-permute-done.12.refs_1_, ...), custom_call_target="tpu_custom_call", output_to_operand_aliasing={{1}: (5, {}), {2}: (6, {})} | custom-call | flops 100000000 | bytes 1000000 | tf_op jit(solution)/shard_map/pallas_call | solution.py:500
  52.7 4.2 %shard_map.126 = (bf16[2,512,192]{2,1,0:T(8,128)(2,1)S(1)}, f32[192,768]{1,0:T(8,128)S(1)}, f32[192,768]{1,0:T(8,128)S(1)}, bf16[16,24,384]{2,1,0:T(8,128)(2,1)S(1)}, bf16[16,24,384]{2,1,0:T(8,128)(2,1)S(1)}) custom-call(bf16[8,32,384]{2,1,0:T(8,128)(2,1)S(1)} %collective-permute-done.13.refs_0_, ...), custom_call_target="tpu_custom_call", output_to_operand_aliasing={{1}: (5, {}), {2}: (6, {})} | custom-call | flops 100000000 | bytes 1000000 | tf_op jit(solution)/shard_map/pallas_call | solution.py:500
  57.4 1.2 %collective-permute-done.15.b_ref = bf16[16,24,384]{2,1,0:T(8,128)(2,1)S(1)} collective-permute-done((bf16[16,24,384]{2,1,0:T(8,128)(2,1)S(1)}, bf16[16,24,384]{2,1,0:T(8,128)(2,1)S(1)}, u32[]{:S(2)}, u32[]{:S(2)}) %collective-permute-start.15) | collective-permute-done | bytes 294944 | tf_op jit(solution)/shard_map/ppermute | solution.py:584
  58.7 0.8 %add_pair.1 = bf16[16,24,384]{2,1,0:T(8,128)(2,1)} custom-call(bf16[16,24,384]{2,1,0:T(8,128)(2,1)S(1)} %get-tuple-element.73.a_ref, bf16[16,24,384]{2,1,0:T(8,128)(2,1)S(1)} %collective-permute-done.15.b_ref), custom_call_target="tpu_custom_call" | custom-call | flops 1000000 | bytes 1000000 | tf_op jit(solution)/shard_map/add_pair/pallas_call | solution.py:517
  59.4 6.9 %all-to-all-start = ((bf16[16,24,384]{2,1,0:T(8,128)(2,1)}), bf16[16,24,384]{2,1,0:T(8,128)(2,1)S(1)}, u32[]{:S(2)}, u32[]{:S(2)}) async-start(bf16[16,24,384]{2,1,0:T(8,128)(2,1)} %add_pair.1), calls=%async_computation | async-start | bytes 589824 | tf_op jit(solution)/shard_map/all_to_all | solution.py:586
  66.3 2.4 %make_output.1 = bf16[32,192,112]{2,1,0:T(8,128)(2,1)} custom-call(bf16[2,384,192]{2,1,0:T(8,128)(2,1)S(1)} %get-tuple-element.53.refs_0_, bf16[2,512,192]{2,1,0:T(8,128)(2,1)S(1)} %get-tuple-element.62.refs_1_, bf16[2,384,192]{2,1,0:T(8,128)(2,1)S(1)} %get-tuple-element.67.refs_2_, bf16[2,512,192]{2,1,0:T(8,128)(2,1)S(1)} %get-tuple-element.72.refs_3_), custom_call_target="tpu_custom_call" | custom-call | flops 100000000 | bytes 1000000 | tf_op jit(solution)/shard_map/make_output/pallas_call | solution.py:415
  68.8 8.8 %all-to-all-done = bf16[16,24,384]{2,1,0:T(8,128)(2,1)S(1)} async-done(((bf16[16,24,384]{2,1,0:T(8,128)(2,1)}), bf16[16,24,384]{2,1,0:T(8,128)(2,1)S(1)}, u32[]{:S(2)}, u32[]{:S(2)}) %all-to-all-start) | async-done | bytes 294944 | tf_op jit(solution)/shard_map/all_to_all | solution.py:586
  (31 shorter events, 3.6 us)
Async XLA Ops:
  6.8 16.8 %copy-start.2 = (bf16[192,576]{1,0:T(8,128)(2,1)S(1)}, bf16[192,576]{1,0:T(8,128)(2,1)}, u32[]{:S(2)}) copy-start(bf16[192,576]{1,0:T(8,128)(2,1)} %wqkv_ref.3) | copy-start | bytes 663556
  6.8 16.8 %copy-start.3 = (bf16[192,192]{1,0:T(8,128)(2,1)S(1)}, bf16[192,192]{1,0:T(8,128)(2,1)}, u32[]{:S(2)}) copy-start(bf16[192,192]{1,0:T(8,128)(2,1)} %wproj_ref.3) | copy-start | bytes 221188
  6.8 16.1 %collective-permute-start = (bf16[14,16,384]{2,1,0:T(8,128)(2,1)S(1)}, bf16[14,16,384]{2,1,0:T(8,128)(2,1)S(1)}, u32[]{:S(2)}, u32[]{:S(2)}) collective-permute-start(bf16[14,16,384]{2,1,0:T(8,128)(2,1)S(1)} %get-tuple-element.40), channel_id=1, source_target_pairs={{0,1},{1,0},{2,3},{3,2},{4,5},{5,4},{6,7},{7,6},{8,9},{9,8},{10,11... | collective-permute-start | bytes 516104 | tf_op jit(solution)/shard_map/ppermute | solution.py:531
  7.3 16.2 %collective-permute-start.1 = (bf16[14,16,384]{2,1,0:T(8,128)(2,1)S(1)}, bf16[14,16,384]{2,1,0:T(8,128)(2,1)S(1)}, u32[]{:S(2)}, u32[]{:S(2)}) collective-permute-start(bf16[14,16,384]{2,1,0:T(8,128)(2,1)S(1)} %get-tuple-element.41), channel_id=1, source_target_pairs={{0,2},{1,3},{2,0},{3,1},{4,6},{5,7},{6,4},{7,5},{8,10},{9,11},{10,... | collective-permute-start | bytes 516104 | tf_op jit(solution)/shard_map/ppermute | solution.py:531
  9.9 13.7 %collective-permute-start.2 = (bf16[14,16,384]{2,1,0:T(8,128)(2,1)S(1)}, bf16[14,16,384]{2,1,0:T(8,128)(2,1)S(1)}, u32[]{:S(2)}, u32[]{:S(2)}) collective-permute-start(bf16[14,16,384]{2,1,0:T(8,128)(2,1)S(1)} %get-tuple-element.42), channel_id=1, source_target_pairs={{0,3},{1,2},{2,1},{3,0},{4,7},{5,6},{6,5},{7,4},{8,11},{9,10},{10,... | collective-permute-start | bytes 516104 | tf_op jit(solution)/shard_map/ppermute | solution.py:531
  14.1 2.2 %collective-permute-start.3 = (bf16[6,16,384]{2,1,0:T(8,128)(2,1)S(1)}, bf16[6,16,384]{2,1,0:T(8,128)(2,1)S(1)}, u32[]{:S(2)}, u32[]{:S(2)}) collective-permute-start(bf16[6,16,384]{2,1,0:T(8,128)(2,1)S(1)} %get-tuple-element.47), channel_id=1, source_target_pairs={{0,1},{1,0},{2,3},{3,2},{4,5},{5,4},{6,7},{7,6},{8,9},{9,8},{10,11... | collective-permute-start | bytes 221192 | tf_op jit(solution)/shard_map/ppermute | solution.py:531
  14.3 6.1 %collective-permute-start.4 = (bf16[6,16,384]{2,1,0:T(8,128)(2,1)S(1)}, bf16[6,16,384]{2,1,0:T(8,128)(2,1)S(1)}, u32[]{:S(2)}, u32[]{:S(2)}) collective-permute-start(bf16[6,16,384]{2,1,0:T(8,128)(2,1)S(1)} %get-tuple-element.48), channel_id=1, source_target_pairs={{0,2},{1,3},{2,0},{3,1},{4,6},{5,7},{6,4},{7,5},{8,10},{9,11},{10,... | collective-permute-start | bytes 221192 | tf_op jit(solution)/shard_map/ppermute | solution.py:531
  16.3 5.2 %collective-permute-start.5 = (bf16[6,16,384]{2,1,0:T(8,128)(2,1)S(1)}, bf16[6,16,384]{2,1,0:T(8,128)(2,1)S(1)}, u32[]{:S(2)}, u32[]{:S(2)}) collective-permute-start(bf16[6,16,384]{2,1,0:T(8,128)(2,1)S(1)} %get-tuple-element.49), channel_id=1, source_target_pairs={{0,3},{1,2},{2,1},{3,0},{4,7},{5,6},{6,5},{7,4},{8,11},{9,10},{10,... | collective-permute-start | bytes 221192 | tf_op jit(solution)/shard_map/ppermute | solution.py:531
  20.4 7.4 %collective-permute-start.7 = (bf16[8,16,384]{2,1,0:T(8,128)(2,1)S(1)}, bf16[8,16,384]{2,1,0:T(8,128)(2,1)S(1)}, u32[]{:S(2)}, u32[]{:S(2)}) collective-permute-start(bf16[8,16,384]{2,1,0:T(8,128)(2,1)S(1)} %get-tuple-element.55), channel_id=1, source_target_pairs={{0,1},{1,0},{2,3},{3,2},{4,5},{5,4},{6,7},{7,6},{8,9},{9,8},{10,11... | collective-permute-start | bytes 294920 | tf_op jit(solution)/shard_map/ppermute | solution.py:531
  21.4 6.3 %collective-permute-start.8 = (bf16[8,16,384]{2,1,0:T(8,128)(2,1)S(1)}, bf16[8,16,384]{2,1,0:T(8,128)(2,1)S(1)}, u32[]{:S(2)}, u32[]{:S(2)}) collective-permute-start(bf16[8,16,384]{2,1,0:T(8,128)(2,1)S(1)} %get-tuple-element.56), channel_id=1, source_target_pairs={{0,2},{1,3},{2,0},{3,1},{4,6},{5,7},{6,4},{7,5},{8,10},{9,11},{10,... | collective-permute-start | bytes 294920 | tf_op jit(solution)/shard_map/ppermute | solution.py:531
  22.9 5.1 %collective-permute-start.9 = (bf16[8,16,384]{2,1,0:T(8,128)(2,1)S(1)}, bf16[8,16,384]{2,1,0:T(8,128)(2,1)S(1)}, u32[]{:S(2)}, u32[]{:S(2)}) collective-permute-start(bf16[8,16,384]{2,1,0:T(8,128)(2,1)S(1)} %get-tuple-element.57), channel_id=1, source_target_pairs={{0,3},{1,2},{2,1},{3,0},{4,7},{5,6},{6,5},{7,4},{8,11},{9,10},{10,... | collective-permute-start | bytes 294920 | tf_op jit(solution)/shard_map/ppermute | solution.py:531
  27.1 8.8 %collective-permute-start.6 = (bf16[6,32,384]{2,1,0:T(8,128)(2,1)S(1)}, bf16[6,32,384]{2,1,0:T(8,128)(2,1)S(1)}, u32[]{:S(2)}, u32[]{:S(2)}) collective-permute-start(bf16[6,32,384]{2,1,0:T(8,128)(2,1)S(1)} %get-tuple-element.51), channel_id=1, source_target_pairs={{0,1},{1,0},{2,3},{3,2},{4,5},{5,4},{6,7},{7,6},{8,9},{9,8},{10,11... | collective-permute-start | bytes 442376 | tf_op jit(solution)/shard_map/ppermute | solution.py:531
  32.5 7.7 %collective-permute-start.10 = (bf16[8,32,384]{2,1,0:T(8,128)(2,1)S(1)}, bf16[8,32,384]{2,1,0:T(8,128)(2,1)S(1)}, u32[]{:S(2)}, u32[]{:S(2)}) collective-permute-start(bf16[8,32,384]{2,1,0:T(8,128)(2,1)S(1)} %get-tuple-element.59), channel_id=1, source_target_pairs={{0,1},{1,0},{2,3},{3,2},{4,5},{5,4},{6,7},{7,6},{8,9},{9,8},{10,11... | collective-permute-start | bytes 589832 | tf_op jit(solution)/shard_map/ppermute | solution.py:531
  32.7 20.0 %collective-permute-start.13 = (bf16[8,32,384]{2,1,0:T(8,128)(2,1)S(1)}, bf16[8,32,384]{2,1,0:T(8,128)(2,1)S(1)}, u32[]{:S(2)}, u32[]{:S(2)}) collective-permute-start(bf16[8,32,384]{2,1,0:T(8,128)(2,1)S(1)} %get-tuple-element.68), channel_id=1, source_target_pairs={{0,2},{1,3},{2,0},{3,1},{4,6},{5,7},{6,4},{7,5},{8,10},{9,11},{10,... | collective-permute-start | bytes 589832 | tf_op jit(solution)/shard_map/ppermute | solution.py:531
  34.4 18.2 %collective-permute-start.14 = (bf16[8,32,384]{2,1,0:T(8,128)(2,1)S(1)}, bf16[8,32,384]{2,1,0:T(8,128)(2,1)S(1)}, u32[]{:S(2)}, u32[]{:S(2)}) collective-permute-start(bf16[8,32,384]{2,1,0:T(8,128)(2,1)S(1)} %get-tuple-element.69), channel_id=1, source_target_pairs={{0,3},{1,2},{2,1},{3,0},{4,7},{5,6},{6,5},{7,4},{8,11},{9,10},{10,... | collective-permute-start | bytes 589832 | tf_op jit(solution)/shard_map/ppermute | solution.py:531
  34.4 13.4 %collective-permute-start.11 = (bf16[6,32,384]{2,1,0:T(8,128)(2,1)S(1)}, bf16[6,32,384]{2,1,0:T(8,128)(2,1)S(1)}, u32[]{:S(2)}, u32[]{:S(2)}) collective-permute-start(bf16[6,32,384]{2,1,0:T(8,128)(2,1)S(1)} %get-tuple-element.63), channel_id=1, source_target_pairs={{0,2},{1,3},{2,0},{3,1},{4,6},{5,7},{6,4},{7,5},{8,10},{9,11},{10,... | collective-permute-start | bytes 442376 | tf_op jit(solution)/shard_map/ppermute | solution.py:531
  35.9 13.9 %collective-permute-start.12 = (bf16[6,32,384]{2,1,0:T(8,128)(2,1)S(1)}, bf16[6,32,384]{2,1,0:T(8,128)(2,1)S(1)}, u32[]{:S(2)}, u32[]{:S(2)}) collective-permute-start(bf16[6,32,384]{2,1,0:T(8,128)(2,1)S(1)} %get-tuple-element.64), channel_id=1, source_target_pairs={{0,3},{1,2},{2,1},{3,0},{4,7},{5,6},{6,5},{7,4},{8,11},{9,10},{10,... | collective-permute-start | bytes 442376 | tf_op jit(solution)/shard_map/ppermute | solution.py:531
  36.2 1.0 %copy-start = (bf16[192,768]{1,0:T(8,128)(2,1)S(1)}, bf16[192,768]{1,0:T(8,128)(2,1)}, u32[]{:S(2)}) copy-start(bf16[192,768]{1,0:T(8,128)(2,1)} %refs_2_.9) | copy-start | bytes 884740
  36.2 1.0 %copy-start.1 = (bf16[768,192]{0,1:T(8,128)(2,1)S(1)}, bf16[768,192]{0,1:T(8,128)(2,1)}, u32[]{:S(2)}) copy-start(bf16[768,192]{0,1:T(8,128)(2,1)} %param.18) | copy-start | bytes 884740
  56.9 1.7 %collective-permute-start.15 = (bf16[16,24,384]{2,1,0:T(8,128)(2,1)S(1)}, bf16[16,24,384]{2,1,0:T(8,128)(2,1)S(1)}, u32[]{:S(2)}, u32[]{:S(2)}) collective-permute-start(bf16[16,24,384]{2,1,0:T(8,128)(2,1)S(1)} %get-tuple-element.74), channel_id=1, source_target_pairs={{0,1},{1,0},{2,3},{3,2},{4,5},{5,4},{6,7},{7,6},{8,9},{9,8},{10,11... | collective-permute-start | bytes 884744 | tf_op jit(solution)/shard_map/ppermute | solution.py:584
  59.4 18.1 %all-to-all-start = ((bf16[16,24,384]{2,1,0:T(8,128)(2,1)}), bf16[16,24,384]{2,1,0:T(8,128)(2,1)S(1)}, u32[]{:S(2)}, u32[]{:S(2)}) async-start(bf16[16,24,384]{2,1,0:T(8,128)(2,1)} %add_pair.1), calls=%async_computation | async-start | bytes 589824 | tf_op jit(solution)/shard_map/all_to_all | solution.py:586
